TPU v7x, 8 devices: a whole 2x2x1 slice. The times are simulated.
8 devices in a mesh: dp: 2 (over z, y), pp: 4 (over x, core).
Axes of the slice: x: 2, y: 2, z: 1, core: 2. Of those that a mesh axis runs over, the one named last changes fastest.
Arguments:
- patches: bfloat16 [8, 2, 256, 588], P('dp'), parts along dimension 0
- labels: int32 [8, 2], P('dp'), parts along dimension 0
- w_patch: bfloat16 [588, 1408], replicated
- b_patch: bfloat16 [1408], replicated
- cls_token: bfloat16 [1408], replicated
- pos_embed: bfloat16 [257, 1408], replicated
- ln1_gain: bfloat16 [4, 1408], P('pp')
- ln1_bias: bfloat16 [4, 1408], P('pp')
- w_qkv: bfloat16 [4, 1408, 3, 16, 88], P('pp')
- b_qkv: bfloat16 [4, 3, 16, 88], P('pp')
- w_proj: bfloat16 [4, 16, 88, 1408], P('pp')
- b_proj: bfloat16 [4, 1408], P('pp')
- ln2_gain: bfloat16 [4, 1408], P('pp')
- ln2_bias: bfloat16 [4, 1408], P('pp')
- w_fc1: bfloat16 [4, 1408, 6144], P('pp')
- b_fc1: bfloat16 [4, 6144], P('pp')
- w_fc2: bfloat16 [4, 6144, 1408], P('pp')
- b_fc2: bfloat16 [4, 1408], P('pp')
- lnf_gain: bfloat16 [1408], replicated
- lnf_bias: bfloat16 [1408], replicated
- w_head: bfloat16 [1408, 1000], replicated
- b_head: bfloat16 [1000], replicated
Outputs:
- output 1: float32 [2], P('dp'), parts along dimension 0
- output 2: float32 [1176, 1408], P('dp'), parts along dimension 0
- output 3: float32 [2816], P('dp'), parts along dimension 0
- output 4: float32 [2816], P('dp'), parts along dimension 0
- output 5: float32 [514, 1408], P('dp'), parts along dimension 0
- output 6: float32 [8, 1408], P(('dp', 'pp')), parts along dimension 0
- output 7: float32 [8, 1408], P(('dp', 'pp')), parts along dimension 0
- output 8: float32 [8, 1408, 3, 16, 88], P(('dp', 'pp')), parts along dimension 0
- output 9: float32 [8, 3, 16, 88], P(('dp', 'pp')), parts along dimension 0
- output 10: float32 [8, 16, 88, 1408], P(('dp', 'pp')), parts along dimension 0
- output 11: float32 [8, 1408], P(('dp', 'pp')), parts along dimension 0
- output 12: float32 [8, 1408], P(('dp', 'pp')), parts along dimension 0
- output 13: float32 [8, 1408], P(('dp', 'pp')), parts along dimension 0
- output 14: float32 [8, 1408, 6144], P(('dp', 'pp')), parts along dimension 0
- output 15: float32 [8, 6144], P(('dp', 'pp')), parts along dimension 0
- output 16: float32 [8, 6144, 1408], P(('dp', 'pp')), parts along dimension 0
- output 17: float32 [8, 1408], P(('dp', 'pp')), parts along dimension 0
- output 18: float32 [2816], P('dp'), parts along dimension 0
- output 19: float32 [2816], P('dp'), parts along dimension 0
- output 20: float32 [2816, 1000], P('dp'), parts along dimension 0
- output 21: float32 [2000], P('dp'), parts along dimension 0
There are 2 independent parts. A program takes and returns all parts, laid end to end along the dimension named above; an argument that names none is the same for every part.
All inputs are finite; a program needn't handle non-finite values.
Results may differ from a plain program's by a relative error of at most 0.02.
Values are sent between devices in bfloat16 or wider.
A program may use at most 1 GiB of HBM per device.

v0:
```python
import functools
import jax
import jax.numpy as jnp
from jax import lax
from jax.sharding import PartitionSpec as P

EPS = 1e-6
SMOOTH = 0.1
exact_gelu = functools.partial(jax.nn.gelu, approximate=False)


def add_all(totals, extra):
    return tuple(total + piece for total, piece in zip(totals, extra))


def layer_norm(hidden, gain, bias):
    values = hidden.astype(jnp.float32)
    centered = values - jnp.mean(values, axis=-1, keepdims=True)
    variance = jnp.mean(jnp.square(centered), axis=-1, keepdims=True)
    return (centered * lax.rsqrt(variance + EPS) * gain + bias).astype(jnp.bfloat16)


def attention_forward(qkv_rows):
    scale = qkv_rows.shape[-1] ** -0.5
    scores = jnp.einsum("bqhe,bkhe->bhqk", qkv_rows[:, :, 0], qkv_rows[:, :, 1], preferred_element_type=jnp.float32) * scale
    probs_full = jax.nn.softmax(scores, axis=-1)
    probs = probs_full.astype(jnp.bfloat16)
    context = jnp.einsum("bhqk,bkhe->bqhe", probs, qkv_rows[:, :, 2], preferred_element_type=jnp.float32).astype(jnp.bfloat16)
    return context, probs_full, probs


def attention_backward(grad_context, qkv_rows, probs_full, probs):
    scale = qkv_rows.shape[-1] ** -0.5
    grad_probs = jnp.einsum("bqhe,bkhe->bhqk", grad_context, qkv_rows[:, :, 2], preferred_element_type=jnp.float32)
    grad_value = jnp.einsum("bhqk,bqhe->bkhe", probs, grad_context, preferred_element_type=jnp.float32).astype(jnp.bfloat16)
    grad_scores = probs_full * (grad_probs - jnp.sum(grad_probs * probs_full, axis=-1, keepdims=True))
    grad_scores = (grad_scores * scale).astype(jnp.bfloat16)
    grad_query = jnp.einsum("bhqk,bkhe->bqhe", grad_scores, qkv_rows[:, :, 1], preferred_element_type=jnp.float32).astype(jnp.bfloat16)
    grad_key = jnp.einsum("bhqk,bqhe->bkhe", grad_scores, qkv_rows[:, :, 0], preferred_element_type=jnp.float32).astype(jnp.bfloat16)
    return jnp.stack([grad_query, grad_key, grad_value], axis=2)


def layer_forward(hidden, weights):
    ln1_gain, ln1_bias, w_qkv, b_qkv, w_proj, b_proj, ln2_gain, ln2_bias, w_fc1, b_fc1, w_fc2, b_fc2 = weights
    normed, ln1_vjp = jax.vjp(layer_norm, hidden, ln1_gain.astype(jnp.float32), ln1_bias.astype(jnp.float32))
    qkv_rows = (jnp.einsum("btd,dkhe->btkhe", normed, w_qkv, preferred_element_type=jnp.float32) + b_qkv.astype(jnp.float32)).astype(jnp.bfloat16)
    context, probs_full, probs = attention_forward(qkv_rows)
    mid = (hidden.astype(jnp.float32) + jnp.einsum("bthe,hed->btd", context, w_proj, preferred_element_type=jnp.float32) + b_proj.astype(jnp.float32)).astype(jnp.bfloat16)
    normed_mlp, ln2_vjp = jax.vjp(layer_norm, mid, ln2_gain.astype(jnp.float32), ln2_bias.astype(jnp.float32))
    pre_act = jnp.einsum("btd,df->btf", normed_mlp, w_fc1, preferred_element_type=jnp.float32) + b_fc1.astype(jnp.float32)
    activ_full, gelu_vjp = jax.vjp(exact_gelu, pre_act)
    activ = activ_full.astype(jnp.bfloat16)
    out = (mid.astype(jnp.float32) + jnp.einsum("btf,fd->btd", activ, w_fc2, preferred_element_type=jnp.float32) + b_fc2.astype(jnp.float32)).astype(jnp.bfloat16)
    return out, (normed, qkv_rows, probs_full, probs, context, normed_mlp, activ, ln1_vjp, ln2_vjp, gelu_vjp)


def layer_backward(grad_out, weights, saved):
    w_qkv, w_proj, w_fc1, w_fc2 = weights[2], weights[4], weights[8], weights[10]
    normed, qkv_rows, probs_full, probs, context, normed_mlp, activ, ln1_vjp, ln2_vjp, gelu_vjp = saved
    g_b_fc2 = jnp.sum(grad_out.astype(jnp.float32), axis=(0, 1))
    g_w_fc2 = jnp.einsum("btf,btd->fd", activ, grad_out, preferred_element_type=jnp.float32)
    grad_activ = jnp.einsum("btd,fd->btf", grad_out, w_fc2, preferred_element_type=jnp.float32).astype(jnp.bfloat16)
    grad_pre = gelu_vjp(grad_activ.astype(jnp.float32))[0]
    g_b_fc1 = jnp.sum(grad_pre, axis=(0, 1))
    grad_pre_low = grad_pre.astype(jnp.bfloat16)
    g_w_fc1 = jnp.einsum("btd,btf->df", normed_mlp, grad_pre_low, preferred_element_type=jnp.float32)
    grad_normed_mlp = jnp.einsum("btf,df->btd", grad_pre_low, w_fc1, preferred_element_type=jnp.float32).astype(jnp.bfloat16)
    grad_mid_norm, g_ln2_gain, g_ln2_bias = ln2_vjp(grad_normed_mlp)
    grad_mid = (grad_out.astype(jnp.float32) + grad_mid_norm.astype(jnp.float32)).astype(jnp.bfloat16)
    g_b_proj = jnp.sum(grad_mid.astype(jnp.float32), axis=(0, 1))
    g_w_proj = jnp.einsum("bthe,btd->hed", context, grad_mid, preferred_element_type=jnp.float32)
    grad_context = jnp.einsum("btd,hed->bthe", grad_mid, w_proj, preferred_element_type=jnp.float32).astype(jnp.bfloat16)
    grad_qkv = attention_backward(grad_context, qkv_rows, probs_full, probs)
    g_b_qkv = jnp.sum(grad_qkv.astype(jnp.float32), axis=(0, 1))
    g_w_qkv = jnp.einsum("btd,btkhe->dkhe", normed, grad_qkv, preferred_element_type=jnp.float32)
    grad_normed = jnp.einsum("btkhe,dkhe->btd", grad_qkv, w_qkv, preferred_element_type=jnp.float32).astype(jnp.bfloat16)
    grad_hidden_norm, g_ln1_gain, g_ln1_bias = ln1_vjp(grad_normed)
    grad_hidden = (grad_mid.astype(jnp.float32) + grad_hidden_norm.astype(jnp.float32)).astype(jnp.bfloat16)
    return grad_hidden, (g_ln1_gain, g_ln1_bias, g_w_qkv, g_b_qkv, g_w_proj, g_b_proj, g_ln2_gain, g_ln2_bias, g_w_fc1, g_b_fc1, g_w_fc2, g_b_fc2)


def stage_forward(hidden, stage_weights):
    saves = []
    for layer_idx in range(stage_weights[0].shape[0]):
        weights = tuple(tensor[layer_idx] for tensor in stage_weights)
        hidden, saved = layer_forward(hidden, weights)
        saves.append((weights, saved))
    return hidden, saves


def stage_backward(grad_hidden, saves):
    layer_grads = []
    for weights, saved in reversed(saves):
        grad_hidden, grads = layer_backward(grad_hidden, weights, saved)
        layer_grads.insert(0, grads)
    stacked = tuple(jnp.stack([grads[index] for grads in layer_grads]) for index in range(len(layer_grads[0])))
    return grad_hidden, stacked


def embed_forward(patch_rows, embed_params):
    w_patch, b_patch, cls_token, pos_embed = embed_params
    batch_size = patch_rows.shape[0]
    projected = jnp.einsum("bnp,pd->bnd", patch_rows, w_patch, preferred_element_type=jnp.float32) + b_patch.astype(jnp.float32)
    cls_rows = jnp.broadcast_to(cls_token.astype(jnp.float32), (batch_size, 1, cls_token.shape[0]))
    return (jnp.concatenate([cls_rows, projected], axis=1) + pos_embed.astype(jnp.float32)).astype(jnp.bfloat16)


def embed_backward(grad_tokens, patch_rows):
    g_pos_embed = jnp.sum(grad_tokens.astype(jnp.float32), axis=0)
    g_cls_token = g_pos_embed[0]
    g_b_patch = jnp.sum(g_pos_embed[1:], axis=0)
    g_w_patch = jnp.einsum("bnp,bnd->pd", patch_rows, grad_tokens[:, 1:], preferred_element_type=jnp.float32)
    return g_w_patch, g_b_patch, g_cls_token, g_pos_embed


def head_forward_backward(hidden, label_rows, head_params, inv_count):
    lnf_gain, lnf_bias, w_head, b_head = head_params
    pooled, lnf_vjp = jax.vjp(layer_norm, hidden[:, 0], lnf_gain.astype(jnp.float32), lnf_bias.astype(jnp.float32))
    logits = jnp.dot(pooled, w_head, preferred_element_type=jnp.float32) + b_head.astype(jnp.float32)
    classes = logits.shape[-1]
    log_probs = jax.nn.log_softmax(logits, axis=-1)
    target = (1.0 - SMOOTH) * jax.nn.one_hot(label_rows, classes, dtype=jnp.float32) + SMOOTH / classes
    loss_part = -jnp.sum(target * log_probs) * inv_count
    grad_logits = (jnp.exp(log_probs) - target) * inv_count
    grad_low = grad_logits.astype(jnp.bfloat16)
    g_w_head = jnp.einsum("bd,bc->dc", pooled, grad_low, preferred_element_type=jnp.float32)
    g_b_head = jnp.sum(grad_logits, axis=0)
    grad_pooled = jnp.einsum("bc,dc->bd", grad_low, w_head, preferred_element_type=jnp.float32).astype(jnp.bfloat16)
    grad_first, g_lnf_gain, g_lnf_bias = lnf_vjp(grad_pooled)
    batch_size, tokens, width = hidden.shape
    grad_hidden = jnp.concatenate([grad_first[:, None], jnp.zeros((batch_size, tokens - 1, width), jnp.bfloat16)], axis=1)
    return loss_part, grad_hidden, (g_lnf_gain, g_lnf_bias, g_w_head, g_b_head)


def solution(mesh):
    stages = mesh.shape["pp"]
    forward_perm = [(index, index + 1) for index in range(stages - 1)]
    backward_perm = [(index + 1, index) for index in range(stages - 1)]
    in_specs = (P("dp"), P("dp"), P(), P(), P(), P()) + (P("pp"),) * 12 + (P(),) * 4
    out_specs = (P("dp"),) * 5 + (P(("dp", "pp")),) * 12 + (P("dp"),) * 4

    def body(patches, labels, w_patch, b_patch, cls_token, pos_embed, *rest):
        stage_weights = rest[:12]
        head_params = rest[12:]
        embed_params = (w_patch, b_patch, cls_token, pos_embed)
        stage = lax.axis_index("pp")
        is_first = stage == 0
        is_last = stage == stages - 1
        micro_count, batch_size = labels.shape
        act_shape = (batch_size,) + pos_embed.shape
        inv_count = 1.0 / (micro_count * batch_size)
        steps = micro_count + stages - 1

        def forward_step(carry, step):
            received, stash = carry
            micro_idx = step - stage
            valid = (micro_idx >= 0) & (micro_idx < micro_count)
            slot = jnp.clip(micro_idx, 0, micro_count - 1)

            def run_stage(received_in):
                stage_in = lax.cond(is_first, lambda: embed_forward(lax.dynamic_index_in_dim(patches, slot, 0, keepdims=False), embed_params), lambda: received_in)
                stage_out, _ = stage_forward(stage_in, stage_weights)
                return stage_out, stage_in

            def skip_stage(received_in):
                return jnp.zeros_like(received_in), lax.dynamic_index_in_dim(stash, slot, 0, keepdims=False)

            stage_out, stage_in = lax.cond(valid, run_stage, skip_stage, received)
            stash = lax.dynamic_update_index_in_dim(stash, stage_in, slot, 0)
            received = lax.ppermute(stage_out, "pp", forward_perm)
            return (received, stash), None

        init = (jnp.zeros(act_shape, jnp.bfloat16), jnp.zeros((micro_count,) + act_shape, jnp.bfloat16))
        (_, stash), _ = lax.scan(forward_step, init, jnp.arange(steps))

        def backward_step(carry, step):
            received, accums = carry
            micro_idx = step - (stages - 1 - stage)
            valid = (micro_idx >= 0) & (micro_idx < micro_count)
            slot = jnp.clip(micro_idx, 0, micro_count - 1)

            def run_stage(operands):
                received_in, (loss_acc, layer_acc, embed_acc, head_acc) = operands
                stage_in = lax.dynamic_index_in_dim(stash, slot, 0, keepdims=False)
                stage_out, saves = stage_forward(stage_in, stage_weights)

                def with_head():
                    label_rows = lax.dynamic_index_in_dim(labels, slot, 0, keepdims=False)
                    loss_part, grad_top, head_grads = head_forward_backward(stage_out, label_rows, head_params, inv_count)
                    return loss_acc + loss_part, grad_top, add_all(head_acc, head_grads)

                def without_head():
                    return loss_acc, received_in, head_acc

                new_loss, grad_out, new_head = lax.cond(is_last, with_head, without_head)
                grad_in, layer_grads = stage_backward(grad_out, saves)

                def with_embed():
                    patch_rows = lax.dynamic_index_in_dim(patches, slot, 0, keepdims=False)
                    return add_all(embed_acc, embed_backward(grad_in, patch_rows))

                def without_embed():
                    return embed_acc

                new_embed = lax.cond(is_first, with_embed, without_embed)
                return grad_in, (new_loss, add_all(layer_acc, layer_grads), new_embed, new_head)

            def skip_stage(operands):
                return jnp.zeros_like(operands[0]), operands[1]

            grad_in, accums = lax.cond(valid, run_stage, skip_stage, (received, accums))
            received = lax.ppermute(grad_in, "pp", backward_perm)
            return (received, accums), None

        zeros_like_f32 = lambda group: tuple(jnp.zeros(tensor.shape, jnp.float32) for tensor in group)
        accums = (jnp.zeros((), jnp.float32), zeros_like_f32(stage_weights), zeros_like_f32(embed_params), zeros_like_f32(head_params))
        (_, accums), _ = lax.scan(backward_step, (jnp.zeros(act_shape, jnp.bfloat16), accums), jnp.arange(steps))
        loss_acc, layer_acc, embed_acc, head_acc = accums
        loss_total = lax.psum(loss_acc, "pp")
        embed_total = tuple(lax.psum(tensor, "pp") for tensor in embed_acc)
        head_total = tuple(lax.psum(tensor, "pp") for tensor in head_acc)
        return (loss_total.reshape(1),) + embed_total + tuple(layer_acc) + head_total

    return jax.shard_map(body, mesh=mesh, in_specs=in_specs, out_specs=out_specs, check_vma=False)
```

profile of v0, /device:TPU:7, one launch (start us, length us, event | category | flops | bytes accessed | tf_op | source)
XLA Modules:
  0.0 4084.6 jit_solution(9706343882273143797)
XLA Ops:
  29.7 1023.5 %while.70 = (s32[]{:T(128)}, bf16[2,257,1408]{2,0,1:T(2,128)(2,1)S(1)}, bf16[4,2,257,1408]{3,2,1,0:T(8,128)(2,1)}, s32[7]{0:T(128)}, s32[]{:T(128)}, /*index=5*/...) while((s32[]{:T(128)}, ...), condition=%wide.region_11.12_spmd, body=%wide.region_0.11_spmd.sunk | while | flops 27839043584 | bytes 201163792 | solution.py:174
  71.8 17.9 collective-permute-done
  100.4 368.7 %collective-permute-done = bf16[2,257,1408]{2,0,1:T(2,128)(2,1)S(1)} collective-permute-done((bf16[2,257,1408]{2,0,1:T(2,128)(2,1)}, bf16[2,257,1408]{2,0,1:T(2,128)(2,1)S(1)}, u32[]{:S(2)}, u32[]{:S(2)}) %collective-permute-start) | collective-permute-done | bytes 1447456 | tf_op jit(solution)/shard_map/while/body/eval_jaxpr/ppermute | solution.py:170
  471.0 123.9 %conditional.7 = (bf16[2,257,1408]{2,1,0:T(8,128)(2,1)}, bf16[1,2,257,1408]{3,2,1,0:T(8,128)(2,1)S(1)}) conditional(s32[]{:T(128)} %convert_element_type.835, (s32[]{:T(128)}, bf16[4,2,257,1408]{3,2,1,0:T(8,128)(2,1)}) %tuple.165, (pred[]{:T(512)}, bf16[2,257,1408]{2,0,1:T(2,128)(2,1)S(1)}, bf16[1408]{0:T(1024)(128)(2,1)}, s32[]{:T(128)}, ...), branch_computations={%region_1.1_spmd, %region_2.10_spmd} | conditional | flops 27839043584 | bytes 189543920 | solution.py:168
  527.6 24.2 fusion.105
  551.8 43.0 %fusion.109 = bf16[2,257,1408]{2,1,0:T(8,128)(2,1)} fusion(bf16[1,6144,1408]{2,1,0:T(8,128)(2,1)} %get-tuple-element.1028, f32[2,257,6144]{2,1,0:T(8,128)} %get-tuple-element.1748, f32[6144]{0:T(1024)S(1)} %bitcast.336, bf16[2,257,1408]{2,1,0:T(8,128)(2,1)S(1)} %get-tuple-element.1747, u8[257,6144]{1,0:T(8,128)(4,1)} %get-tuple-element.1580, ...), kind=kOutput, calls=%fused_computation.136 | convolution fusion | flops 9120088064 | bytes 36016640 | tf_op jit(solution)/shard_map/while/body/eval_jaxpr/cond/branch_1_fun/btf,fd->btd/dot_general | solution.py:53
  601.0 17.9 collective-permute-done
  620.7 123.9 %conditional.7 = (bf16[2,257,1408]{2,1,0:T(8,128)(2,1)}, bf16[1,2,257,1408]{3,2,1,0:T(8,128)(2,1)S(1)}) conditional(s32[]{:T(128)} %convert_element_type.835, (s32[]{:T(128)}, bf16[4,2,257,1408]{3,2,1,0:T(8,128)(2,1)}) %tuple.165, (pred[]{:T(512)}, bf16[2,257,1408]{2,0,1:T(2,128)(2,1)S(1)}, bf16[1408]{0:T(1024)(128)(2,1)}, s32[]{:T(128)}, ...), branch_computations={%region_1.1_spmd, %region_2.10_spmd} | conditional | flops 27839043584 | bytes 189543920 | solution.py:168
  677.4 24.2 fusion.105
  701.6 43.0 %fusion.109 = bf16[2,257,1408]{2,1,0:T(8,128)(2,1)} fusion(bf16[1,6144,1408]{2,1,0:T(8,128)(2,1)} %get-tuple-element.1028, f32[2,257,6144]{2,1,0:T(8,128)} %get-tuple-element.1748, f32[6144]{0:T(1024)S(1)} %bitcast.336, bf16[2,257,1408]{2,1,0:T(8,128)(2,1)S(1)} %get-tuple-element.1747, u8[257,6144]{1,0:T(8,128)(4,1)} %get-tuple-element.1580, ...), kind=kOutput, calls=%fused_computation.136 | convolution fusion | flops 9120088064 | bytes 36016640 | tf_op jit(solution)/shard_map/while/body/eval_jaxpr/cond/branch_1_fun/btf,fd->btd/dot_general | solution.py:53
  750.8 17.8 collective-permute-done
  770.5 123.9 %conditional.7 = (bf16[2,257,1408]{2,1,0:T(8,128)(2,1)}, bf16[1,2,257,1408]{3,2,1,0:T(8,128)(2,1)S(1)}) conditional(s32[]{:T(128)} %convert_element_type.835, (s32[]{:T(128)}, bf16[4,2,257,1408]{3,2,1,0:T(8,128)(2,1)}) %tuple.165, (pred[]{:T(512)}, bf16[2,257,1408]{2,0,1:T(2,128)(2,1)S(1)}, bf16[1408]{0:T(1024)(128)(2,1)}, s32[]{:T(128)}, ...), branch_computations={%region_1.1_spmd, %region_2.10_spmd} | conditional | flops 27839043584 | bytes 189543920 | solution.py:168
  827.2 24.2 fusion.105
  851.3 43.0 %fusion.109 = bf16[2,257,1408]{2,1,0:T(8,128)(2,1)} fusion(bf16[1,6144,1408]{2,1,0:T(8,128)(2,1)} %get-tuple-element.1028, f32[2,257,6144]{2,1,0:T(8,128)} %get-tuple-element.1748, f32[6144]{0:T(1024)S(1)} %bitcast.336, bf16[2,257,1408]{2,1,0:T(8,128)(2,1)S(1)} %get-tuple-element.1747, u8[257,6144]{1,0:T(8,128)(4,1)} %get-tuple-element.1580, ...), kind=kOutput, calls=%fused_computation.136 | convolution fusion | flops 9120088064 | bytes 36016640 | tf_op jit(solution)/shard_map/while/body/eval_jaxpr/cond/branch_1_fun/btf,fd->btd/dot_general | solution.py:53
  900.5 17.9 collective-permute-done
  920.2 123.9 %conditional.7 = (bf16[2,257,1408]{2,1,0:T(8,128)(2,1)}, bf16[1,2,257,1408]{3,2,1,0:T(8,128)(2,1)S(1)}) conditional(s32[]{:T(128)} %convert_element_type.835, (s32[]{:T(128)}, bf16[4,2,257,1408]{3,2,1,0:T(8,128)(2,1)}) %tuple.165, (pred[]{:T(512)}, bf16[2,257,1408]{2,0,1:T(2,128)(2,1)S(1)}, bf16[1408]{0:T(1024)(128)(2,1)}, s32[]{:T(128)}, ...), branch_computations={%region_1.1_spmd, %region_2.10_spmd} | conditional | flops 27839043584 | bytes 189543920 | solution.py:168
  976.9 24.2 fusion.105
  1001.1 43.0 %fusion.109 = bf16[2,257,1408]{2,1,0:T(8,128)(2,1)} fusion(bf16[1,6144,1408]{2,1,0:T(8,128)(2,1)} %get-tuple-element.1028, f32[2,257,6144]{2,1,0:T(8,128)} %get-tuple-element.1748, f32[6144]{0:T(1024)S(1)} %bitcast.336, bf16[2,257,1408]{2,1,0:T(8,128)(2,1)S(1)} %get-tuple-element.1747, u8[257,6144]{1,0:T(8,128)(4,1)} %get-tuple-element.1580, ...), kind=kOutput, calls=%fused_computation.136 | convolution fusion | flops 9120088064 | bytes 36016640 | tf_op jit(solution)/shard_map/while/body/eval_jaxpr/cond/branch_1_fun/btf,fd->btd/dot_general | solution.py:53
  1103.6 2416.3 %while.71 = (s32[]{:T(128)}, bf16[2,257,1408]{2,0,1:T(2,128)(2,1)S(1)}, f32[]{:T(128)}, f32[1,1408]{1,0:T(1,128)}, f32[1,1408]{1,0:T(1,128)}, /*index=5*/f32[1,1...) while((s32[]{:T(128)}, ...), condition=%wide.region_51.52_spmd, body=%wide.region_12.51_spmd.sunk | while | flops 81422548992 | bytes 943204480 | solution.py:217
  1105.7 391.2 %conditional.8 = (bf16[2,257,1408]{2,1,0:T(8,128)(2,1)}, f32[]{:T(128)}, f32[1,1408]{1,0:T(1,128)}, f32[1,1408]{1,0:T(1,128)}, f32[1,1408,3,16,88]{1,4,3,2,0:T(8...) conditional(s32[]{:T(128)} %convert_element_type.836, ...), branch_computations={%region_13.13_spmd, %region_14.50_spmd} | conditional | flops 81422548992 | bytes 934518912 | solution.py:211
  1167.6 24.1 fusion.258
  1191.7 32.8 multiply_convert_fusion.1
  1242.2 21.0 conditional.2
  1263.2 24.2 fusion.343
  1342.2 20.6 convert_bitcast_fusion.4
  1362.8 20.8 convert_bitcast_fusion.3
  1410.3 22.3 bitcast_add_fusion.2
  1432.6 30.8 bitcast_add_fusion.1
  1463.4 33.1 bitcast_add_fusion
  1507.7 391.2 %conditional.8 = (bf16[2,257,1408]{2,1,0:T(8,128)(2,1)}, f32[]{:T(128)}, f32[1,1408]{1,0:T(1,128)}, f32[1,1408]{1,0:T(1,128)}, f32[1,1408,3,16,88]{1,4,3,2,0:T(8...) conditional(s32[]{:T(128)} %convert_element_type.836, ...), branch_computations={%region_13.13_spmd, %region_14.50_spmd} | conditional | flops 81422548992 | bytes 934518912 | solution.py:211
  1569.6 24.1 fusion.258
  1593.7 32.8 multiply_convert_fusion.1
  1644.2 21.0 conditional.2
  1665.2 24.2 fusion.343
  1744.2 20.6 convert_bitcast_fusion.4
  1764.8 20.8 convert_bitcast_fusion.3
  1812.3 22.3 bitcast_add_fusion.2
  1834.6 30.8 bitcast_add_fusion.1
  1865.4 33.1 bitcast_add_fusion
  1909.7 391.2 %conditional.8 = (bf16[2,257,1408]{2,1,0:T(8,128)(2,1)}, f32[]{:T(128)}, f32[1,1408]{1,0:T(1,128)}, f32[1,1408]{1,0:T(1,128)}, f32[1,1408,3,16,88]{1,4,3,2,0:T(8...) conditional(s32[]{:T(128)} %convert_element_type.836, ...), branch_computations={%region_13.13_spmd, %region_14.50_spmd} | conditional | flops 81422548992 | bytes 934518912 | solution.py:211
  1971.7 24.1 fusion.258
  1995.7 32.8 multiply_convert_fusion.1
  2046.2 21.0 conditional.2
  2067.2 24.2 fusion.343
  2146.2 20.6 convert_bitcast_fusion.4
  2166.8 20.8 convert_bitcast_fusion.3
  2214.3 22.3 bitcast_add_fusion.2
  2236.6 30.8 bitcast_add_fusion.1
  2267.4 33.1 bitcast_add_fusion
  2311.7 391.2 %conditional.8 = (bf16[2,257,1408]{2,1,0:T(8,128)(2,1)}, f32[]{:T(128)}, f32[1,1408]{1,0:T(1,128)}, f32[1,1408]{1,0:T(1,128)}, f32[1,1408,3,16,88]{1,4,3,2,0:T(8...) conditional(s32[]{:T(128)} %convert_element_type.836, ...), branch_computations={%region_13.13_spmd, %region_14.50_spmd} | conditional | flops 81422548992 | bytes 934518912 | solution.py:211
  2373.7 24.1 fusion.258
  2397.7 32.8 multiply_convert_fusion.1
  2448.2 21.0 conditional.2
  2469.2 24.2 fusion.343
  2548.2 20.6 convert_bitcast_fusion.4
  2568.9 20.8 convert_bitcast_fusion.3
  2616.3 22.3 bitcast_add_fusion.2
  2638.7 30.8 bitcast_add_fusion.1
  2669.5 33.1 bitcast_add_fusion
  2723.1 368.5 %collective-permute-start.1 = (bf16[2,257,1408]{2,0,1:T(2,128)(2,1)S(1)}, bf16[2,257,1408]{2,0,1:T(2,128)(2,1)S(1)}, u32[]{:S(2)}, u32[]{:S(2)}) collective-permute-start(bf16[2,257,1408]{2,0,1:T(2,128)(2,1)S(1)} %copy.139), channel_id=1, source_target_pairs={{1,0},{2,1},{3,2},{5,4},{6,5},{7,6}} | collective-permute-start | bytes 4342280 | tf_op jit(solution)/shard_map/while/body/eval_jaxpr/ppermute | solution.py:212
  3100.0 21.5 collective-permute-start.1
  3129.9 385.8 %collective-permute-start.1 = (bf16[2,257,1408]{2,0,1:T(2,128)(2,1)S(1)}, bf16[2,257,1408]{2,0,1:T(2,128)(2,1)S(1)}, u32[]{:S(2)}, u32[]{:S(2)}) collective-permute-start(bf16[2,257,1408]{2,0,1:T(2,128)(2,1)S(1)} %copy.139), channel_id=1, source_target_pairs={{1,0},{2,1},{3,2},{5,4},{6,5},{7,6}} | collective-permute-start | bytes 4342280 | tf_op jit(solution)/shard_map/while/body/eval_jaxpr/ppermute | solution.py:212
  3520.6 380.1 %all-reduce.1 = (f32[1]{0:T(128)}, f32[1408]{0:T(1024)}, f32[1408]{0:T(1024)}, f32[1408]{0:T(1024)}, f32[1408]{0:T(1024)}, /*index=5*/f32[1000]{0:T(1024)}) all-reduce(f32[1]{0:T(128)} %bitcast.70, f32[1408]{0:T(1024)S(1)} %copy-done.52, f32[1408]{0:T(1024)S(1)} %copy-done.49, ...), channel_id=1, replica_groups=mesh['dp'=2,'pp'=4] {'pp'}, use_global_device_ids=true, to_apply=%region_52.53 | all-reduce | flops 6633 | bytes 53064 | tf_op jit(solution)/shard_map/psum | solution.py:219
  3900.8 167.6 %all-reduce.5.cloned.1.call-done = (f32[588,1408]{1,0:T(8,128)}, f32[257,1408]{1,0:T(8,128)}, f32[1408,1000]{0,1:T(8,128)}) async-done(((f32[588,1408]{1,0:T(8,128)}, f32[257,1408]{1,0:T(8,128)}, f32[1408,1000]{0,1:T(8,128)}), (f32[588,1408]{1,0:T(8,128)}, f32[257,1408]{1,0:T(8,128)}, f32[1408,1000]{0,1:T(8,128)})) %all-reduce.5.cloned.1.call-update) | async-done | bytes 10391056 | tf_op jit(solution)/shard_map/psum | solution.py:220
  (1020 shorter events, 1169.2 us)
Async XLA Ops:
  7.2 4061.2 %all-reduce.5.cloned.1.call-start = ((), (), s32[]{:S(2)}) async-start(), calls=%async_computation | async-start | bytes 20905984 | tf_op jit(solution)/shard_map/psum | solution.py:220
  55.7 5.3 collective-permute-start
  69.2 20.4 collective-permute-start
  97.8 371.2 %collective-permute-start = (bf16[2,257,1408]{2,0,1:T(2,128)(2,1)}, bf16[2,257,1408]{2,0,1:T(2,128)(2,1)S(1)}, u32[]{:S(2)}, u32[]{:S(2)}) collective-permute-start(bf16[2,257,1408]{2,0,1:T(2,128)(2,1)} %copy.138), channel_id=1, source_target_pairs={{0,1},{1,2},{2,3},{4,5},{5,6},{6,7}} | collective-permute-start | bytes 4342280 | tf_op jit(solution)/shard_map/while/body/eval_jaxpr/ppermute | solution.py:170
  471.2 46.0 %copy-start = (bf16[2,257,1408]{2,1,0:T(8,128)(2,1)}, bf16[2,257,1408]{2,1,0:T(8,128)(2,1)S(1)}, u32[]{:S(2)}) copy-start(bf16[2,257,1408]{2,1,0:T(8,128)(2,1)S(1)} %get-tuple-element.2561) | copy-start | bytes 4342276 | tf_op jit(solution)/shard_map/while/body/eval_jaxpr/cond
  551.8 43.0 %copy-start.1 = (bf16[2,257,1408]{2,1,0:T(8,128)(2,1)S(1)}, bf16[2,257,1408]{2,1,0:T(8,128)(2,1)}, u32[]{:S(2)}) copy-start(bf16[2,257,1408]{2,1,0:T(8,128)(2,1)} %copy-done) | copy-start | bytes 4342276 | tf_op jit(solution)/shard_map/while/body/eval_jaxpr/cond
  598.4 20.4 collective-permute-start
  620.9 46.0 %copy-start = (bf16[2,257,1408]{2,1,0:T(8,128)(2,1)}, bf16[2,257,1408]{2,1,0:T(8,128)(2,1)S(1)}, u32[]{:S(2)}) copy-start(bf16[2,257,1408]{2,1,0:T(8,128)(2,1)S(1)} %get-tuple-element.2561) | copy-start | bytes 4342276 | tf_op jit(solution)/shard_map/while/body/eval_jaxpr/cond
  701.6 43.0 %copy-start.1 = (bf16[2,257,1408]{2,1,0:T(8,128)(2,1)S(1)}, bf16[2,257,1408]{2,1,0:T(8,128)(2,1)}, u32[]{:S(2)}) copy-start(bf16[2,257,1408]{2,1,0:T(8,128)(2,1)} %copy-done) | copy-start | bytes 4342276 | tf_op jit(solution)/shard_map/while/body/eval_jaxpr/cond
  748.2 20.4 collective-permute-start
  770.7 46.0 %copy-start = (bf16[2,257,1408]{2,1,0:T(8,128)(2,1)}, bf16[2,257,1408]{2,1,0:T(8,128)(2,1)S(1)}, u32[]{:S(2)}) copy-start(bf16[2,257,1408]{2,1,0:T(8,128)(2,1)S(1)} %get-tuple-element.2561) | copy-start | bytes 4342276 | tf_op jit(solution)/shard_map/while/body/eval_jaxpr/cond
  851.3 43.0 %copy-start.1 = (bf16[2,257,1408]{2,1,0:T(8,128)(2,1)S(1)}, bf16[2,257,1408]{2,1,0:T(8,128)(2,1)}, u32[]{:S(2)}) copy-start(bf16[2,257,1408]{2,1,0:T(8,128)(2,1)} %copy-done) | copy-start | bytes 4342276 | tf_op jit(solution)/shard_map/while/body/eval_jaxpr/cond
  898.0 20.4 collective-permute-start
  920.5 46.0 %copy-start = (bf16[2,257,1408]{2,1,0:T(8,128)(2,1)}, bf16[2,257,1408]{2,1,0:T(8,128)(2,1)S(1)}, u32[]{:S(2)}) copy-start(bf16[2,257,1408]{2,1,0:T(8,128)(2,1)S(1)} %get-tuple-element.2561) | copy-start | bytes 4342276 | tf_op jit(solution)/shard_map/while/body/eval_jaxpr/cond
  1001.1 43.0 %copy-start.1 = (bf16[2,257,1408]{2,1,0:T(8,128)(2,1)S(1)}, bf16[2,257,1408]{2,1,0:T(8,128)(2,1)}, u32[]{:S(2)}) copy-start(bf16[2,257,1408]{2,1,0:T(8,128)(2,1)} %copy-done) | copy-start | bytes 4342276 | tf_op jit(solution)/shard_map/while/body/eval_jaxpr/cond
  1047.7 5.1 collective-permute-start
  1110.2 57.5 %copy-start.53 = (f32[1408]{0:T(1024)}, f32[1408]{0:T(1024)S(1)}, u32[]{:S(2)}) copy-start(f32[1408]{0:T(1024)S(1)} %get-tuple-element.1768) | copy-start | bytes 16900 | tf_op jit(solution)/shard_map/while/body/eval_jaxpr/cond
  1110.9 198.4 %copy-start.27 = (f32[1408]{0:T(1024)}, f32[1408]{0:T(1024)S(1)}, u32[]{:S(2)}) copy-start(f32[1408]{0:T(1024)S(1)} %get-tuple-element.1769) | copy-start | bytes 16900 | tf_op jit(solution)/shard_map/while/body/eval_jaxpr/cond
  1167.0 57.5 %copy-start.2 = (bf16[2,257,1408]{2,1,0:T(8,128)(2,1)}, bf16[2,257,1408]{2,1,0:T(8,128)(2,1)S(1)}, u32[]{:S(2)}) copy-start(bf16[2,257,1408]{2,1,0:T(8,128)(2,1)S(1)} %get-tuple-element.1761) | copy-start | bytes 4342276 | tf_op jit(solution)/shard_map/while/body/eval_jaxpr/cond
  1167.1 142.3 %copy-start.31 = (f32[2,257]{1,0:T(2,128)}, f32[2,257]{1,0:T(2,128)S(1)}, u32[]{:S(2)}) copy-start(f32[2,257]{1,0:T(2,128)S(1)} %broadcast_multiply_fusion.3) | copy-start | bytes 6172 | tf_op jit(solution)/shard_map/while/body/eval_jaxpr/cond
  1167.6 141.7 %copy-start.39 = (f32[2,257]{1,0:T(2,128)}, f32[2,257]{1,0:T(2,128)S(1)}, u32[]{:S(2)}) copy-start(f32[2,257]{1,0:T(2,128)S(1)} %fusion.328) | copy-start | bytes 6172 | tf_op jit(solution)/shard_map/while/body/eval_jaxpr/cond
  1263.2 24.2 copy-start.69
  1263.2 24.2 copy-start.33
  1263.2 25.1 copy-start.57
  1463.4 33.1 copy-start.44
  1463.4 33.1 copy-start.46
  1463.4 33.1 copy-start.70
  1499.4 4.1 collective-permute-start.1
  1512.2 57.5 %copy-start.53 = (f32[1408]{0:T(1024)}, f32[1408]{0:T(1024)S(1)}, u32[]{:S(2)}) copy-start(f32[1408]{0:T(1024)S(1)} %get-tuple-element.1768) | copy-start | bytes 16900 | tf_op jit(solution)/shard_map/while/body/eval_jaxpr/cond
  1512.9 198.4 %copy-start.27 = (f32[1408]{0:T(1024)}, f32[1408]{0:T(1024)S(1)}, u32[]{:S(2)}) copy-start(f32[1408]{0:T(1024)S(1)} %get-tuple-element.1769) | copy-start | bytes 16900 | tf_op jit(solution)/shard_map/while/body/eval_jaxpr/cond
  1569.0 57.5 %copy-start.2 = (bf16[2,257,1408]{2,1,0:T(8,128)(2,1)}, bf16[2,257,1408]{2,1,0:T(8,128)(2,1)S(1)}, u32[]{:S(2)}) copy-start(bf16[2,257,1408]{2,1,0:T(8,128)(2,1)S(1)} %get-tuple-element.1761) | copy-start | bytes 4342276 | tf_op jit(solution)/shard_map/while/body/eval_jaxpr/cond
  1569.1 142.3 %copy-start.31 = (f32[2,257]{1,0:T(2,128)}, f32[2,257]{1,0:T(2,128)S(1)}, u32[]{:S(2)}) copy-start(f32[2,257]{1,0:T(2,128)S(1)} %broadcast_multiply_fusion.3) | copy-start | bytes 6172 | tf_op jit(solution)/shard_map/while/body/eval_jaxpr/cond
  1569.6 141.7 %copy-start.39 = (f32[2,257]{1,0:T(2,128)}, f32[2,257]{1,0:T(2,128)S(1)}, u32[]{:S(2)}) copy-start(f32[2,257]{1,0:T(2,128)S(1)} %fusion.328) | copy-start | bytes 6172 | tf_op jit(solution)/shard_map/while/body/eval_jaxpr/cond
  1665.2 24.2 copy-start.33
  1665.2 25.1 copy-start.57
  1865.4 33.1 copy-start.44
  1865.4 33.1 copy-start.46
  1865.4 33.1 copy-start.70
  1901.5 4.1 collective-permute-start.1
  1914.2 57.5 %copy-start.53 = (f32[1408]{0:T(1024)}, f32[1408]{0:T(1024)S(1)}, u32[]{:S(2)}) copy-start(f32[1408]{0:T(1024)S(1)} %get-tuple-element.1768) | copy-start | bytes 16900 | tf_op jit(solution)/shard_map/while/body/eval_jaxpr/cond
  1914.9 198.4 %copy-start.27 = (f32[1408]{0:T(1024)}, f32[1408]{0:T(1024)S(1)}, u32[]{:S(2)}) copy-start(f32[1408]{0:T(1024)S(1)} %get-tuple-element.1769) | copy-start | bytes 16900 | tf_op jit(solution)/shard_map/while/body/eval_jaxpr/cond
  1971.0 57.5 %copy-start.2 = (bf16[2,257,1408]{2,1,0:T(8,128)(2,1)}, bf16[2,257,1408]{2,1,0:T(8,128)(2,1)S(1)}, u32[]{:S(2)}) copy-start(bf16[2,257,1408]{2,1,0:T(8,128)(2,1)S(1)} %get-tuple-element.1761) | copy-start | bytes 4342276 | tf_op jit(solution)/shard_map/while/body/eval_jaxpr/cond
  1971.1 142.3 %copy-start.31 = (f32[2,257]{1,0:T(2,128)}, f32[2,257]{1,0:T(2,128)S(1)}, u32[]{:S(2)}) copy-start(f32[2,257]{1,0:T(2,128)S(1)} %broadcast_multiply_fusion.3) | copy-start | bytes 6172 | tf_op jit(solution)/shard_map/while/body/eval_jaxpr/cond
  1971.6 141.7 %copy-start.39 = (f32[2,257]{1,0:T(2,128)}, f32[2,257]{1,0:T(2,128)S(1)}, u32[]{:S(2)}) copy-start(f32[2,257]{1,0:T(2,128)S(1)} %fusion.328) | copy-start | bytes 6172 | tf_op jit(solution)/shard_map/while/body/eval_jaxpr/cond
  2067.2 24.2 copy-start.33
  2067.2 25.1 copy-start.57
  2267.4 33.1 copy-start.44
  2267.4 33.1 copy-start.46
  2267.4 33.1 copy-start.70
  2303.5 4.1 collective-permute-start.1
  2316.2 57.5 %copy-start.53 = (f32[1408]{0:T(1024)}, f32[1408]{0:T(1024)S(1)}, u32[]{:S(2)}) copy-start(f32[1408]{0:T(1024)S(1)} %get-tuple-element.1768) | copy-start | bytes 16900 | tf_op jit(solution)/shard_map/while/body/eval_jaxpr/cond
  2316.9 198.4 %copy-start.27 = (f32[1408]{0:T(1024)}, f32[1408]{0:T(1024)S(1)}, u32[]{:S(2)}) copy-start(f32[1408]{0:T(1024)S(1)} %get-tuple-element.1769) | copy-start | bytes 16900 | tf_op jit(solution)/shard_map/while/body/eval_jaxpr/cond
  2373.0 57.5 %copy-start.2 = (bf16[2,257,1408]{2,1,0:T(8,128)(2,1)}, bf16[2,257,1408]{2,1,0:T(8,128)(2,1)S(1)}, u32[]{:S(2)}) copy-start(bf16[2,257,1408]{2,1,0:T(8,128)(2,1)S(1)} %get-tuple-element.1761) | copy-start | bytes 4342276 | tf_op jit(solution)/shard_map/while/body/eval_jaxpr/cond
  2373.1 142.3 %copy-start.31 = (f32[2,257]{1,0:T(2,128)}, f32[2,257]{1,0:T(2,128)S(1)}, u32[]{:S(2)}) copy-start(f32[2,257]{1,0:T(2,128)S(1)} %broadcast_multiply_fusion.3) | copy-start | bytes 6172 | tf_op jit(solution)/shard_map/while/body/eval_jaxpr/cond
  2373.6 141.7 %copy-start.39 = (f32[2,257]{1,0:T(2,128)}, f32[2,257]{1,0:T(2,128)S(1)}, u32[]{:S(2)}) copy-start(f32[2,257]{1,0:T(2,128)S(1)} %fusion.328) | copy-start | bytes 6172 | tf_op jit(solution)/shard_map/while/body/eval_jaxpr/cond
  2469.2 24.2 copy-start.33
  2469.2 25.1 copy-start.57
  2669.4 33.1 copy-start.44
  2669.4 33.1 copy-start.46
  2669.4 33.1 copy-start.70
  2705.5 4.1 collective-permute-start.1
  2723.1 371.2 %collective-permute-start.1 = (bf16[2,257,1408]{2,0,1:T(2,128)(2,1)S(1)}, bf16[2,257,1408]{2,0,1:T(2,128)(2,1)S(1)}, u32[]{:S(2)}, u32[]{:S(2)}) collective-permute-start(bf16[2,257,1408]{2,0,1:T(2,128)(2,1)S(1)} %copy.139), channel_id=1, source_target_pairs={{1,0},{2,1},{3,2},{5,4},{6,5},{7,6}} | collective-permute-start | bytes 4342280 | tf_op jit(solution)/shard_map/while/body/eval_jaxpr/ppermute | solution.py:212
  3100.0 24.3 collective-permute-start.1
  3129.9 388.6 %collective-permute-start.1 = (bf16[2,257,1408]{2,0,1:T(2,128)(2,1)S(1)}, bf16[2,257,1408]{2,0,1:T(2,128)(2,1)S(1)}, u32[]{:S(2)}, u32[]{:S(2)}) collective-permute-start(bf16[2,257,1408]{2,0,1:T(2,128)(2,1)S(1)} %copy.139), channel_id=1, source_target_pairs={{1,0},{2,1},{3,2},{5,4},{6,5},{7,6}} | collective-permute-start | bytes 4342280 | tf_op jit(solution)/shard_map/while/body/eval_jaxpr/ppermute | solution.py:212
  (235 other events, 2670.9 us)
Sparse Core Ops, SparseCore 0:
  3520.1 548.2 all-reduce.4
where the time goes:
time: 4090 us; the launch traced here: 4080 us
  matrix products  1590 us (39%)
  starting transfers between devices  790 us (19%)
  waiting for transfers between devices  632 us (15%)
  other arithmetic  399 us (10%)
  blocking collectives  380 us (9%)
  local copies, waits for them, and re-layouts  220 us (5%)
  loops' own time  53.2 us (1%)
    ppermute x7, starting transfers between devices, backward_step(): received = lax.ppermute(grad_in, 'pp', backward_perm)  781 us
    ppermute x7, waiting for transfers between devices, forward_step(): received = lax.ppermute(stage_out, 'pp', forward_perm)  445 us
    psum x1, blocking collectives, body(): loss_total = lax.psum(loss_acc, 'pp')  380 us
    dot_general x8, matrix products, layer_forward(): jnp.einsum('btf,fd->btd', activ, w_fc2, preferred_element_type=jnp.float32)  243 us
    dot_general x8, matrix products, layer_forward(): jnp.einsum('btd,df->btf', normed_mlp, w_fc1, preferred_element_type=jnp.f...  193 us
    psum x1, waiting for transfers between devices, body(): embed_total = tuple((lax.psum(tensor, 'pp') for tensor in embed_acc))  168 us
    sub x8, other arithmetic, attention_forward(): probs_full = jax.nn.softmax(scores, axis=-1)  134 us
    dot_general x4, matrix products, layer_backward(): jnp.einsum('btf,btd->fd', activ, grad_out, preferred_element_type=jnp.flo...  132 us
  transfers between devices with their start and end apart: 15, of which 15 were waited for; matrix products, arithmetic and copies ran while one was open for 0% of the time, Pallas kernels for 0%

commit v1 on v0

v1 whole, which is shorter than its diff:
```python
import functools
import jax
import jax.numpy as jnp
from jax import lax
from jax.sharding import PartitionSpec as P

EPS = 1e-6
SMOOTH = 0.1
F32 = jnp.float32
BF16 = jnp.bfloat16
exact_gelu = functools.partial(jax.nn.gelu, approximate=False)


def layer_norm(hidden, gain, bias):
    values = hidden.astype(F32)
    centered = values - jnp.mean(values, axis=-1, keepdims=True)
    variance = jnp.mean(jnp.square(centered), axis=-1, keepdims=True)
    return (centered * lax.rsqrt(variance + EPS) * gain + bias).astype(BF16)


def norm_backward(grad, hidden, gain):
    values = hidden.astype(F32)
    centered = values - jnp.mean(values, axis=-1, keepdims=True)
    inv = lax.rsqrt(jnp.mean(jnp.square(centered), axis=-1, keepdims=True) + EPS)
    unit = centered * inv
    grad = grad.astype(F32)
    scaled = grad * gain
    grad_in = inv * (scaled - jnp.mean(scaled, axis=-1, keepdims=True) - unit * jnp.mean(scaled * unit, axis=-1, keepdims=True))
    return grad_in, jnp.sum(grad * unit, axis=(0, 1)), jnp.sum(grad, axis=(0, 1))


def dot(spec, left, right):
    return jnp.einsum(spec, left, right, preferred_element_type=F32)


def layer_forward(hidden, weights):
    ln1_gain, ln1_bias, w_qkv, b_qkv, w_proj, b_proj, ln2_gain, ln2_bias, w_fc1, b_fc1, w_fc2, b_fc2 = weights
    scale = w_qkv.shape[-1] ** -0.5
    normed = layer_norm(hidden, ln1_gain, ln1_bias)
    qkv = (dot("btd,dkhe->btkhe", normed, w_qkv) + b_qkv).astype(BF16)
    scores = dot("bqhe,bkhe->bhqk", qkv[:, :, 0], qkv[:, :, 1]) * scale
    probs = jax.nn.softmax(scores, axis=-1)
    context = dot("bhqk,bkhe->bqhe", probs.astype(BF16), qkv[:, :, 2]).astype(BF16)
    mid = (hidden.astype(F32) + dot("bthe,hed->btd", context, w_proj) + b_proj).astype(BF16)
    normed_mlp = layer_norm(mid, ln2_gain, ln2_bias)
    pre_act = dot("btd,df->btf", normed_mlp, w_fc1) + b_fc1
    activ = exact_gelu(pre_act).astype(BF16)
    out = (mid.astype(F32) + dot("btf,fd->btd", activ, w_fc2) + b_fc2).astype(BF16)
    return out, (hidden, normed, qkv, probs, context, mid, normed_mlp, pre_act, activ)


def layer_backward(grad_out, weights, saved):
    ln1_gain, ln1_bias, w_qkv, b_qkv, w_proj, b_proj, ln2_gain, ln2_bias, w_fc1, b_fc1, w_fc2, b_fc2 = weights
    hidden, normed, qkv, probs, context, mid, normed_mlp, pre_act, activ = saved
    scale = w_qkv.shape[-1] ** -0.5
    grad_activ = dot("btd,fd->btf", grad_out, w_fc2).astype(BF16)
    grad_pre = jax.vjp(exact_gelu, pre_act)[1](grad_activ.astype(F32))[0]
    g_b_fc1 = jnp.sum(grad_pre, axis=(0, 1))
    grad_pre = grad_pre.astype(BF16)
    grad_normed_mlp = dot("btf,df->btd", grad_pre, w_fc1).astype(BF16)
    grad_mid, g_ln2_gain, g_ln2_bias = norm_backward(grad_normed_mlp, mid, ln2_gain)
    grad_mid = (grad_out.astype(F32) + grad_mid).astype(BF16)
    grad_context = dot("btd,hed->bthe", grad_mid, w_proj).astype(BF16)
    grad_probs = dot("bqhe,bkhe->bhqk", grad_context, qkv[:, :, 2])
    grad_value = dot("bhqk,bqhe->bkhe", probs.astype(BF16), grad_context).astype(BF16)
    grad_scores = probs * (grad_probs - jnp.sum(grad_probs * probs, axis=-1, keepdims=True))
    grad_scores = (grad_scores * scale).astype(BF16)
    grad_query = dot("bhqk,bkhe->bqhe", grad_scores, qkv[:, :, 1]).astype(BF16)
    grad_key = dot("bhqk,bqhe->bkhe", grad_scores, qkv[:, :, 0]).astype(BF16)
    grad_qkv = jnp.stack([grad_query, grad_key, grad_value], axis=2)
    grad_normed = dot("btkhe,dkhe->btd", grad_qkv, w_qkv).astype(BF16)
    grad_hidden, g_ln1_gain, g_ln1_bias = norm_backward(grad_normed, hidden, ln1_gain)
    grad_hidden = (grad_mid.astype(F32) + grad_hidden).astype(BF16)
    return grad_hidden, (grad_out, grad_pre, grad_mid, grad_qkv), (g_ln1_gain, g_ln1_bias, g_ln2_gain, g_ln2_bias, g_b_fc1)


def solution(mesh):
    stages = mesh.shape["pp"]
    forward_perm = [(index, index + 1) for index in range(stages - 1)]
    backward_perm = [(index + 1, index) for index in range(stages - 1)]
    in_specs = (P("dp"), P("dp"), P(), P(), P(), P()) + (P("pp"),) * 12 + (P(),) * 4
    out_specs = (P("dp"),) * 5 + (P(("dp", "pp")),) * 12 + (P("dp"),) * 4

    def body(patches, labels, w_patch, b_patch, cls_token, pos_embed, *rest):
        weights = [tensor[0] for tensor in rest[:12]]
        for index in (0, 1, 3, 5, 6, 7, 9, 11):
            weights[index] = weights[index].astype(F32)
        weights = tuple(weights)
        lnf_gain, lnf_bias, w_head, b_head = rest[12:]
        stage = lax.axis_index("pp")
        is_first = stage == 0
        is_last = stage == stages - 1
        micros, batch = labels.shape
        tokens, width = pos_embed.shape
        inv_count = 1.0 / (micros * batch)
        steps = micros + stages - 1

        projected = dot("mbnp,pd->mbnd", patches, w_patch) + b_patch.astype(F32)
        first = jnp.broadcast_to(cls_token.astype(F32), (micros, batch, 1, width))
        embedded = (jnp.concatenate([first, projected], axis=2) + pos_embed.astype(F32)).astype(BF16)

        received = embedded[0]
        saves, outs = [], []
        for step in range(steps):
            stage_in = jnp.where(is_first, embedded[min(step, micros - 1)], received)
            out, saved = layer_forward(stage_in, weights)
            saves.append(saved)
            outs.append(out)
            if step < steps - 1:
                received = lax.ppermute(out, "pp", forward_perm)
        tops = jnp.stack([out[:, 0] for out in outs[stages - 1:]])
        tops = lax.all_gather(tops, "pp")[stages - 1].reshape(micros * batch, width)

        pooled, lnf_vjp = jax.vjp(layer_norm, tops, lnf_gain.astype(F32), lnf_bias.astype(F32))
        logits = jnp.dot(pooled, w_head, preferred_element_type=F32) + b_head.astype(F32)
        classes = logits.shape[-1]
        log_probs = jax.nn.log_softmax(logits, axis=-1)
        target = (1.0 - SMOOTH) * jax.nn.one_hot(labels.reshape(-1), classes, dtype=F32) + SMOOTH / classes
        loss = -jnp.sum(target * log_probs) * inv_count
        grad_logits = (jnp.exp(log_probs) - target) * inv_count
        grad_low = grad_logits.astype(BF16)
        g_w_head = dot("bd,bc->dc", pooled, grad_low)
        g_b_head = jnp.sum(grad_logits, axis=0)
        grad_pooled = dot("bc,dc->bd", grad_low, w_head).astype(BF16)
        grad_tops, g_lnf_gain, g_lnf_bias = lnf_vjp(grad_pooled)
        grad_tops = grad_tops.reshape(micros, batch, 1, width)
        grad_tops = jnp.concatenate([grad_tops, jnp.zeros((micros, batch, tokens - 1, width), BF16)], axis=2)

        stacks = [jnp.stack(group) for group in zip(*saves)]
        received = grad_tops[0]
        parts, smalls, grads_in = [], [], []
        for step in range(steps):
            grad_out = jnp.where(is_last, grad_tops[min(step, micros - 1)], received)
            slot = jnp.clip(step - (stages - 1) + 2 * stage, 0, steps - 1)
            saved = tuple(lax.dynamic_index_in_dim(stack, slot, 0, keepdims=False) for stack in stacks)
            grad_in, part, small = layer_backward(grad_out, weights, saved)
            micro = step - (stages - 1 - stage)
            valid = (micro >= 0) & (micro < micros)
            parts.append(part)
            smalls.append(tuple(jnp.where(valid, piece, 0.0) for piece in small))
            grads_in.append(grad_in)
            if step < steps - 1:
                received = lax.ppermute(grad_in, "pp", backward_perm)

        g_ln1_gain, g_ln1_bias, g_ln2_gain, g_ln2_bias, g_b_fc1 = (sum(group) for group in zip(*smalls))
        window = lambda stack, start: lax.dynamic_slice_in_dim(stack, start, micros, 0)
        grad_out, grad_pre, grad_mid, grad_qkv = (window(jnp.stack(group), stages - 1 - stage) for group in zip(*parts))
        normed, context, normed_mlp, activ = (window(stacks[index], stage) for index in (1, 4, 6, 8))
        total = lambda grad: jnp.sum(grad.astype(F32), axis=(0, 1, 2))
        grad_embedded = jnp.stack(grads_in[stages - 1:])
        mine = grad_embedded
        for other in range(1, stages):
            moved = lax.ppermute(mine, "pp", [(0, other)])
            grad_embedded = jnp.where(stage == other, moved, grad_embedded)
        layer_grads = (
            g_ln1_gain, g_ln1_bias,
            dot("mbtd,mbtkhe->dkhe", normed, grad_qkv), total(grad_qkv),
            dot("mbthe,mbtd->hed", context, grad_mid), total(grad_mid),
            g_ln2_gain, g_ln2_bias,
            dot("mbtd,mbtf->df", normed_mlp, grad_pre), g_b_fc1,
            dot("mbtf,mbtd->fd", activ, grad_out), total(grad_out),
        )
        g_pos_embed = jnp.sum(grad_embedded.astype(F32), axis=(0, 1))
        embed_grads = (
            dot("mbnp,mbnd->pd", patches, grad_embedded[:, :, 1:]),
            jnp.sum(g_pos_embed[1:], axis=0), g_pos_embed[0], g_pos_embed,
        )
        return (loss.reshape(1),) + embed_grads + tuple(grad[None] for grad in layer_grads) + (g_lnf_gain, g_lnf_bias, g_w_head, g_b_head)

    return jax.shard_map(body, mesh=mesh, in_specs=in_specs, out_specs=out_specs, check_vma=False)
```

time: 4090 us -> 2620 us (0.64)
  starting transfers between devices: 790 us -> 83 us
  waiting for transfers between devices: 632 us -> 0.04 us
  other arithmetic: 399 us -> 790 us
  blocking collectives: 380 us -> 13.2 us
  local copies, waits for them, and re-layouts: 220 us -> 104 us
  loops' own time: 53.2 us -> 0 us
    ppermute x14 -> x15, starting transfers between devices: 790 us -> 83 us  [the longest x6 66.8 us: body(): received = lax.ppermute(grad_in, 'pp', backward_perm)]
    ppermute x14 -> x15, waiting for transfers between devices: 465 us -> 0.04 us  [the longest x6 0.02 us: body(): received = lax.ppermute(grad_in, 'pp', backward_perm)]
    unnamed x0 -> x50, other arithmetic: none -> 433 us
    psum x1 -> x0, blocking collectives: 380 us -> none  [body(): loss_total = lax.psum(loss_acc, 'pp')]
    psum x1 -> x0, waiting for transfers between devices: 168 us -> none  [body(): embed_total = tuple((lax.psum(tensor, 'pp') for tensor in embed_acc))]
    convert_element_type x64 -> x22, other arithmetic: 187 us -> 34.5 us  [the longest x6 16.3 us: layer_backward(): grad_hidden = (grad_mid.astype(F32) + grad_hidden).astype(BF16)]
    sub x0 -> x7, matrix products: none -> 90.2 us  [layer_backward(): grad_probs - jnp.sum(grad_probs * probs, axis=-1, keepdims=True)]
    cond x578 -> x0, local copies, waits for them, and re-layouts: 81.5 us -> none
  transfers between devices with their start and end apart: 15 -> 15, of which waited for: 15 -> 0; matrix products, arithmetic and copies ran while one was open for 0% -> 17% of each run, Pallas kernels for 0% -> 0%
where the time goes in v1:
time: 2620 us; the launch traced here: 2610 us
  matrix products  1610 us (61%)
  other arithmetic  790 us (30%)
  local copies, waits for them, and re-layouts  104 us (4%)
  starting transfers between devices  83 us (3%)
    dot_general x106, matrix products, dot(): return jnp.einsum(spec, left, right, preferred_element_type=F32)  1520 us
    unnamed x50, other arithmetic  433 us
    sub x7, other arithmetic, layer_forward(): probs = jax.nn.softmax(scores, axis=-1)  119 us
    sub x7, matrix products, layer_backward(): grad_probs - jnp.sum(grad_probs * probs, axis=-1, keepdims=True)  90.2 us
    ppermute x6, starting transfers between devices, body(): received = lax.ppermute(grad_in, 'pp', backward_perm)  66.8 us
    another operation x6, other arithmetic, body(): stacks = [jnp.stack(group) for group in zip(*saves)]  63.9 us
  transfers between devices with their start and end apart: 15, of which 0 were waited for; matrix products, arithmetic and copies ran while one was open for 17% of the time, Pallas kernels for 0%

profile of v1, /device:TPU:7, one launch (start us, length us, event | category | flops | bytes accessed | tf_op | source)
XLA Modules:
  0.0 2608.8 jit_solution(8503823209991903633)
XLA Ops:
  27.6 16.2 bitcast_dynamic-update-slice_fusion.41
  53.9 17.0 fusion.1178
  85.8 24.7 fusion.669
  110.5 33.3 %bitcast_dynamic-update-slice_fusion.20 = (bf16[7,2,257,6144]{3,2,1,0:T(8,128)(2,1)}, bf16[2,257,6144]{2,1,0:T(8,128)(2,1)S(1)}) fusion(u8[257,6144]{1,0:T(8,128)(4,1)} %get-tuple-element.34, u8[257,6144]{1,0:T(8,128)(4,1)} %get-tuple-element.33, f32[2,257,6144]{2,1,0:T(8,128)} %get-tuple-element.204, f32[6144]{0:T(1024)S(1)} %bitcast.2366), kind=kLoop, calls=%fused_computation.581 | loop fusion | flops 224219136 | bytes 28618752
  143.8 14.9 fusion.691
  198.4 15.8 bitcast_dynamic-update-slice_fusion.40
  224.4 17.0 fusion.1179
  254.9 24.7 fusion.670
  279.6 33.0 %bitcast_dynamic-update-slice_fusion.19 = (bf16[7,2,257,6144]{3,2,1,0:T(8,128)(2,1)}, bf16[2,257,6144]{2,1,0:T(8,128)(2,1)S(1)}) fusion(bf16[7,2,257,6144]{3,2,1,0:T(8,128)(2,1)} %get-tuple-element.136, u8[257,6144]{1,0:T(8,128)(4,1)} %get-tuple-element.32, u8[257,6144]{1,0:T(8,128)(4,1)} %get-tuple-element.31, f32[2,257,6144]{2,1,0:T(8,128)} %get-tuple-element.209, ...), kind=kLoop, calls=%fused_computation.580 | loop fusion | flops 224219136 | bytes 29048832
  312.6 14.9 fusion.688
  362.9 15.8 bitcast_dynamic-update-slice_fusion.39
  388.8 17.0 fusion.1180
  419.4 24.7 fusion.671
  444.1 33.0 %bitcast_dynamic-update-slice_fusion.18 = (bf16[7,2,257,6144]{3,2,1,0:T(8,128)(2,1)}, bf16[2,257,6144]{2,1,0:T(8,128)(2,1)S(1)}) fusion(bf16[7,2,257,6144]{3,2,1,0:T(8,128)(2,1)} %get-tuple-element.134, u8[257,6144]{1,0:T(8,128)(4,1)} %get-tuple-element.30, u8[257,6144]{1,0:T(8,128)(4,1)} %get-tuple-element.29, f32[2,257,6144]{2,1,0:T(8,128)} %get-tuple-element.214, ...), kind=kLoop, calls=%fused_computation.579 | loop fusion | flops 224219136 | bytes 29048832
  477.1 14.9 fusion.685
  527.5 15.8 bitcast_dynamic-update-slice_fusion.38
  553.4 17.0 fusion.1181
  584.0 24.7 fusion.672
  608.6 33.0 %bitcast_dynamic-update-slice_fusion.17 = (bf16[7,2,257,6144]{3,2,1,0:T(8,128)(2,1)}, bf16[2,257,6144]{2,1,0:T(8,128)(2,1)S(1)}) fusion(bf16[7,2,257,6144]{3,2,1,0:T(8,128)(2,1)} %get-tuple-element.132, u8[257,6144]{1,0:T(8,128)(4,1)} %get-tuple-element.28, u8[257,6144]{1,0:T(8,128)(4,1)} %get-tuple-element.27, f32[2,257,6144]{2,1,0:T(8,128)} %get-tuple-element.219, ...), kind=kLoop, calls=%fused_computation.578 | loop fusion | flops 224219136 | bytes 29048832
  641.7 14.8 fusion.682
  690.7 15.8 bitcast_dynamic-update-slice_fusion.37
  716.6 17.0 fusion.1182
  747.2 24.7 fusion.673
  771.9 33.0 %bitcast_dynamic-update-slice_fusion.16 = (bf16[7,2,257,6144]{3,2,1,0:T(8,128)(2,1)}, bf16[2,257,6144]{2,1,0:T(8,128)(2,1)S(1)}) fusion(bf16[7,2,257,6144]{3,2,1,0:T(8,128)(2,1)} %get-tuple-element.130, u8[257,6144]{1,0:T(8,128)(4,1)} %get-tuple-element.26, u8[257,6144]{1,0:T(8,128)(4,1)} %get-tuple-element.25, f32[2,257,6144]{2,1,0:T(8,128)} %get-tuple-element.224, ...), kind=kLoop, calls=%fused_computation.577 | loop fusion | flops 224219136 | bytes 29048832
  804.9 14.8 fusion.679
  853.9 15.8 bitcast_dynamic-update-slice_fusion.36
  879.8 17.0 fusion.1183
  910.4 24.7 fusion.674
  935.1 33.0 %bitcast_dynamic-update-slice_fusion.15 = (bf16[7,2,257,6144]{3,2,1,0:T(8,128)(2,1)}, bf16[2,257,6144]{2,1,0:T(8,128)(2,1)S(1)}) fusion(bf16[7,2,257,6144]{3,2,1,0:T(8,128)(2,1)} %get-tuple-element.128, u8[257,6144]{1,0:T(8,128)(4,1)} %get-tuple-element.24, u8[257,6144]{1,0:T(8,128)(4,1)} %get-tuple-element.23, f32[2,257,6144]{2,1,0:T(8,128)} %get-tuple-element.229, ...), kind=kLoop, calls=%fused_computation.576 | loop fusion | flops 224219136 | bytes 29048832
  968.1 14.8 fusion.676
  1016.6 15.8 bitcast_dynamic-update-slice_fusion.35
  1042.5 17.0 fusion.1184
  1074.0 24.7 fusion.675
  1098.7 32.9 %bitcast_dynamic-update-slice_fusion.14 = (bf16[7,2,257,6144]{3,2,1,0:T(8,128)(2,1)}, bf16[2,257,6144]{2,1,0:T(8,128)(2,1)S(1)}) fusion(bf16[7,2,257,6144]{3,2,1,0:T(8,128)(2,1)} %get-tuple-element.126, u8[257,6144]{1,0:T(8,128)(4,1)} %get-tuple-element.22, u8[257,6144]{1,0:T(8,128)(4,1)} %get-tuple-element.21, f32[2,257,6144]{2,1,0:T(8,128)} %get-tuple-element.234, ...), kind=kLoop, calls=%fused_computation.575 | loop fusion | flops 224219136 | bytes 29048832 | tf_op jit(solution)/shard_map/stack | solution.py:129
  1164.4 29.4 %dynamic-slice_bitcast_fusion = (bf16[2,257,3,16,88]{4,1,3,2,0:T(8,128)(2,1)}, bf16[2,257,3,16,88]{4,1,3,2,0:T(8,128)(2,1)}, bf16[2,257,3,16,88]{4,1,3,2,0:T(8,1...) fusion(bf16[7,2,257,3,16,88]{5,2,4,3,1,0:T(8,128)(2,1)} %get-tu, ...), kind=kLoop, calls=%fused_computation.603 | loop fusion | bytes 60791836 | tf_op jit(solution)/shard_map/jit(dynamic_index_in_dim)/squeeze | solution.py:135
  1230.2 43.2 %bitcast_dynamic-update-slice_fusion.27 = (bf16[7,2,257,6144]{3,2,1,0:T(8,128)(2,1)}, f32[2,257,6144]{2,1,0:T(8,128)}) fusion(bf16[1,6144,1408]{2,1,0:T(8,128)(2,1)} %param.38, bf16[4,2,1,1408]{3,2,1,0:T(2,128)(2,1)S(1)} %reshape.1217, f32[7,2,257,6144]{3,2,1,0:T(8,128)} %bitcast_dynamic-update-slice_fusion, s32[]{:T(128)S(6)} %min.22), kind=kOutput, calls=%fused_computation.588 | convolution fusion | flops 9126666240 | bytes 49420292 | tf_op jit(solution)/shard_map/btd,fd->btf/dot_general | solution.py:33
  1273.5 20.8 fusion.965
  1360.3 16.3 fusion.966
  1389.9 44.1 %bitcast_dynamic-update-slice_fusion.26 = (bf16[7,2,257,6144]{3,2,1,0:T(8,128)(2,1)}, f32[2,257,6144]{2,1,0:T(8,128)}) fusion(bf16[7,2,257,6144]{3,2,1,0:T(8,128)(2,1)} %get-tuple-element.280, bf16[1,6144,1408]{2,1,0:T(8,128)(2,1)} %param.38, bf16[4,2,1,1408]{3,2,1,0:T(2,128)(2,1)S(1)} %reshape.1217, bf16[2,257,1408]{2,0,1:T(2,128)(2,1)S(1)} %collective-permute-done.6, ...), kind=kOutput, calls=%fused_computation.587 | convolution fusion | flops 9127390208 | bytes 51211780 | tf_op jit(solution)/shard_map/btd,fd->btf/dot_general | solution.py:33
  1434.0 19.1 fusion.967
  1510.7 14.4 fusion.968
  1546.8 44.1 %bitcast_dynamic-update-slice_fusion.25 = (bf16[7,2,257,6144]{3,2,1,0:T(8,128)(2,1)}, f32[2,257,6144]{2,1,0:T(8,128)}) fusion(bf16[7,2,257,6144]{3,2,1,0:T(8,128)(2,1)} %get-tuple-element.282, bf16[1,6144,1408]{2,1,0:T(8,128)(2,1)} %param.38, bf16[4,2,1,1408]{3,2,1,0:T(2,128)(2,1)S(1)} %reshape.1217, bf16[2,257,1408]{2,0,1:T(2,128)(2,1)S(1)} %collective-permute-done.7, ...), kind=kOutput, calls=%fused_computation.586 | convolution fusion | flops 9127390208 | bytes 51211780 | tf_op jit(solution)/shard_map/btd,fd->btf/dot_general | solution.py:33
  1590.9 19.3 fusion.969
  1667.5 14.5 fusion.970
  1685.8 16.3 collective-permute-start.8
  1708.7 44.1 %bitcast_dynamic-update-slice_fusion.24 = (bf16[7,2,257,6144]{3,2,1,0:T(8,128)(2,1)}, f32[2,257,6144]{2,1,0:T(8,128)}) fusion(bf16[7,2,257,6144]{3,2,1,0:T(8,128)(2,1)} %get-tuple-element.284, bf16[1,6144,1408]{2,1,0:T(8,128)(2,1)} %param.38, bf16[2,257,1408]{2,0,1:T(2,128)(2,1)S(1)} %collective-permute-done.8, pred[]{:T(512)S(6)} %eq.40, ...), kind=kOutput, calls=%fused_computation.585 | convolution fusion | flops 9127390208 | bytes 51211780 | tf_op jit(solution)/shard_map/btd,fd->btf/dot_general | solution.py:33
  1752.8 19.3 fusion.971
  1829.3 14.5 fusion.972
  1867.8 44.0 %bitcast_dynamic-update-slice_fusion.23 = (bf16[7,2,257,6144]{3,2,1,0:T(8,128)(2,1)}, f32[2,257,6144]{2,1,0:T(8,128)}) fusion(bf16[7,2,257,6144]{3,2,1,0:T(8,128)(2,1)} %get-tuple-element.286, bf16[1,6144,1408]{2,1,0:T(8,128)(2,1)} %param.38, bf16[2,257,1408]{2,0,1:T(2,128)(2,1)S(1)} %collective-permute-done.9, pred[]{:T(512)S(6)} %eq.40, ...), kind=kOutput, calls=%fused_computation.584 | convolution fusion | flops 9127390208 | bytes 51211780 | tf_op jit(solution)/shard_map/btd,fd->btf/dot_general | solution.py:33
  1911.9 19.3 fusion.973
  1962.9 14.2 fusion.163
  1988.6 14.4 fusion.974
  2007.9 15.2 collective-permute-start.10
  2055.5 44.3 %bitcast_dynamic-update-slice_fusion.22 = (bf16[7,2,257,6144]{3,2,1,0:T(8,128)(2,1)}, f32[2,257,6144]{2,1,0:T(8,128)}) fusion(bf16[7,2,257,6144]{3,2,1,0:T(8,128)(2,1)} %get-tuple-element.288, bf16[1,6144,1408]{2,1,0:T(8,128)(2,1)} %param.38, bf16[2,257,1408]{2,0,1:T(2,128)(2,1)} %collective-permute-done.10, pred[]{:T(512)S(6)} %eq.40, ...), kind=kOutput, calls=%fused_computation.583 | convolution fusion | flops 9127390208 | bytes 51211780 | tf_op jit(solution)/shard_map/btd,fd->btf/dot_general | solution.py:33
  2099.8 19.5 fusion.975
  2176.9 14.5 fusion.976
  2234.6 44.7 %bitcast_dynamic-update-slice_fusion.21 = (bf16[7,2,257,6144]{3,2,1,0:T(8,128)(2,1)}, f32[2,257,6144]{2,1,0:T(8,128)}) fusion(bf16[7,2,257,6144]{3,2,1,0:T(8,128)(2,1)} %get-tuple-element.290, bf16[1,6144,1408]{2,1,0:T(8,128)(2,1)} %param.38, bf16[2,257,1408]{2,0,1:T(2,128)(2,1)} %collective-permute-done.11, pred[]{:T(512)S(6)} %eq.40, ...), kind=kOutput, calls=%fused_computation.582 | convolution fusion | flops 9127390208 | bytes 51211780 | tf_op jit(solution)/shard_map/btd,fd->btf/dot_general | solution.py:33
  2285.2 18.5 fusion.977
  2336.2 14.2 fusion.157
  2412.6 24.3 convert_reduce_fusion
  2437.0 15.0 fusion.423
  2452.0 48.4 %fusion.23 = f32[1,1408,6144]{2,1,0:T(8,128)} fusion(bf16[7,2,257,6144]{3,2,1,0:T(8,128)(2,1)} %get-tuple-element.292, s32[]{:T(128)S(6)} %select_n.659, bf16[7,2,257,1408]{3,2,1,0:T(8,128)(2,1)} %get-tuple-element.185, s32[]{:T(128)S(6)} %select_n.658), kind=kOutput, calls=%fused_computation.22 | convolution fusion | flops 35571892224 | bytes 66502664 | tf_op jit(solution)/shard_map/mbtd,mbtf->df/dot_general | solution.py:33
  2500.5 51.0 %fusion.20 = f32[1,6144,1408]{2,1,0:T(8,128)} fusion(bf16[4,2,257,1408]{3,2,1,0:T(8,128)(2,1)S(1)} %bitcast.2364, bf16[7,2,257,6144]{3,2,1,0:T(8,128)(2,1)} %get-tuple-element.124, s32[]{:T(128)S(6)} %select_n.658), kind=kOutput, calls=%fused_computation.21 | convolution fusion | flops 35571892224 | bytes 66344964 | tf_op jit(solution)/shard_map/mbtf,mbtd->fd/dot_general | solution.py:33
  2552.2 37.4 %fusion.82 = f32[1,1408,3,16,88]{1,4,3,2,0:T(8,128)} fusion(bf16[4,2,257,3,16,88]{2,5,4,1,3,0:T(8,128)(2,1)} %get-tuple-element.153, bf16[7,2,257,1408]{3,2,1,0:T(8,128)(2,1)S(1)} %copy-done.126, s32[]{:T(128)S(6)} %select_n.658), kind=kOutput, calls=%fused_computation.107 | convolution fusion | flops 24455675904 | bytes 47106052 | tf_op jit(solution)/shard_map/mbtd,mbtkhe->dkhe/dot_general | solution.py:33
  (875 shorter events, 1081.5 us)
Async XLA Ops:
  0.7 1205.1 %copy-start = (bf16[1408,1000]{0,1:T(8,128)(2,1)S(1)}, bf16[1408,1000]{0,1:T(8,128)(2,1)}, u32[]{:S(2)}) copy-start(bf16[1408,1000]{0,1:T(8,128)(2,1)} %param.42) | copy-start | bytes 8448004
  27.6 989.0 %copy-start.96 = (f32[1408]{0:T(1024)}, f32[1408]{0:T(1024)S(1)}, u32[]{:S(2)}) copy-start(f32[1408]{0:T(1024)S(1)} %get-tuple-element.295) | copy-start | bytes 16900
  27.6 989.0 %copy-start.120 = (f32[1408]{0:T(1024)}, f32[1408]{0:T(1024)S(1)}, u32[]{:S(2)}) copy-start(f32[1408]{0:T(1024)S(1)} %get-tuple-element.294) | copy-start | bytes 16900
  85.8 1074.3 %copy-start.104 = (f32[1408]{0:T(1024)}, f32[1408]{0:T(1024)S(1)}, u32[]{:S(2)}) copy-start(f32[1408]{0:T(1024)S(1)} %get-tuple-element.297) | copy-start | bytes 16900
  160.8 33.4 %collective-permute-start = (bf16[2,257,1408]{2,0,1:T(2,128)(2,1)}, bf16[2,257,1408]{2,0,1:T(2,128)(2,1)}, u32[]{:S(2)}, u32[]{:S(2)}) collective-permute-start(bf16[2,257,1408]{2,0,1:T(2,128)(2,1)} %copy.622), channel_id=1, source_target_pairs={{0,1},{1,2},{2,3},{4,5},{5,6},{6,7}} | collective-permute-start | bytes 4342280 | tf_op jit(solution)/shard_map/ppermute | solution.py:110
  197.6 52.6 %copy-start.26 = (bf16[2,257,1408]{2,1,0:T(8,128)(2,1)}, bf16[2,257,1408]{2,1,0:T(8,128)(2,1)S(1)}, u32[]{:S(2)}) copy-start(bf16[2,257,1408]{2,1,0:T(8,128)(2,1)S(1)} %get-tuple-element.167) | copy-start | bytes 4342276
  329.7 29.0 %collective-permute-start.1 = (bf16[2,257,1408]{2,0,1:T(2,128)(2,1)}, bf16[2,257,1408]{2,0,1:T(2,128)(2,1)}, u32[]{:S(2)}, u32[]{:S(2)}) collective-permute-start(bf16[2,257,1408]{2,0,1:T(2,128)(2,1)} %copy.627), channel_id=1, source_target_pairs={{0,1},{1,2},{2,3},{4,5},{5,6},{6,7}} | collective-permute-start | bytes 4342280 | tf_op jit(solution)/shard_map/ppermute | solution.py:110
  362.0 52.6 %copy-start.28 = (bf16[2,257,1408]{2,1,0:T(8,128)(2,1)}, bf16[2,257,1408]{2,1,0:T(8,128)(2,1)S(1)}, u32[]{:S(2)}) copy-start(bf16[2,257,1408]{2,1,0:T(8,128)(2,1)S(1)} %get-tuple-element.165) | copy-start | bytes 4342276
  494.2 29.2 %collective-permute-start.2 = (bf16[2,257,1408]{2,0,1:T(2,128)(2,1)}, bf16[2,257,1408]{2,0,1:T(2,128)(2,1)}, u32[]{:S(2)}, u32[]{:S(2)}) collective-permute-start(bf16[2,257,1408]{2,0,1:T(2,128)(2,1)} %copy.632), channel_id=1, source_target_pairs={{0,1},{1,2},{2,3},{4,5},{5,6},{6,7}} | collective-permute-start | bytes 4342280 | tf_op jit(solution)/shard_map/ppermute | solution.py:110
  526.6 52.6 %copy-start.18 = (bf16[2,257,1408]{2,1,0:T(8,128)(2,1)}, bf16[2,257,1408]{2,1,0:T(8,128)(2,1)S(1)}, u32[]{:S(2)}) copy-start(bf16[2,257,1408]{2,1,0:T(8,128)(2,1)S(1)} %get-tuple-element.163) | copy-start | bytes 4342276
  659.9 26.6 %collective-permute-start.3 = (bf16[2,257,1408]{2,0,1:T(2,128)(2,1)}, bf16[2,257,1408]{2,0,1:T(2,128)(2,1)}, u32[]{:S(2)}, u32[]{:S(2)}) collective-permute-start(bf16[2,257,1408]{2,0,1:T(2,128)(2,1)} %copy.637), channel_id=1, source_target_pairs={{0,1},{1,2},{2,3},{4,5},{5,6},{6,7}} | collective-permute-start | bytes 4342280 | tf_op jit(solution)/shard_map/ppermute | solution.py:110
  689.8 52.6 %copy-start.22 = (bf16[2,257,1408]{2,1,0:T(8,128)(2,1)}, bf16[2,257,1408]{2,1,0:T(8,128)(2,1)S(1)}, u32[]{:S(2)}) copy-start(bf16[2,257,1408]{2,1,0:T(8,128)(2,1)S(1)} %get-tuple-element.161) | copy-start | bytes 4342276
  823.1 26.6 %collective-permute-start.4 = (bf16[2,257,1408]{2,0,1:T(2,128)(2,1)}, bf16[2,257,1408]{2,0,1:T(2,128)(2,1)}, u32[]{:S(2)}, u32[]{:S(2)}) collective-permute-start(bf16[2,257,1408]{2,0,1:T(2,128)(2,1)} %copy.642), channel_id=1, source_target_pairs={{0,1},{1,2},{2,3},{4,5},{5,6},{6,7}} | collective-permute-start | bytes 4342280 | tf_op jit(solution)/shard_map/ppermute | solution.py:110
  853.0 52.6 %copy-start.24 = (bf16[2,257,1408]{2,1,0:T(8,128)(2,1)}, bf16[2,257,1408]{2,1,0:T(8,128)(2,1)S(1)}, u32[]{:S(2)}) copy-start(bf16[2,257,1408]{2,1,0:T(8,128)(2,1)S(1)} %get-tuple-element.159) | copy-start | bytes 4342276
  986.3 26.1 %collective-permute-start.5 = (bf16[2,257,1408]{2,0,1:T(2,128)(2,1)}, bf16[2,257,1408]{2,0,1:T(2,128)(2,1)}, u32[]{:S(2)}, u32[]{:S(2)}) collective-permute-start(bf16[2,257,1408]{2,0,1:T(2,128)(2,1)} %copy.647), channel_id=1, source_target_pairs={{0,1},{1,2},{2,3},{4,5},{5,6},{6,7}} | collective-permute-start | bytes 4342280 | tf_op jit(solution)/shard_map/ppermute | solution.py:110
  1015.7 52.6 %copy-start.20 = (bf16[2,257,1408]{2,1,0:T(8,128)(2,1)}, bf16[2,257,1408]{2,1,0:T(8,128)(2,1)S(1)}, u32[]{:S(2)}) copy-start(bf16[2,257,1408]{2,1,0:T(8,128)(2,1)S(1)} %get-tuple-element.157) | copy-start | bytes 4342276
  1159.9 48.2 %copy-start.148 = (f32[8]{0:T(128)}, f32[8]{0:T(128)S(1)}, u32[]{:S(2)}) copy-start(f32[8]{0:T(128)S(1)} %div.369) | copy-start | bytes 100
  1230.2 43.2 %copy-start.105 = (f32[1408]{0:T(1024)S(1)}, f32[1408]{0:T(1024)}, u32[]{:S(2)}) copy-start(f32[1408]{0:T(1024)} %copy-done.104) | copy-start | bytes 16900
  1230.2 43.2 %copy-start.145 = (f32[2,257]{1,0:T(2,128)S(1)}, f32[2,257]{1,0:T(2,128)}, u32[]{:S(2)}) copy-start(f32[2,257]{1,0:T(2,128)} %copy-done.144) | copy-start | bytes 6172
  1230.2 43.3 %copy-start.156 = (f32[2,257]{1,0:T(2,128)S(1)}, f32[2,257]{1,0:T(2,128)}, u32[]{:S(2)}) copy-start(f32[2,257]{1,0:T(2,128)} %broadcast_multiply_fusion.5) | copy-start | bytes 6172
  1230.2 43.3 %copy-start.158 = (f32[2,257]{1,0:T(2,128)S(1)}, f32[2,257]{1,0:T(2,128)}, u32[]{:S(2)}) copy-start(f32[2,257]{1,0:T(2,128)} %broadcast_multiply_fusion.11) | copy-start | bytes 6172
  1230.2 43.3 %copy-start.160 = (f32[2,257]{1,0:T(2,128)S(1)}, f32[2,257]{1,0:T(2,128)}, u32[]{:S(2)}) copy-start(f32[2,257]{1,0:T(2,128)} %broadcast_multiply_fusion.17) | copy-start | bytes 6172
  1230.2 43.3 %copy-start.163 = (f32[2,257]{1,0:T(2,128)S(1)}, f32[2,257]{1,0:T(2,128)}, u32[]{:S(2)}) copy-start(f32[2,257]{1,0:T(2,128)} %broadcast_multiply_fusion.23) | copy-start | bytes 6172
  1230.2 43.3 %copy-start.166 = (f32[2,257]{1,0:T(2,128)S(1)}, f32[2,257]{1,0:T(2,128)}, u32[]{:S(2)}) copy-start(f32[2,257]{1,0:T(2,128)} %broadcast_multiply_fusion.29) | copy-start | bytes 6172
  1230.2 43.3 %copy-start.168 = (f32[2,257]{1,0:T(2,128)S(1)}, f32[2,257]{1,0:T(2,128)}, u32[]{:S(2)}) copy-start(f32[2,257]{1,0:T(2,128)} %broadcast_multiply_fusion.35) | copy-start | bytes 6172
  1230.2 43.3 %copy-start.196 = (f32[2,257]{1,0:T(2,128)S(1)}, f32[2,257]{1,0:T(2,128)}, u32[]{:S(2)}) copy-start(f32[2,257]{1,0:T(2,128)} %add_rsqrt_fusion.13) | copy-start | bytes 6172
  1381.0 8.9 collective-permute-start.6
  1389.9 44.1 %copy-start.106 = (f32[1408]{0:T(1024)S(1)}, f32[1408]{0:T(1024)}, u32[]{:S(2)}) copy-start(f32[1408]{0:T(1024)} %copy-done.104) | copy-start | bytes 16900
  1389.9 44.1 %copy-start.169 = (f32[2,257]{1,0:T(2,128)S(1)}, f32[2,257]{1,0:T(2,128)}, u32[]{:S(2)}) copy-start(f32[2,257]{1,0:T(2,128)} %broadcast_multiply_fusion.35) | copy-start | bytes 6172
  1389.9 44.1 %copy-start.172 = (f32[2,257]{1,0:T(2,128)S(1)}, f32[2,257]{1,0:T(2,128)}, u32[]{:S(2)}) copy-start(f32[2,257]{1,0:T(2,128)} %add_rsqrt_fusion.11) | copy-start | bytes 6172
  1528.9 17.9 collective-permute-start.7
  1546.8 44.1 %copy-start.107 = (f32[1408]{0:T(1024)S(1)}, f32[1408]{0:T(1024)}, u32[]{:S(2)}) copy-start(f32[1408]{0:T(1024)} %copy-done.104) | copy-start | bytes 16900
  1546.8 44.1 %copy-start.167 = (f32[2,257]{1,0:T(2,128)S(1)}, f32[2,257]{1,0:T(2,128)}, u32[]{:S(2)}) copy-start(f32[2,257]{1,0:T(2,128)} %broadcast_multiply_fusion.29) | copy-start | bytes 6172
  1546.8 44.1 %copy-start.173 = (f32[2,257]{1,0:T(2,128)S(1)}, f32[2,257]{1,0:T(2,128)}, u32[]{:S(2)}) copy-start(f32[2,257]{1,0:T(2,128)} %add_rsqrt_fusion.9) | copy-start | bytes 6172
  1667.4 37.6 %copy-start.113 = (f32[8,1408]{1,0:T(8,128)S(1)}, f32[8,1408]{1,0:T(8,128)}, u32[]{:S(2)}) copy-start(f32[8,1408]{1,0:T(8,128)} %copy-done.112) | copy-start | bytes 135172
  1667.4 37.6 %copy-start.118 = (f32[8,1000]{1,0:T(8,128)S(1)}, f32[8,1000]{1,0:T(8,128)}, u32[]{:S(2)}) copy-start(f32[8,1000]{1,0:T(8,128)} %copy-done.117) | copy-start | bytes 96004
  1667.4 37.6 %copy-start.125 = (f32[1408]{0:T(1024)S(1)}, f32[1408]{0:T(1024)}, u32[]{:S(2)}) copy-start(f32[1408]{0:T(1024)} %convert_element_type.1000) | copy-start | bytes 16900
  1685.8 22.9 collective-permute-start.8
  1708.7 44.1 %copy-start.108 = (f32[1408]{0:T(1024)S(1)}, f32[1408]{0:T(1024)}, u32[]{:S(2)}) copy-start(f32[1408]{0:T(1024)} %copy-done.104) | copy-start | bytes 16900
  1708.7 44.1 %copy-start.164 = (f32[2,257]{1,0:T(2,128)S(1)}, f32[2,257]{1,0:T(2,128)}, u32[]{:S(2)}) copy-start(f32[2,257]{1,0:T(2,128)} %broadcast_multiply_fusion.23) | copy-start | bytes 6172
  1708.7 44.1 %copy-start.171 = (f32[2,257]{1,0:T(2,128)S(1)}, f32[2,257]{1,0:T(2,128)}, u32[]{:S(2)}) copy-start(f32[2,257]{1,0:T(2,128)} %add_rsqrt_fusion.7) | copy-start | bytes 6172
  1846.6 65.2 %copy-start.9 = (bf16[2,257,1408]{2,1,0:T(8,128)(2,1)}, bf16[2,257,1408]{2,1,0:T(8,128)(2,1)S(1)}, u32[]{:S(2)}) copy-start(bf16[2,257,1408]{2,1,0:T(8,128)(2,1)S(1)} %fusion.889) | copy-start | bytes 4342276
  1847.8 20.0 collective-permute-start.9
  1867.8 44.1 %copy-start.109 = (f32[1408]{0:T(1024)S(1)}, f32[1408]{0:T(1024)}, u32[]{:S(2)}) copy-start(f32[1408]{0:T(1024)} %copy-done.104) | copy-start | bytes 16900
  1867.8 44.1 %copy-start.161 = (f32[2,257]{1,0:T(2,128)S(1)}, f32[2,257]{1,0:T(2,128)}, u32[]{:S(2)}) copy-start(f32[2,257]{1,0:T(2,128)} %broadcast_multiply_fusion.17) | copy-start | bytes 6172
  1867.8 44.1 %copy-start.170 = (f32[2,257]{1,0:T(2,128)S(1)}, f32[2,257]{1,0:T(2,128)}, u32[]{:S(2)}) copy-start(f32[2,257]{1,0:T(2,128)} %add_rsqrt_fusion.5) | copy-start | bytes 6172
  2007.9 47.6 %collective-permute-start.10 = (bf16[2,257,1408]{2,0,1:T(2,128)(2,1)}, bf16[2,257,1408]{2,0,1:T(2,128)(2,1)}, u32[]{:S(2)}, u32[]{:S(2)}) collective-permute-start(bf16[2,257,1408]{2,0,1:T(2,128)(2,1)} %copy.706), channel_id=1, source_target_pairs={{1,0},{2,1},{3,2},{5,4},{6,5},{7,6}} | collective-permute-start | bytes 4342280 | tf_op jit(solution)/shard_map/ppermute | solution.py:143
  2055.5 44.3 %copy-start.110 = (f32[1408]{0:T(1024)S(1)}, f32[1408]{0:T(1024)}, u32[]{:S(2)}) copy-start(f32[1408]{0:T(1024)} %copy-done.104) | copy-start | bytes 16900
  2055.5 44.3 %copy-start.159 = (f32[2,257]{1,0:T(2,128)S(1)}, f32[2,257]{1,0:T(2,128)}, u32[]{:S(2)}) copy-start(f32[2,257]{1,0:T(2,128)} %broadcast_multiply_fusion.11) | copy-start | bytes 6172
  2055.5 44.3 %copy-start.165 = (f32[2,257]{1,0:T(2,128)S(1)}, f32[2,257]{1,0:T(2,128)}, u32[]{:S(2)}) copy-start(f32[2,257]{1,0:T(2,128)} %add_rsqrt_fusion.3) | copy-start | bytes 6172
  2196.2 38.4 %collective-permute-start.11 = (bf16[2,257,1408]{2,0,1:T(2,128)(2,1)}, bf16[2,257,1408]{2,0,1:T(2,128)(2,1)}, u32[]{:S(2)}, u32[]{:S(2)}) collective-permute-start(bf16[2,257,1408]{2,0,1:T(2,128)(2,1)} %copy.717), channel_id=1, source_target_pairs={{1,0},{2,1},{3,2},{5,4},{6,5},{7,6}} | collective-permute-start | bytes 4342280 | tf_op jit(solution)/shard_map/ppermute | solution.py:143
  2386.3 203.3 %collective-permute-start.14 = (bf16[4,2,257,1408]{3,0,2,1:T(4,128)(2,1)}, bf16[4,2,257,1408]{3,0,2,1:T(4,128)(2,1)}, u32[]{:S(2)}, u32[]{:S(2)}) collective-permute-start(bf16[4,2,257,1408]{3,0,2,1:T(4,128)(2,1)} %copy.728), channel_id=1, source_target_pairs={{0,1},{4,5}} | collective-permute-start | bytes 17369096 | tf_op jit(solution)/shard_map/ppermute | solution.py:153
  2389.9 199.6 %collective-permute-start.13 = (bf16[4,2,257,1408]{3,0,2,1:T(4,128)(2,1)}, bf16[4,2,257,1408]{3,0,2,1:T(4,128)(2,1)}, u32[]{:S(2)}, u32[]{:S(2)}) collective-permute-start(bf16[4,2,257,1408]{3,0,2,1:T(4,128)(2,1)} %copy.728), channel_id=1, source_target_pairs={{0,2},{4,6}} | collective-permute-start | bytes 17369096 | tf_op jit(solution)/shard_map/ppermute | solution.py:153
  2393.2 196.4 %collective-permute-start.12 = (bf16[4,2,257,1408]{3,0,2,1:T(4,128)(2,1)}, bf16[4,2,257,1408]{3,0,2,1:T(4,128)(2,1)}, u32[]{:S(2)}, u32[]{:S(2)}) collective-permute-start(bf16[4,2,257,1408]{3,0,2,1:T(4,128)(2,1)} %copy.728), channel_id=1, source_target_pairs={{0,3},{4,7}} | collective-permute-start | bytes 17369096 | tf_op jit(solution)/shard_map/ppermute | solution.py:153
  2437.0 63.5 %slice-start.3 = ((s8[5947392]{0:T(1024)(128)(4,1)}), s8[4194304]{0:T(1024)(128)(4,1)S(1)}, s32[]{:S(2)}) async-start(s8[5947392]{0:T(1024)(128)(4,1)} %bitcast.2363), calls=%async_computation.3 | async-start | bytes 8388608
  2452.0 48.4 %slice-start.4 = ((s8[5947392]{0:T(1024)(128)(4,1)}), s8[1753088]{0:T(1024)(128)(4,1)S(1)}, s32[]{:S(2)}) async-start(s8[5947392]{0:T(1024)(128)(4,1)} %bitcast.2363), calls=%async_computation.4 | async-start | bytes 3506176
  2500.5 51.0 %copy-start.129 = (f32[6144]{0:T(1024)S(1)}, f32[6144]{0:T(1024)}, u32[]{:S(2)}) copy-start(f32[6144]{0:T(1024)} %reduce_sum.1476) | copy-start | bytes 73732
  2500.5 51.0 %copy-start.130 = (f32[6144]{0:T(1024)S(1)}, f32[6144]{0:T(1024)}, u32[]{:S(2)}) copy-start(f32[6144]{0:T(1024)} %reduce_sum.1477) | copy-start | bytes 73732
  2500.5 51.0 %copy-start.131 = (f32[6144]{0:T(1024)S(1)}, f32[6144]{0:T(1024)}, u32[]{:S(2)}) copy-start(f32[6144]{0:T(1024)} %reduce_sum.1478) | copy-start | bytes 73732
  2500.5 51.0 %copy-start.132 = (f32[6144]{0:T(1024)S(1)}, f32[6144]{0:T(1024)}, u32[]{:S(2)}) copy-start(f32[6144]{0:T(1024)} %reduce_sum.1479) | copy-start | bytes 73732
  2500.5 51.0 %copy-start.133 = (f32[6144]{0:T(1024)S(1)}, f32[6144]{0:T(1024)}, u32[]{:S(2)}) copy-start(f32[6144]{0:T(1024)} %reduce_sum.1480) | copy-start | bytes 73732
  2500.5 51.0 %copy-start.134 = (f32[6144]{0:T(1024)S(1)}, f32[6144]{0:T(1024)}, u32[]{:S(2)}) copy-start(f32[6144]{0:T(1024)} %reduce_sum.1481) | copy-start | bytes 73732
  2500.5 51.0 %copy-start.135 = (f32[6144]{0:T(1024)S(1)}, f32[6144]{0:T(1024)}, u32[]{:S(2)}) copy-start(f32[6144]{0:T(1024)} %reduce_sum.1482) | copy-start | bytes 73732
  2500.5 51.7 %copy-start.126 = (bf16[7,2,257,1408]{3,2,1,0:T(8,128)(2,1)S(1)}, bf16[7,2,257,1408]{3,2,1,0:T(8,128)(2,1)}, u32[]{:S(2)}) copy-start(bf16[7,2,257,1408]{3,2,1,0:T(8,128)(2,1)} %bitcast_dynamic-update-slice_fusion.69) | copy-start | bytes 30395908
  (217 other events, 3474.8 us)

commit v2 on v1

v2 whole, which is shorter than its diff:
```python
import functools
import math
import jax
import jax.numpy as jnp
from jax import lax
from jax.experimental import pallas as pl
from jax.experimental.pallas import tpu as pltpu
from jax.sharding import PartitionSpec as P

EPS = 1e-6
SMOOTH = 0.1
F32 = jnp.float32
BF16 = jnp.bfloat16
MESH = pl.DeviceIdType.MESH
CHUNK = 512
GROUP = 2
BLOCK = 64


def layer_norm(hidden, gain, bias):
    values = hidden.astype(F32)
    centered = values - jnp.mean(values, axis=-1, keepdims=True)
    variance = jnp.mean(jnp.square(centered), axis=-1, keepdims=True)
    return (centered * lax.rsqrt(variance + EPS) * gain + bias).astype(BF16)


def dot(left, right, left_axis=1, right_axis=0):
    return lax.dot_general(left, right, (((left_axis,), (right_axis,)), ((), ())), preferred_element_type=F32)


def by_rows(rows, visit):
    def step(index, carry):
        visit(pl.ds(pl.multiple_of(index * BLOCK, BLOCK), BLOCK))
        return carry

    lax.fori_loop(0, rows // BLOCK, step, 0)
    if rows % BLOCK:
        visit(pl.ds(rows - rows % BLOCK, rows % BLOCK))


def fold(values):
    rows, columns = values.shape
    return jnp.sum(values.reshape(rows // 8, 8, columns), axis=0)


def everyone(stage, stages):
    barrier = pltpu.get_barrier_semaphore()
    for hop in range(1, stages):
        pl.semaphore_signal(barrier, inc=1, device_id={"pp": lax.rem(stage + hop, stages)}, device_id_type=MESH)
    pl.semaphore_wait(barrier, stages - 1)


def forward_kernel(dims, *refs):
    (emb, wqkv, wproj, wfc1, wfc2, g1, b1, bqkv, bproj, g2, b2, bfc1, bfc2,
     x_s, a_s, qkv_s, c_s, h_s, n_s, d_s, g_s, p_s, tops_out,
     vqkv, vproj, vfc1, vfc2, xin, act, qkv, ctx, mid, yacc, ubuf, gbuf, pbuf, yout, tops,
     wsem, qsem, recv_sem, send_sem, top_sem, save_sem, usem, gsem, psem, free_sem) = refs
    stages, images, tokens, heads, head = dims
    rows, width = mid.shape
    chunks = vfc1.shape[1] // CHUNK
    stage = lax.axis_index("pp")
    is_first = stage == 0
    is_last = stage == stages - 1
    scale2 = head ** -0.5 / math.log(2.0)

    def qkv_copy(index, slot):
        part = lax.rem(index, 3)
        return pltpu.make_async_copy(wqkv.at[pl.ds(part * width, width)], vqkv.at[slot], qsem.at[slot])

    def emb_copy(image, slot):
        return pltpu.make_async_copy(emb.at[image], xin.at[slot], recv_sem.at[slot])

    qkv_copy(0, 0).start()

    @pl.when(is_first)
    def _():
        emb_copy(0, 0).start()
        emb_copy(1, 1).start()

    qkv_copy(1, 1).start()
    proj_copy = pltpu.make_async_copy(wproj, vproj, wsem.at[0])
    fc1_copy = pltpu.make_async_copy(wfc1, vfc1, wsem.at[1])
    fc2_copy = pltpu.make_async_copy(wfc2, vfc2, wsem.at[2])
    proj_copy.start()
    fc1_copy.start()
    fc2_copy.start()
    everyone(stage, stages)

    def saves(image, slot):
        pairs = ((xin.at[slot], x_s), (act, a_s), (qkv, qkv_s), (ctx, c_s), (mid, h_s), (act, n_s))
        return [pltpu.make_async_copy(src, dst.at[image], save_sem.at[at]) for at, (src, dst) in enumerate(pairs)]

    def u_save(image, chunk):
        slot = lax.rem(chunk, 3)
        return pltpu.make_async_copy(ubuf.at[slot], d_s.at[image, :, pl.ds(pl.multiple_of(chunk * CHUNK, CHUNK), CHUNK)], usem.at[slot])

    def g_save(image, chunk):
        slot = lax.rem(chunk, 2)
        return pltpu.make_async_copy(gbuf.at[slot], g_s.at[image, :, pl.ds(pl.multiple_of(chunk * CHUNK, CHUNK), CHUNK)], gsem.at[slot])

    def p_save(image, group):
        slot = group % 2
        return pltpu.make_async_copy(pbuf.at[slot], p_s.at[image, pl.ds(group * GROUP, GROUP)], psem.at[slot])

    def top_copy(image, other):
        return pltpu.make_async_remote_copy(
            src_ref=yout.at[pl.ds(0, 16)], dst_ref=tops.at[image], send_sem=send_sem.at[1 + other], recv_sem=top_sem,
            device_id={"pp": other}, device_id_type=MESH)

    def next_copy(image, slot):
        return pltpu.make_async_remote_copy(
            src_ref=yout, dst_ref=xin.at[slot], send_sem=send_sem.at[0], recv_sem=recv_sem.at[slot],
            device_id={"pp": lax.rem(stage + 1, stages)}, device_id_type=MESH)

    def wait_sent(image):
        @pl.when(jnp.logical_not(is_last))
        def _():
            next_copy(image, 0).wait_send()

        @pl.when(is_last)
        def _():
            for other in range(stages - 1):
                top_copy(image, other).wait_send()

    def one_image(image, carry):
        slot = lax.rem(image, 2)
        save_x, save_a, save_qkv, save_c, save_h, save_n = saves(image, slot)
        emb_copy(image, slot).wait()
        save_x.start()

        @pl.when(image > 0)
        def _():
            save_n.wait()
            save_qkv.wait()

        def norm1(lines):
            act[lines, :] = layer_norm(xin[slot, lines, :], g1[...], b1[...])

        by_rows(rows, norm1)
        save_a.start()

        def qkv_part(part, carry):
            index = image * 3 + part
            where = lax.rem(index, 2)
            qkv_copy(index, where).wait()
            columns = pl.ds(pl.multiple_of(part * width, 128), width)
            qkv[:, columns] = (dot(act[...], vqkv[where], 1, 1) + bqkv[:, columns]).astype(BF16)

            @pl.when(index + 2 < images * 3)
            def _():
                qkv_copy(index + 2, where).start()

            return carry

        lax.fori_loop(0, 3, qkv_part, 0)
        save_qkv.start()

        @pl.when(image > 0)
        def _():
            save_c.wait()
            save_h.wait()
            p_save(image, 0).wait()
            p_save(image, 1).wait()

        for group in range(heads // GROUP):
            if group >= 2:
                p_save(image, group).wait()
            for inner in range(GROUP):
                at = (group * GROUP + inner) * head
                q = qkv[:, at:at + head]
                k = qkv[:, width + at:width + at + head]
                v = qkv[:, 2 * width + at:2 * width + at + head]
                scores = dot(k, q, 1, 1)
                top, tail = scores[:tokens - 1], scores[tokens - 1:]
                most = jnp.maximum(jnp.max(top, axis=0, keepdims=True), tail[:1])
                top = jnp.exp2((top - most) * scale2)
                real = lax.broadcasted_iota(jnp.int32, tail.shape, 0) < 1
                tail = jnp.where(real, jnp.exp2(jnp.minimum(tail - most, 0.0) * scale2), 0.0)
                inv = 1.0 / (jnp.sum(top, axis=0, keepdims=True) + jnp.sum(tail, axis=0, keepdims=True))
                probs = jnp.concatenate([top, tail], axis=0) * inv
                pbuf[group % 2, inner] = probs
                ctx[:, at:at + head] = dot(probs.astype(BF16), v, 0, 0).astype(BF16)
            p_save(image, group).start()
        save_c.start()

        @pl.when(image == 0)
        def _():
            proj_copy.wait()

        mid[...] = (dot(ctx[...], vproj[...]) + bproj[...] + xin[slot].astype(F32)).astype(BF16)
        save_h.start()
        save_x.wait()

        @pl.when(jnp.logical_and(is_first, image + 2 < images))
        def _():
            emb_copy(image + 2, slot).start()

        @pl.when(jnp.logical_and(stage > 0, image + 2 < images))
        def _():
            pl.semaphore_signal(free_sem, inc=1, device_id={"pp": lax.rem(stage + stages - 1, stages)}, device_id_type=MESH)

        save_a.wait()

        def norm2(lines):
            hidden = mid[lines, :]
            act[lines, :] = layer_norm(hidden, g2[...], b2[...])
            yacc[lines, :] = hidden.astype(F32) + bfc2[...]

        by_rows(rows, norm2)
        save_n.start()

        @pl.when(image == 0)
        def _():
            fc1_copy.wait()
            fc2_copy.wait()

        @pl.when(image > 0)
        def _():
            for chunk in range(3):
                u_save(image, chunk).wait()
            for chunk in range(2):
                g_save(image, chunk).wait()

        def fc1(chunk):
            columns = pl.ds(pl.multiple_of(chunk * CHUNK, CHUNK), CHUNK)
            ubuf[lax.rem(chunk, 3)] = dot(act[...], vfc1[:, columns]) + bfc1[:, columns]

        def fc2(chunk):
            slot3, slot2 = lax.rem(chunk, 3), lax.rem(chunk, 2)
            pre = ubuf[slot3]
            cdf = 0.5 + 0.5 * lax.erf(pre * (0.5 ** 0.5))
            pdf = jnp.exp2(pre * pre * (-0.5 / math.log(2.0))) * ((2.0 * math.pi) ** -0.5)
            activ = (pre * cdf).astype(BF16)
            gbuf[slot2] = activ
            ubuf[slot3] = cdf + pre * pdf
            yacc[...] += dot(activ, vfc2[pl.ds(pl.multiple_of(chunk * CHUNK, CHUNK), CHUNK), :])

        fc1(0)

        def mlp_step(chunk, carry):
            @pl.when(chunk >= 3)
            def _():
                u_save(image, chunk).wait()
                g_save(image, chunk - 1).wait()

            fc1(chunk)
            fc2(chunk - 1)
            u_save(image, chunk - 1).start()
            g_save(image, chunk - 1).start()
            return carry

        lax.fori_loop(1, chunks, mlp_step, 0)
        g_save(image, chunks - 1).wait()
        fc2(chunks - 1)
        u_save(image, chunks - 1).start()
        g_save(image, chunks - 1).start()

        @pl.when(image > 0)
        def _():
            wait_sent(image)

        yout[...] = yacc[...].astype(BF16)

        @pl.when(jnp.logical_and(jnp.logical_not(is_last), image >= 2))
        def _():
            pl.semaphore_wait(free_sem, 1)

        @pl.when(jnp.logical_not(is_last))
        def _():
            next_copy(image, slot).start()

        @pl.when(is_last)
        def _():
            for other in range(stages - 1):
                top_copy(image, other).start()
            tops[image] = yout[pl.ds(0, 16), :]

        return carry

    lax.fori_loop(0, images, one_image, 0)
    wait_sent(images - 1)
    _, _, save_qkv, save_c, save_h, save_n = saves(images - 1, 0)
    for copy in (save_qkv, save_c, save_h, save_n):
        copy.wait()
    for chunk in range(3):
        u_save(images - 1, chunk).wait()
    for chunk in range(2):
        g_save(images - 1, chunk).wait()
        p_save(images - 1, chunk).wait()

    @pl.when(jnp.logical_not(is_last))
    def _():
        pltpu.make_async_copy(tops_out, tops, top_sem).wait()

    out = pltpu.make_async_copy(tops, tops_out, wsem.at[0])
    out.start()
    out.wait()


def norm_backward(grad, hidden, gain):
    values = hidden.astype(F32)
    centered = values - jnp.mean(values, axis=-1, keepdims=True)
    inv = lax.rsqrt(jnp.mean(jnp.square(centered), axis=-1, keepdims=True) + EPS)
    unit = centered * inv
    scaled = grad * gain
    grad_in = inv * (scaled - jnp.mean(scaled, axis=-1, keepdims=True) - unit * jnp.mean(scaled * unit, axis=-1, keepdims=True))
    return grad_in, grad * unit


def backward_kernel(dims, *refs):
    (gtop, wqkv, wproj, wfc1, wfc2, g1, g2, x_s, qkv_s, h_s, d_s, p_s,
     gy_s, gpre_s, gmid_s, gqkv_s, gemb, sum1g, sum1b, sum2g, sum2b, sumproj, sumfc2, sumqkv, sumfc1,
     vqkv, vproj, vfc1, vfc2, gin, acc, dbuf, abuf, gbuf, hid, gmid, gctx, qkv, gqkv, pbuf, gout,
     wsem, qsem, recv_sem, send_sem, emb_sem, save_sem, load_sem, dsem, gsem, psem, free_sem) = refs
    stages, images, tokens, heads, head = dims
    rows, width = gmid.shape
    chunks = vfc1.shape[1] // CHUNK
    groups = heads // GROUP
    stage = lax.axis_index("pp")
    is_first = stage == 0
    is_last = stage == stages - 1
    scale = head ** -0.5

    def qkv_copy(index, slot):
        part = lax.rem(index, 3)
        return pltpu.make_async_copy(wqkv.at[pl.ds(part * width, width)], vqkv.at[slot], qsem.at[slot])

    def top_copy(image, slot):
        return pltpu.make_async_copy(gtop.at[image], gin.at[slot], recv_sem.at[slot])

    def d_load(image, chunk):
        slot = lax.rem(chunk, 3)
        return pltpu.make_async_copy(d_s.at[image, :, pl.ds(pl.multiple_of(chunk * CHUNK, CHUNK), CHUNK)], dbuf.at[slot], dsem.at[slot])

    def g_save(image, chunk):
        slot = lax.rem(chunk, 2)
        return pltpu.make_async_copy(gbuf.at[slot], gpre_s.at[image, :, pl.ds(pl.multiple_of(chunk * CHUNK, CHUNK), CHUNK)], gsem.at[slot])

    def p_load(image, group):
        slot = group % 2
        return pltpu.make_async_copy(p_s.at[image, pl.ds(group * GROUP, GROUP)], pbuf.at[slot], psem.at[slot])

    def saves(image, slot):
        pairs = ((gin.at[slot], gy_s), (gmid, gmid_s), (gqkv, gqkv_s))
        return [pltpu.make_async_copy(src, dst.at[image], save_sem.at[at]) for at, (src, dst) in enumerate(pairs)]

    def loads(image):
        pairs = ((h_s, hid), (x_s, hid), (qkv_s, qkv))
        return [pltpu.make_async_copy(src.at[image], dst, load_sem.at[at]) for at, (src, dst) in enumerate(pairs)]

    def next_copy(slot):
        return pltpu.make_async_remote_copy(
            src_ref=gout, dst_ref=gin.at[slot], send_sem=send_sem.at[0], recv_sem=recv_sem.at[slot],
            device_id={"pp": lax.rem(stage + stages - 1, stages)}, device_id_type=MESH)

    def emb_send(image, other):
        return pltpu.make_async_remote_copy(
            src_ref=gout, dst_ref=gemb.at[image], send_sem=send_sem.at[other], recv_sem=emb_sem,
            device_id={"pp": other}, device_id_type=MESH)

    def emb_local(image):
        return pltpu.make_async_copy(gout, gemb.at[image], save_sem.at[3])

    def wait_sent(image):
        @pl.when(jnp.logical_not(is_first))
        def _():
            next_copy(0).wait_send()

        @pl.when(is_first)
        def _():
            for other in range(1, stages):
                emb_send(image, other).wait_send()
            emb_local(image).wait()

    @pl.when(is_last)
    def _():
        top_copy(0, 0).start()
        top_copy(1, 1).start()

    fc2_copy = pltpu.make_async_copy(wfc2, vfc2, wsem.at[2])
    fc1_copy = pltpu.make_async_copy(wfc1, vfc1, wsem.at[1])
    proj_copy = pltpu.make_async_copy(wproj, vproj, wsem.at[0])
    fc2_copy.start()
    for chunk in range(3):
        d_load(0, chunk).start()
    fc1_copy.start()
    loads(0)[0].start()
    loads(0)[2].start()
    proj_copy.start()
    for group in range(2):
        p_load(0, group).start()
    qkv_copy(0, 0).start()
    qkv_copy(1, 1).start()
    for total in (sum1g, sum1b, sum2g, sum2b, sumproj, sumfc2, sumqkv, sumfc1):
        total[...] = jnp.zeros_like(total)
    everyone(stage, stages)

    def one_image(image, carry):
        slot = lax.rem(image, 2)
        more = image + 1 < images
        save_gy, save_mid, save_qkv = saves(image, slot)
        load_h, load_x, load_qkv = loads(image)
        top_copy(image, slot).wait()
        save_gy.start()

        @pl.when(image == 0)
        def _():
            fc2_copy.wait()
            fc1_copy.wait()

        @pl.when(image > 0)
        def _():
            for chunk in range(2):
                g_save(image, chunk).wait()

        acc[...] = jnp.zeros_like(acc)

        def fc2(chunk):
            lines = pl.ds(pl.multiple_of(chunk * CHUNK, CHUNK), CHUNK)
            abuf[lax.rem(chunk, 2)] = dot(gin[slot], vfc2[lines, :], 1, 1).astype(BF16)

        def fc1(chunk):
            columns = pl.ds(pl.multiple_of(chunk * CHUNK, CHUNK), CHUNK)
            slot2 = lax.rem(chunk, 2)
            pre = abuf[slot2].astype(F32) * dbuf[lax.rem(chunk, 3)]
            sumfc1[:, columns] += fold(pre)
            low = pre.astype(BF16)
            gbuf[slot2] = low
            acc[...] += dot(low, vfc1[:, columns], 1, 1)

        fc2(0)

        def mlp_step(chunk, carry):
            d_load(image, chunk - 1).wait()

            @pl.when(chunk >= 3)
            def _():
                g_save(image, chunk - 1).wait()

            fc2(chunk)
            fc1(chunk - 1)
            g_save(image, chunk - 1).start()

            @pl.when(chunk + 2 < chunks)
            def _():
                d_load(image, chunk + 2).start()

            return carry

        lax.fori_loop(1, chunks, mlp_step, 0)
        d_load(image, chunks - 1).wait()
        g_save(image, chunks - 1).wait()
        fc1(chunks - 1)
        g_save(image, chunks - 1).start()

        @pl.when(more)
        def _():
            for chunk in range(3):
                d_load(image + 1, chunk).start()

        load_h.wait()

        @pl.when(image > 0)
        def _():
            save_mid.wait()
            save_qkv.wait()

        def back2(lines):
            grad = acc[lines, :].astype(BF16).astype(F32)
            grad_in, by_unit = norm_backward(grad, hid[lines, :], g2[...])
            sum2g[...] += fold(by_unit)
            sum2b[...] += fold(grad)
            top = gin[slot, lines, :].astype(F32)
            sumfc2[...] += fold(top)
            low = (top + grad_in).astype(BF16)
            gmid[lines, :] = low
            sumproj[...] += fold(low.astype(F32))

        by_rows(rows, back2)
        save_mid.start()
        load_x.start()
        save_gy.wait()

        @pl.when(jnp.logical_and(is_last, image + 2 < images))
        def _():
            top_copy(image + 2, slot).start()

        @pl.when(jnp.logical_and(stage < stages - 1, image + 2 < images))
        def _():
            pl.semaphore_signal(free_sem, inc=1, device_id={"pp": lax.rem(stage + 1, stages)}, device_id_type=MESH)

        @pl.when(image == 0)
        def _():
            proj_copy.wait()

        gctx[...] = dot(gmid[...], vproj[...], 1, 1).astype(BF16)
        load_qkv.wait()
        for group in range(groups):
            p_load(image, group).wait()
            for inner in range(GROUP):
                at = (group * GROUP + inner) * head
                q = qkv[:, at:at + head]
                k = qkv[:, width + at:width + at + head]
                v = qkv[:, 2 * width + at:2 * width + at + head]
                grad = gctx[:, at:at + head]
                probs = pbuf[group % 2, inner]
                grad_probs = dot(v, grad, 1, 1)
                mean = jnp.sum(grad_probs * probs, axis=0, keepdims=True)
                low = (probs * (grad_probs - mean) * scale).astype(BF16)
                gqkv[:, at:at + head] = dot(low, k, 0, 0).astype(BF16)
                gqkv[:, width + at:width + at + head] = dot(low, q).astype(BF16)
                gqkv[:, 2 * width + at:2 * width + at + head] = dot(probs.astype(BF16), grad).astype(BF16)
            if group + 2 < groups:
                p_load(image, group + 2).start()
            else:
                @pl.when(more)
                def _():
                    p_load(image + 1, group + 2 - groups).start()
        save_qkv.start()

        @pl.when(more)
        def _():
            loads(image + 1)[2].start()

        def qkv_part(part, carry):
            index = image * 3 + part
            where = lax.rem(index, 2)
            qkv_copy(index, where).wait()
            columns = pl.ds(pl.multiple_of(part * width, 128), width)
            piece = gqkv[:, columns]
            sumqkv[:, columns] += fold(piece.astype(F32))
            acc[...] += dot(piece, vqkv[where])

            @pl.when(index + 2 < images * 3)
            def _():
                qkv_copy(index + 2, where).start()

            return carry

        acc[...] = jnp.zeros_like(acc)
        lax.fori_loop(0, 3, qkv_part, 0)
        load_x.wait()

        @pl.when(image > 0)
        def _():
            wait_sent(image)

        def back1(lines):
            grad = acc[lines, :].astype(BF16).astype(F32)
            grad_in, by_unit = norm_backward(grad, hid[lines, :], g1[...])
            sum1g[...] += fold(by_unit)
            sum1b[...] += fold(grad)
            gout[lines, :] = (gmid[lines, :].astype(F32) + grad_in).astype(BF16)

        by_rows(rows, back1)

        @pl.when(more)
        def _():
            loads(image + 1)[0].start()

        @pl.when(jnp.logical_and(jnp.logical_not(is_first), image >= 2))
        def _():
            pl.semaphore_wait(free_sem, 1)

        @pl.when(jnp.logical_not(is_first))
        def _():
            next_copy(slot).start()

        @pl.when(is_first)
        def _():
            for other in range(1, stages):
                emb_send(image, other).start()
            emb_local(image).start()

        return carry

    lax.fori_loop(0, images, one_image, 0)
    wait_sent(images - 1)
    _, save_mid, save_qkv = saves(images - 1, 0)
    save_mid.wait()
    save_qkv.wait()
    for chunk in range(2):
        g_save(images - 1, chunk).wait()

    @pl.when(jnp.logical_not(is_first))
    def _():
        pltpu.make_async_copy(gemb, gemb, emb_sem).wait()


ANY = pl.BlockSpec(memory_space=pl.ANY)
VMEM = pl.BlockSpec(memory_space=pltpu.VMEM)
LIMIT = 67_043_328
DMA = pltpu.SemaphoreType.DMA


def run_forward(dims, emb, wqkv, wproj, wfc1, wfc2, vectors):
    stages, images, tokens, heads, head = dims
    rows, width = emb.shape[1:]
    hidden = wfc1.shape[1]
    hbm = lambda *shape, dtype=BF16: jax.ShapeDtypeStruct((images, rows) + shape, dtype)
    return pl.pallas_call(
        functools.partial(forward_kernel, dims),
        out_shape=(
            hbm(width), hbm(width), hbm(3 * width), hbm(width), hbm(width), hbm(width), hbm(hidden, dtype=F32), hbm(hidden),
            jax.ShapeDtypeStruct((images, heads, rows, rows), F32), jax.ShapeDtypeStruct((images, 16, width), BF16)),
        in_specs=[ANY] * 5 + [VMEM] * 8,
        out_specs=(ANY,) * 10,
        scratch_shapes=[
            pltpu.VMEM((2, width, width), BF16), pltpu.VMEM(wproj.shape, BF16), pltpu.VMEM(wfc1.shape, BF16), pltpu.VMEM(wfc2.shape, BF16),
            pltpu.VMEM((2, rows, width), BF16), pltpu.VMEM((rows, width), BF16), pltpu.VMEM((rows, 3 * width), BF16),
            pltpu.VMEM((rows, width), BF16), pltpu.VMEM((rows, width), BF16), pltpu.VMEM((rows, width), F32),
            pltpu.VMEM((3, rows, CHUNK), F32), pltpu.VMEM((2, rows, CHUNK), BF16), pltpu.VMEM((2, GROUP, rows, rows), F32),
            pltpu.VMEM((rows, width), BF16), pltpu.VMEM((images, 16, width), BF16),
            DMA((3,)), DMA((2,)), DMA((2,)), DMA((stages,)), DMA(()), DMA((6,)), DMA((3,)), DMA((2,)), DMA((2,)),
            pltpu.SemaphoreType.REGULAR],
        compiler_params=pltpu.CompilerParams(collective_id=0, has_side_effects=True, vmem_limit_bytes=LIMIT),
        name="forward",
    )(emb, wqkv, wproj, wfc1, wfc2, *vectors)


def run_backward(dims, gtop, wqkv, wproj, wfc1, wfc2, g1, g2, x_s, qkv_s, h_s, d_s, p_s):
    stages, images, tokens, heads, head = dims
    rows, width = gtop.shape[1:]
    hidden = wfc1.shape[1]
    hbm = lambda *shape: jax.ShapeDtypeStruct((images, rows) + shape, BF16)
    total = lambda size: jax.ShapeDtypeStruct((8, size), F32)
    return pl.pallas_call(
        functools.partial(backward_kernel, dims),
        out_shape=(hbm(width), hbm(hidden), hbm(width), hbm(3 * width), hbm(width)) + (total(width),) * 6 + (total(3 * width), total(hidden)),
        in_specs=[ANY] * 5 + [VMEM] * 2 + [ANY] * 5,
        out_specs=(ANY,) * 5 + (VMEM,) * 8,
        scratch_shapes=[
            pltpu.VMEM((2, width, width), BF16), pltpu.VMEM(wproj.shape, BF16), pltpu.VMEM(wfc1.shape, BF16), pltpu.VMEM(wfc2.shape, BF16),
            pltpu.VMEM((2, rows, width), BF16), pltpu.VMEM((rows, width), F32), pltpu.VMEM((3, rows, CHUNK), F32),
            pltpu.VMEM((2, rows, CHUNK), BF16), pltpu.VMEM((2, rows, CHUNK), BF16),
            pltpu.VMEM((rows, width), BF16), pltpu.VMEM((rows, width), BF16), pltpu.VMEM((rows, width), BF16),
            pltpu.VMEM((rows, 3 * width), BF16), pltpu.VMEM((rows, 3 * width), BF16), pltpu.VMEM((2, GROUP, rows, rows), F32),
            pltpu.VMEM((rows, width), BF16),
            DMA((3,)), DMA((2,)), DMA((2,)), DMA((stages,)), DMA(()), DMA((4,)), DMA((3,)), DMA((3,)), DMA((2,)), DMA((2,)),
            pltpu.SemaphoreType.REGULAR],
        compiler_params=pltpu.CompilerParams(collective_id=1, has_side_effects=True, vmem_limit_bytes=LIMIT),
        name="backward",
    )(gtop, wqkv, wproj, wfc1, wfc2, g1, g2, x_s, qkv_s, h_s, d_s, p_s)


def matmul_rows(spec, left, right):
    return jnp.einsum(spec, left, right, preferred_element_type=F32)


def solution(mesh):
    stages = mesh.shape["pp"]
    in_specs = (P("dp"), P("dp"), P(), P(), P(), P()) + (P("pp"),) * 12 + (P(),) * 4
    out_specs = (P("dp"),) * 5 + (P(("dp", "pp")),) * 12 + (P("dp"),) * 4

    def body(patches, labels, w_patch, b_patch, cls_token, pos_embed, *rest):
        ln1_gain, ln1_bias, w_qkv, b_qkv, w_proj, b_proj, ln2_gain, ln2_bias, w_fc1, b_fc1, w_fc2, b_fc2 = (tensor[0] for tensor in rest[:12])
        lnf_gain, lnf_bias, w_head, b_head = rest[12:]
        tokens, width = pos_embed.shape
        heads, head = w_qkv.shape[2:]
        images = labels.size
        inv_count = 1.0 / images
        rows = -(-tokens // 16) * 16
        dims = (stages, images, tokens, heads, head)
        pad = ((0, 0), (0, rows - tokens), (0, 0))

        patch_rows = patches.reshape((images,) + patches.shape[2:])
        projected = matmul_rows("inp,pd->ind", patch_rows, w_patch) + b_patch.astype(F32)
        first = jnp.broadcast_to(cls_token.astype(F32), (images, 1, width))
        embedded = (jnp.concatenate([first, projected], axis=1) + pos_embed.astype(F32)).astype(BF16)
        embedded = jnp.pad(embedded, pad)

        line = lambda tensor: tensor.astype(F32).reshape(1, -1)
        wqkv_t = jnp.transpose(w_qkv, (1, 2, 3, 0)).reshape(3 * width, width)
        big = (wqkv_t, w_proj.reshape(width, width), w_fc1, w_fc2)
        vectors = tuple(map(line, (ln1_gain, ln1_bias, b_qkv, b_proj, ln2_gain, ln2_bias, b_fc1, b_fc2)))
        x_s, a_s, qkv_s, c_s, h_s, n_s, d_s, g_s, p_s, tops = run_forward(dims, embedded, *big, vectors)

        pooled, lnf_vjp = jax.vjp(layer_norm, tops[:, 0], lnf_gain.astype(F32), lnf_bias.astype(F32))
        logits = jnp.dot(pooled, w_head, preferred_element_type=F32) + b_head.astype(F32)
        classes = logits.shape[-1]
        log_probs = jax.nn.log_softmax(logits, axis=-1)
        target = (1.0 - SMOOTH) * jax.nn.one_hot(labels.reshape(-1), classes, dtype=F32) + SMOOTH / classes
        loss = -jnp.sum(target * log_probs) * inv_count
        grad_logits = (jnp.exp(log_probs) - target) * inv_count
        grad_low = grad_logits.astype(BF16)
        g_w_head = matmul_rows("bd,bc->dc", pooled, grad_low)
        g_b_head = jnp.sum(grad_logits, axis=0)
        grad_pooled = matmul_rows("bc,dc->bd", grad_low, w_head).astype(BF16)
        grad_tops, g_lnf_gain, g_lnf_bias = lnf_vjp(grad_pooled)
        gtop = jnp.pad(grad_tops[:, None], ((0, 0), (0, rows - 1), (0, 0)))

        gy_s, gpre_s, gmid_s, gqkv_s, gemb, *sums = run_backward(dims, gtop, *big, vectors[0], vectors[4], x_s, qkv_s, h_s, d_s, p_s)
        g_ln1_gain, g_ln1_bias, g_ln2_gain, g_ln2_bias, g_b_proj, g_b_fc2, g_b_qkv, g_b_fc1 = (jnp.sum(total, axis=0) for total in sums)

        flat = lambda array: array.reshape(images * rows, -1)
        g_w_qkv = matmul_rows("tn,td->nd", flat(gqkv_s), flat(a_s)).reshape(3, heads, head, width)
        layer_grads = (
            g_ln1_gain, g_ln1_bias, jnp.transpose(g_w_qkv, (3, 0, 1, 2)), g_b_qkv.reshape(3, heads, head),
            matmul_rows("tn,td->nd", flat(c_s), flat(gmid_s)).reshape(heads, head, width), g_b_proj,
            g_ln2_gain, g_ln2_bias,
            matmul_rows("tn,td->nd", flat(n_s), flat(gpre_s)), g_b_fc1,
            matmul_rows("tn,td->nd", flat(g_s), flat(gy_s)), g_b_fc2,
        )
        grad_embedded = gemb[:, :tokens]
        g_pos_embed = jnp.sum(grad_embedded.astype(F32), axis=0)
        embed_grads = (
            matmul_rows("inp,ind->pd", patch_rows, grad_embedded[:, 1:]),
            jnp.sum(g_pos_embed[1:], axis=0), g_pos_embed[0], g_pos_embed,
        )
        return (loss.reshape(1),) + embed_grads + tuple(grad[None] for grad in layer_grads) + (g_lnf_gain, g_lnf_bias, g_w_head, g_b_head)

    return jax.shard_map(body, mesh=mesh, in_specs=in_specs, out_specs=out_specs, check_vma=False)
```

time: 2620 us -> 1080 us (0.41)
  matrix products: 1610 us -> 182 us
  Pallas kernels: 0 us -> 811 us
  other arithmetic: 790 us -> 22 us
  starting transfers between devices: 83 us -> 0 us
  local copies, waits for them, and re-layouts: 104 us -> 51.7 us
    dot_general x106 -> x8, matrix products: 1520 us -> 180 us  [matmul_rows(): return jnp.einsum(spec, left, right, preferred_element_type=F32)]
    pallas_call x0 -> x2, Pallas kernels: none -> 811 us  [the longest x1 437 us: run_backward(): pl.pallas_call(functools.partial(backward_kernel, dims), out_shape=(hbm(w...]
    unnamed x50 -> x0, other arithmetic: 433 us -> none
    sub x7 -> x0, other arithmetic: 119 us -> none  [layer_forward(): probs = jax.nn.softmax(scores, axis=-1)]
    reduce_sum x15 -> x9, other arithmetic: 100 us -> 1.62 us  [the longest x1 0.81 us: body(): g_pos_embed = jnp.sum(grad_embedded.astype(F32), axis=0)]
    sub x7 -> x0, matrix products: 90.2 us -> none  [layer_backward(): grad_probs - jnp.sum(grad_probs * probs, axis=-1, keepdims=True)]
    ppermute x15 -> x0, starting transfers between devices: 83 us -> none  [the longest x6 66.8 us: body(): received = lax.ppermute(grad_in, 'pp', backward_perm)]
    another operation x11 -> x0, other arithmetic: 76.7 us -> none  [the longest x6 63.9 us: body(): stacks = [jnp.stack(group) for group in zip(*saves)]]
  transfers between devices with their start and end apart: 15 -> 0, of which waited for: 0 -> 0; matrix products, arithmetic and copies ran while one was open for 17% -> 0% of each run, Pallas kernels for 0% -> 0%
where the time goes in v2:
time: 1080 us; the launch traced here: 1070 us
  Pallas kernels  811 us (75%)
  matrix products  182 us (17%)
  local copies, waits for them, and re-layouts  51.7 us (5%)
  other arithmetic  22 us (2%)
    pallas_call x1, Pallas kernels, run_backward(): pl.pallas_call(functools.partial(backward_kernel, dims), out_shape=(hbm(w...  437 us
    pallas_call x1, Pallas kernels, run_forward(): pl.pallas_call(functools.partial(forward_kernel, dims), out_shape=(hbm(wi...  375 us
    dot_general x8, matrix products, matmul_rows(): return jnp.einsum(spec, left, right, preferred_element_type=F32)  180 us
    dot_general x2, local copies, waits for them, and re-layouts, matmul_rows(): return jnp.einsum(spec, left, right, preferred_element_type=F32)  33.9 us

profile of v2, /device:TPU:7, one launch (start us, length us, event | category | flops | bytes accessed | tf_op | source)
XLA Modules:
  0.0 1070.3 jit_solution(2978652050174517161)
XLA Ops:
  0.7 1.3 convert_element_type.110
  1.9 2.0 copy.48
  3.9 0.0 copy-start.2
  4.0 0.7 convert_element_type.93
  4.7 9.3 convolution_add_fusion
  14.0 0.1 convert_element_type.94
  14.2 8.3 fusion
  22.5 0.0 copy-start.33
  22.5 0.0 copy-start.34
  22.5 0.0 copy-start.20
  22.5 0.0 copy-start.35
  22.5 5.8 pad.8.refs_0_
  28.4 0.6 convert_element_type.96.refs_5_
  29.0 0.0 copy-done.31
  29.0 0.6 convert_element_type.97.refs_6_
  29.6 0.7 reshape.147.refs_7_
  30.3 0.6 convert_element_type.100.refs_8_
  30.9 0.6 convert_element_type.101.refs_9_.refs_6_
  31.5 0.6 convert_element_type.102.refs_10_
  32.1 0.0 copy-done.20
  32.1 0.6 convert_element_type.103.refs_11_
  32.7 0.0 copy-done.35
  32.7 0.6 convert_element_type.104.refs_12_
  33.3 374.5 %forward.1 = (bf16[8,272,1408]{2,1,0:T(8,128)(2,1)}, bf16[8,272,1408]{2,1,0:T(8,128)(2,1)}, bf16[8,272,4224]{2,1,0:T(8,128)(2,1)}, bf16[8,272,1408]{2,1,0:T(8,12...) custom-call(bf16[8,272,1408]{2,1,0:T(8,128)(2,1)} %pad.8.refs_0_, ...), custom_call_target="tpu_custom_call" | custom-call | tf_op jit(solution)/shard_map/forward/pallas_call | solution.py:601
  407.9 0.9 slice_convert_fusion
  408.8 0.0 copy-start.3
  408.8 0.7 convert_element_type.108
  409.5 0.7 convert_element_type.107
  410.2 1.1 fusion.12
  411.3 0.2 multiply_reduce_fusion.2
  411.6 2.8 fusion.17
  414.3 0.2 exponential_reduce_fusion
  414.6 0.8 copy.47
  415.3 0.1 eq.22
  415.4 0.7 fusion.9
  416.8 3.0 multiply_reduce_fusion
  419.7 0.2 fusion.16
  419.9 0.1 fusion.8
  420.0 3.1 pad.9.refs_0_
  423.1 0.0 copy-done.23
  423.2 0.0 copy-done.5
  423.2 0.0 copy-done.25
  423.2 436.5 %backward.1 = (bf16[8,272,1408]{2,1,0:T(8,128)(2,1)}, bf16[8,272,6144]{2,1,0:T(8,128)(2,1)}, bf16[8,272,1408]{2,1,0:T(8,128)(2,1)}, bf16[8,272,4224]{2,1,0:T(8,1...) custom-call(bf16[8,272,1408]{2,1,0:T(8,128)(2,1)} %pad.9.refs_0_, ...), custom_call_target="tpu_custom_call" | custom-call | tf_op jit(solution)/shard_map/backward/pallas_call | solution.py:627
  859.7 9.3 fusion.3
  869.0 0.8 convert_reduce_fusion
  869.9 0.0 copy-start
  869.9 0.9 slice_reduce_fusion
  870.8 0.2 copy-done
  871.0 0.6 slice_reduce_fusion.1
  871.6 0.6 broadcast_in_dim.56
  872.2 0.6 broadcast_in_dim.57
  872.8 24.5 %copy.50 = bf16[4224,2176]{1,0:T(8,128)(2,1)} copy(bf16[4224,2176]{0,1:T(8,128)(2,1)} %bitcast.83) | data formatting | bytes 36765696 | tf_op jit(solution)/shard_map/tn,td->nd/dot_general | solution.py:647
  897.4 37.6 %convolution_bitcast_fusion.2 = f32[1,1408,3,16,88]{1,4,3,2,0:T(8,128)} fusion(bf16[2176,1408,1,1]{1,0,3,2:T(8,128)(2,1)} %bitcast.92, bf16[3,16,88,2176]{3,2,1,0:T(8,128)(2,1)} %bitcast.84), kind=kOutput, calls=%fused_computation.2 | convolution fusion | flops 25883049984 | bytes 48300032 | tf_op jit(solution)/shard_map/tn,td->nd/dot_general | solution.py:647
  935.0 0.7 broadcast_in_dim_reshape.4
  935.7 9.3 copy.51
  945.0 16.0 %convolution_bitcast_fusion.3 = f32[1,16,88,1408]{3,2,1,0:T(8,128)} fusion(bf16[16,88,2176]{2,1,0:T(8,128)(2,1)} %bitcast.88, bf16[2176,1408,1]{1,0,2:T(8,128)(2,1)} %bitcast.93), kind=kOutput, calls=%fused_computation.9 | convolution fusion | flops 8627683328 | bytes 20185088 | tf_op jit(solution)/shard_map/tn,td->nd/dot_general | solution.py:647
  961.1 0.6 broadcast_in_dim.59
  961.7 0.6 broadcast_in_dim.60
  962.3 0.6 broadcast_in_dim.61
  962.9 48.6 %convolution_bitcast_fusion.1 = f32[1,1408,6144]{2,1,0:T(8,128)} fusion(bf16[8,272,1408]{2,1,0:T(8,128)(2,1)} %get-tuple-element.61, bf16[8,272,6144]{2,1,0:T(8,128)(2,1)} %get-tuple-element.62), kind=kOutput, calls=%fused_computation.1 | convolution fusion | flops 37648072704 | bytes 67469312 | tf_op jit(solution)/shard_map/tn,td->nd/dot_general | solution.py:647
  1011.5 0.7 reduce_sum.202
  1012.2 52.2 %convolution_bitcast_fusion = f32[1,6144,1408]{2,1,0:T(8,128)} fusion(bf16[8,272,6144]{2,1,0:T(8,128)(2,1)} %get-tuple-element.64, bf16[8,272,1408]{2,1,0:T(8,128)(2,1)} %get-tuple-element.65), kind=kOutput, calls=%fused_computation | convolution fusion | flops 37648072704 | bytes 67469312 | tf_op jit(solution)/shard_map/tn,td->nd/dot_general | solution.py:647
  1064.5 0.6 broadcast_in_dim.65
  1065.2 3.6 fusion.13
  (78 shorter events, 0.4 us)
Async XLA Ops:
  3.9 10.1 copy-start.2
  4.7 9.3 copy-start.38
  4.7 9.4 copy-start.7
  22.5 5.9 copy-start.30
  22.5 6.5 copy-start.31
  22.5 7.1 copy-start.27
  22.5 7.8 copy-start.32
  22.5 8.4 copy-start.33
  22.5 9.0 copy-start.34
  22.5 9.6 copy-start.20
  22.5 10.2 copy-start.35
  408.8 14.3 %copy-start.3 = (f32[8,1,1408]{2,1,0:T(1,128)}, f32[8,1,1408]{2,1,0:T(1,128)S(1)}, u32[]{:S(2)}) copy-start(f32[8,1,1408]{2,1,0:T(1,128)S(1)} %slice_convert_fusion) | copy-start | bytes 135172
  409.5 2.0 copy-start.10
  410.2 12.9 %copy-start.8 = (f32[1408]{0:T(1024)}, f32[1408]{0:T(1024)S(1)}, u32[]{:S(2)}) copy-start(f32[1408]{0:T(1024)S(1)} %convert_element_type.107) | copy-start | bytes 16900
  411.3 11.8 %copy-start.21 = (f32[8]{0:T(128)}, f32[8]{0:T(128)S(1)}, u32[]{:S(2)}) copy-start(f32[8]{0:T(128)S(1)} %broadcast_multiply_fusion) | copy-start | bytes 100
  411.5 11.6 %copy-start.23 = (f32[8]{0:T(128)}, f32[8]{0:T(128)S(1)}, u32[]{:S(2)}) copy-start(f32[8]{0:T(128)S(1)} %fusion.11) | copy-start | bytes 100
  414.3 8.8 copy-start.5
  414.3 8.8 copy-start.25
  414.5 8.6 copy-start.36
  415.4 7.8 copy-start.28
  859.7 9.3 copy-start.1
  869.0 2.6 copy-start.19
  869.0 3.2 copy-start.18
  869.9 1.1 copy-start
  897.4 37.6 %copy-start.13 = (f32[8,4224]{1,0:T(8,128)S(1)}, f32[8,4224]{1,0:T(8,128)}, u32[]{:S(2)}) copy-start(f32[8,4224]{1,0:T(8,128)} %get-tuple-element.55) | copy-start | bytes 405508
  945.0 16.0 %copy-start.17 = (f32[8,1408]{1,0:T(8,128)S(1)}, f32[8,1408]{1,0:T(8,128)}, u32[]{:S(2)}) copy-start(f32[8,1408]{1,0:T(8,128)} %get-tuple-element.58) | copy-start | bytes 135172
  945.0 16.6 %copy-start.16 = (f32[8,1408]{1,0:T(8,128)S(1)}, f32[8,1408]{1,0:T(8,128)}, u32[]{:S(2)}) copy-start(f32[8,1408]{1,0:T(8,128)} %get-tuple-element.59) | copy-start | bytes 135172
  945.0 17.3 %copy-start.15 = (f32[8,1408]{1,0:T(8,128)S(1)}, f32[8,1408]{1,0:T(8,128)}, u32[]{:S(2)}) copy-start(f32[8,1408]{1,0:T(8,128)} %get-tuple-element.60) | copy-start | bytes 135172
  962.9 48.6 %copy-start.12 = (f32[8,6144]{1,0:T(8,128)S(1)}, f32[8,6144]{1,0:T(8,128)}, u32[]{:S(2)}) copy-start(f32[8,6144]{1,0:T(8,128)} %get-tuple-element.63) | copy-start | bytes 589828
  1012.2 52.3 %copy-start.14 = (f32[8,1408]{1,0:T(8,128)S(1)}, f32[8,1408]{1,0:T(8,128)}, u32[]{:S(2)}) copy-start(f32[8,1408]{1,0:T(8,128)} %get-tuple-element.66) | copy-start | bytes 135172
  1012.2 52.9 %copy-start.4 = (f32[8,1,1408]{2,1,0:T(1,128)S(1)}, f32[8,1,1408]{2,1,0:T(1,128)}, u32[]{:S(2)}) copy-start(f32[8,1,1408]{2,1,0:T(1,128)} %copy-done.3) | copy-start | bytes 135172
  1012.2 52.9 %copy-start.6 = (f32[8,1000]{1,0:T(8,128)S(1)}, f32[8,1000]{1,0:T(8,128)}, u32[]{:S(2)}) copy-start(f32[8,1000]{1,0:T(8,128)} %copy-done.5) | copy-start | bytes 96004
  1012.2 52.9 %copy-start.9 = (f32[1408]{0:T(1024)S(1)}, f32[1408]{0:T(1024)}, u32[]{:S(2)}) copy-start(f32[1408]{0:T(1024)} %copy-done.8) | copy-start | bytes 16900
  1012.2 52.9 %copy-start.11 = (f32[1408]{0:T(1024)S(1)}, f32[1408]{0:T(1024)}, u32[]{:S(2)}) copy-start(f32[1408]{0:T(1024)} %copy-done.10) | copy-start | bytes 16900
  1012.2 52.9 %copy-start.22 = (f32[8]{0:T(128)S(1)}, f32[8]{0:T(128)}, u32[]{:S(2)}) copy-start(f32[8]{0:T(128)} %copy-done.21) | copy-start | bytes 100
  1012.2 52.9 %copy-start.24 = (f32[8]{0:T(128)S(1)}, f32[8]{0:T(128)}, u32[]{:S(2)}) copy-start(f32[8]{0:T(128)} %copy-done.23) | copy-start | bytes 100
  1012.2 52.9 %copy-start.26 = (f32[8]{0:T(128)S(1)}, f32[8]{0:T(128)}, u32[]{:S(2)}) copy-start(f32[8]{0:T(128)} %copy-done.25) | copy-start | bytes 100
  1012.2 52.9 %copy-start.29 = (s32[8]{0:T(128)S(1)}, s32[8]{0:T(128)}, u32[]{:S(2)}) copy-start(s32[8]{0:T(128)} %copy-done.28) | copy-start | bytes 100
  1012.2 52.9 %copy-start.37 = (f32[8]{0:T(128)S(1)}, f32[8]{0:T(128)}, u32[]{:S(2)}) copy-start(f32[8]{0:T(128)} %copy-done.36) | copy-start | bytes 100

commit v3 on v2

v3 whole, which is shorter than its diff:
```python
import functools
import math
import jax
import jax.numpy as jnp
from jax import lax
from jax.experimental import pallas as pl
from jax.experimental.pallas import tpu as pltpu
from jax.sharding import PartitionSpec as P

EPS = 1e-6
SMOOTH = 0.1
F32 = jnp.float32
BF16 = jnp.bfloat16
MESH = pl.DeviceIdType.MESH
LANES = 128
HALF = 384
CHUNK = 2 * HALF
GROUP = 4
BLOCK = 136


def layer_norm(hidden, gain, bias):
    values = hidden.astype(F32)
    centered = values - jnp.mean(values, axis=-1, keepdims=True)
    variance = jnp.mean(jnp.square(centered), axis=-1, keepdims=True)
    return (centered * lax.rsqrt(variance + EPS) * gain + bias).astype(BF16)


def dot(left, right, left_axis=1, right_axis=0):
    return lax.dot_general(left, right, (((left_axis,), (right_axis,)), ((), ())), preferred_element_type=F32)


def by_rows(rows, visit):
    def step(index, carry):
        visit(pl.ds(pl.multiple_of(index * BLOCK, BLOCK), BLOCK))
        return carry

    lax.fori_loop(0, rows // BLOCK, step, 0)
    if rows % BLOCK:
        visit(pl.ds(rows - rows % BLOCK, rows % BLOCK))


def fold(values):
    rows, columns = values.shape
    return jnp.sum(values.reshape(rows // 8, 8, columns), axis=0)


def everyone(stage, stages):
    barrier = pltpu.get_barrier_semaphore()
    for hop in range(1, stages):
        pl.semaphore_signal(barrier, inc=1, device_id={"pp": lax.rem(stage + hop, stages)}, device_id_type=MESH)
    pl.semaphore_wait(barrier, stages - 1)


def forward_kernel(dims, *refs):
    (emb, wqkv, wproj, wfc1, wfc2, *given,
     x_s, a_s, qkv_s, c_s, h_s, n_s, d_s, g_s, p_s, tops_out,
     vqkv, vproj, vfc1, vfc2, xin, act, qkv, mid, yacc, ubuf, gbuf, pbuf, tops,
     g1, b1, bqkv, bproj, g2, b2, bfc1, bfc2,
     wsem, qsem, recv_sem, send_sem, top_sem, save_sem, usem, gsem, psem, free_sem) = refs
    stages, images, tokens, heads, head = dims
    rows, width = mid.shape
    chunks = vfc1.shape[1] // CHUNK
    stage = lax.axis_index("pp")
    is_first = stage == 0
    is_last = stage == stages - 1
    scale2 = head ** -0.5 / math.log(2.0)


    def qkv_copy(index):
        slot = lax.rem(index, 2)
        lines = pl.ds(pl.multiple_of(lax.rem(index, 3) * width, 128), width)
        return pltpu.make_async_copy(wqkv.at[lines], vqkv.at[slot], qsem.at[slot])

    def emb_copy(image, slot):
        return pltpu.make_async_copy(emb.at[image], xin.at[slot], recv_sem.at[slot])

    qkv_copy(0).start()

    @pl.when(is_first)
    def _():
        emb_copy(0, 0).start()
        emb_copy(1, 1).start()

    qkv_copy(1).start()
    proj_copy = pltpu.make_async_copy(wproj, vproj, wsem.at[0])
    fc1_copy = pltpu.make_async_copy(wfc1, vfc1, wsem.at[1])
    fc2_copy = pltpu.make_async_copy(wfc2, vfc2, wsem.at[2])
    proj_copy.start()
    fc1_copy.start()
    fc2_copy.start()
    qkv[...] = jnp.zeros_like(qkv)
    for low, wide in zip(given, (g1, b1, bqkv, bproj, g2, b2, bfc1, bfc2)):
        wide[...] = low[...].astype(F32)
    everyone(stage, stages)

    def saves(image, slot):
        pairs = ((xin.at[slot], x_s), (act, a_s), (qkv, qkv_s), (act, c_s), (mid, h_s), (act, n_s))
        return [pltpu.make_async_copy(src, dst.at[image], save_sem.at[at]) for at, (src, dst) in enumerate(pairs)]

    class u_save:
        def __init__(self, image, chunk):
            slot = lax.rem(chunk, 3)
            self.copies = [
                pltpu.make_async_copy(ubuf.at[slot, :, pl.ds(side * HALF, HALF)], d_s.at[image, chunk * 2 + side], usem.at[slot, side])
                for side in range(2)]

        def start(self):
            for copy in self.copies:
                copy.start()

        def wait(self):
            for copy in self.copies:
                copy.wait()

    def g_save(image, chunk):
        slot = lax.rem(chunk, 2)
        return pltpu.make_async_copy(gbuf.at[slot], g_s.at[image, :, pl.ds(pl.multiple_of(chunk * CHUNK, CHUNK), CHUNK)], gsem.at[slot])

    def p_save(image, group):
        slot = group % 2
        return pltpu.make_async_copy(pbuf.at[slot], p_s.at[image, pl.ds(group * GROUP, GROUP)], psem.at[slot])

    def top_copy(image, other):
        return pltpu.make_async_remote_copy(
            src_ref=mid.at[pl.ds(0, 16)], dst_ref=tops.at[image], send_sem=send_sem.at[1 + other], recv_sem=top_sem,
            device_id={"pp": other}, device_id_type=MESH)

    def next_copy(image, slot):
        return pltpu.make_async_remote_copy(
            src_ref=mid, dst_ref=xin.at[slot], send_sem=send_sem.at[0], recv_sem=recv_sem.at[slot],
            device_id={"pp": lax.rem(stage + 1, stages)}, device_id_type=MESH)

    def wait_sent(image):
        @pl.when(jnp.logical_not(is_last))
        def _():
            next_copy(image, 0).wait_send()

        @pl.when(is_last)
        def _():
            for other in range(stages - 1):
                top_copy(image, other).wait_send()

    def one_image(image, carry):
        slot = lax.rem(image, 2)
        save_x, save_a, save_qkv, save_c, save_h, save_n = saves(image, slot)
        emb_copy(image, slot).wait()
        save_x.start()

        @pl.when(image > 0)
        def _():
            save_n.wait()
            save_qkv.wait()

        def norm1(lines):
            act[lines, :] = layer_norm(xin[slot, lines, :], g1[...], b1[...])

        by_rows(rows, norm1)
        save_a.start()

        def qkv_part(part, carry):
            index = image * 3 + part
            qkv_copy(index).wait()
            low = (dot(act[...], vqkv[lax.rem(index, 2)], 1, 1) + bqkv[part]).astype(BF16)
            for at in range(heads):
                lane = part * (heads * LANES) + at * LANES
                qkv[:, pl.ds(pl.multiple_of(lane, LANES), head)] = low[:, at * head:(at + 1) * head]

            @pl.when(index + 2 < images * 3)
            def _():
                qkv_copy(index + 2).start()

            return carry

        lax.fori_loop(0, 3, qkv_part, 0)
        save_qkv.start()

        save_a.wait()

        @pl.when(image > 0)
        def _():
            p_save(image, 0).wait()
            p_save(image, 1).wait()

        def scores_of(number):
            q, k = (qkv[:, lane:lane + LANES] for lane in (number * LANES, (heads + number) * LANES))
            return dot(k, q, 1, 1)

        def attend(number, scores):
            group, inner = number // GROUP, number % GROUP
            if group >= 2 and inner == 0:
                p_save(image, group).wait()
            v = qkv[:, (2 * heads + number) * LANES:(2 * heads + number + 1) * LANES]
            top, tail = scores[:tokens - 1], scores[tokens - 1:]
            most = jnp.maximum(jnp.max(top, axis=0, keepdims=True), tail[:1])
            top = jnp.exp2((top - most) * scale2)
            real = lax.broadcasted_iota(jnp.int32, tail.shape, 0) < 1
            tail = jnp.where(real, jnp.exp2(jnp.minimum(tail - most, 0.0) * scale2), 0.0)
            inv = 1.0 / (jnp.sum(top, axis=0, keepdims=True) + jnp.sum(tail, axis=0, keepdims=True))
            probs = jnp.concatenate([top, tail], axis=0) * inv
            pbuf[group % 2, inner, :, :rows] = probs
            act[:, number * head:(number + 1) * head] = dot(probs.astype(BF16), v, 0, 0).astype(BF16)[:, :head]
            if inner == GROUP - 1:
                p_save(image, group).start()

        scores = scores_of(0)
        for number in range(heads):
            later = scores_of(number + 1) if number + 1 < heads else None
            attend(number, scores)
            scores = later
        save_c.start()

        @pl.when(image == 0)
        def _():
            proj_copy.wait()

        @pl.when(image > 0)
        def _():
            wait_sent(image)

        mid[...] = (dot(act[...], vproj[...]) + bproj[...] + xin[slot].astype(F32)).astype(BF16)
        save_h.start()
        save_x.wait()

        @pl.when(jnp.logical_and(is_first, image + 2 < images))
        def _():
            emb_copy(image + 2, slot).start()

        @pl.when(jnp.logical_and(stage > 0, image + 2 < images))
        def _():
            pl.semaphore_signal(free_sem, inc=1, device_id={"pp": lax.rem(stage + stages - 1, stages)}, device_id_type=MESH)

        save_c.wait()

        def norm2(lines):
            hidden = mid[lines, :]
            act[lines, :] = layer_norm(hidden, g2[...], b2[...])
            yacc[lines, :] = hidden.astype(F32) + bfc2[...]

        by_rows(rows, norm2)
        save_n.start()

        @pl.when(image == 0)
        def _():
            fc1_copy.wait()
            fc2_copy.wait()

        @pl.when(image > 0)
        def _():
            for chunk in range(3):
                u_save(image, chunk).wait()
            for chunk in range(2):
                g_save(image, chunk).wait()

        def fc1(chunk):
            columns = pl.ds(pl.multiple_of(chunk * CHUNK, CHUNK), CHUNK)
            ubuf[lax.rem(chunk, 3)] = dot(act[...], vfc1[:, columns]) + bfc1[:, columns]

        def gelu(chunk):
            slot3, slot2 = lax.rem(chunk, 3), lax.rem(chunk, 2)
            pre = ubuf[slot3]
            cdf = 0.5 + 0.5 * lax.erf(pre * (0.5 ** 0.5))
            pdf = jnp.exp2(pre * pre * (-0.5 / math.log(2.0))) * ((2.0 * math.pi) ** -0.5)
            activ = (pre * cdf).astype(BF16)
            gbuf[slot2] = activ
            ubuf[slot3] = cdf + pre * pdf
            return activ

        def fc2(chunk, activ):
            yacc[...] += dot(activ, vfc2[pl.ds(pl.multiple_of(chunk * CHUNK, CHUNK), CHUNK), :])

        fc1(0)

        def mlp_step(chunk, carry):
            @pl.when(chunk >= 3)
            def _():
                u_save(image, chunk).wait()
                g_save(image, chunk - 1).wait()

            @pl.when(chunk >= 2)
            def _():
                u_save(image, chunk - 2).start()
                g_save(image, chunk - 2).start()

            activ = gelu(chunk - 1)
            fc1(chunk)
            fc2(chunk - 1, activ)
            return carry

        lax.fori_loop(1, chunks, mlp_step, 0)
        g_save(image, chunks - 1).wait()
        u_save(image, chunks - 2).start()
        g_save(image, chunks - 2).start()
        fc2(chunks - 1, gelu(chunks - 1))
        u_save(image, chunks - 1).start()
        g_save(image, chunks - 1).start()

        save_h.wait()
        mid[...] = yacc[...].astype(BF16)

        @pl.when(jnp.logical_and(jnp.logical_not(is_last), image >= 2))
        def _():
            pl.semaphore_wait(free_sem, 1)

        @pl.when(jnp.logical_not(is_last))
        def _():
            next_copy(image, slot).start()

        @pl.when(is_last)
        def _():
            for other in range(stages - 1):
                top_copy(image, other).start()
            tops[image] = mid[pl.ds(0, 16), :]

        return carry

    lax.fori_loop(0, images, one_image, 0)
    wait_sent(images - 1)
    _, _, save_qkv, _, _, save_n = saves(images - 1, 0)
    save_qkv.wait()
    save_n.wait()
    for chunk in range(3):
        u_save(images - 1, chunk).wait()
    for chunk in range(2):
        g_save(images - 1, chunk).wait()
        p_save(images - 1, chunk).wait()

    @pl.when(jnp.logical_not(is_last))
    def _():
        pltpu.make_async_copy(tops, tops, top_sem).wait()

    for image in range(images):
        tops_out[image:image + 1, :] = tops[image, 0:1, :]


def norm_backward(grad, hidden, gain):
    values = hidden.astype(F32)
    centered = values - jnp.mean(values, axis=-1, keepdims=True)
    inv = lax.rsqrt(jnp.mean(jnp.square(centered), axis=-1, keepdims=True) + EPS)
    unit = centered * inv
    scaled = grad * gain
    grad_in = inv * (scaled - jnp.mean(scaled, axis=-1, keepdims=True) - unit * jnp.mean(scaled * unit, axis=-1, keepdims=True))
    return grad_in, grad * unit


def backward_kernel(dims, *refs):
    (gtop, wqkv, wproj, wfc1, wfc2, low1, low2, x_s, qkv_s, h_s, d_s, p_s,
     gy_s, gpre_s, gmid_s, gqkv_s, gemb, *sums_out,
     vqkv, vproj, vfc1, vfc2, gin, acc, shared, abuf, gbuf, hid, gmid, gctx, qkv, gqkv, gout, g1, g2,
     sum1g, sum1b, sum2g, sum2b, sumproj, sumfc2, sumqkv, sumfc1,
     wsem, qsem, recv_sem, top_sem, send_sem, emb_sem, save_sem, load_sem, dsem, gsem, psem, free_sem) = refs
    stages, images, tokens, heads, head = dims
    rows, width = gmid.shape
    chunks = vfc1.shape[1] // CHUNK
    groups = heads // GROUP
    stage = lax.axis_index("pp")
    is_first = stage == 0
    is_last = stage == stages - 1
    scale = head ** -0.5

    pieces = ((0, vqkv.shape[1]), (vqkv.shape[1], width - vqkv.shape[1]))

    def qkv_copy(part, side):
        slot = lax.rem(part * 2 + side, 3)
        at, size = pieces[side]
        lines = pl.ds(pl.multiple_of(lax.rem(part, 3) * width + at, 128), size)
        return pltpu.make_async_copy(wqkv.at[lines], vqkv.at[slot, pl.ds(0, size)], qsem.at[slot])

    def top_copy(image, slot):
        return pltpu.make_async_copy(gtop.at[image], gin.at[slot, pl.ds(0, 16)], top_sem.at[slot])

    def d_load(image, chunk):
        slot = lax.rem(chunk, 4)
        return pltpu.make_async_copy(d_s.at[image, pl.ds(chunk * 2, 2)], shared.at[pl.ds(slot * 2, 2)], dsem.at[slot])

    def g_save(image, chunk):
        slot = lax.rem(chunk, 2)
        return pltpu.make_async_copy(gbuf.at[slot], gpre_s.at[image, :, pl.ds(pl.multiple_of(chunk * CHUNK, CHUNK), CHUNK)], gsem.at[slot])

    def p_load(image, group):
        slot = group % 2
        return pltpu.make_async_copy(p_s.at[image, pl.ds(group * GROUP, GROUP)], shared.at[pl.ds(slot * GROUP, GROUP)], psem.at[slot])

    def saves(image, slot):
        pairs = ((gin.at[slot], gy_s), (gmid, gmid_s), (gqkv, gqkv_s))
        return [pltpu.make_async_copy(src, dst.at[image], save_sem.at[at]) for at, (src, dst) in enumerate(pairs)]

    def loads(image):
        pairs = ((h_s, hid), (x_s, hid), (qkv_s, qkv))
        return [pltpu.make_async_copy(src.at[image], dst, load_sem.at[at]) for at, (src, dst) in enumerate(pairs)]

    def next_copy(slot):
        return pltpu.make_async_remote_copy(
            src_ref=gout, dst_ref=gin.at[slot], send_sem=send_sem.at[0], recv_sem=recv_sem.at[slot],
            device_id={"pp": lax.rem(stage + stages - 1, stages)}, device_id_type=MESH)

    def emb_send(image, other):
        return pltpu.make_async_remote_copy(
            src_ref=gout, dst_ref=gemb.at[image], send_sem=send_sem.at[other], recv_sem=emb_sem,
            device_id={"pp": other}, device_id_type=MESH)

    def emb_local(image):
        return pltpu.make_async_copy(gout, gemb.at[image], save_sem.at[3])

    def wait_sent(image):
        @pl.when(jnp.logical_not(is_first))
        def _():
            next_copy(0).wait_send()

        @pl.when(is_first)
        def _():
            for other in range(1, stages):
                emb_send(image, other).wait_send()
            emb_local(image).wait()

    @pl.when(is_last)
    def _():
        gin[...] = jnp.zeros_like(gin)
        top_copy(0, 0).start()
        top_copy(1, 1).start()

    fc2_copy = pltpu.make_async_copy(wfc2, vfc2, wsem.at[2])
    fc1_copy = pltpu.make_async_copy(wfc1, vfc1, wsem.at[1])
    proj_copy = pltpu.make_async_copy(wproj, vproj, wsem.at[0])
    fc2_copy.start()
    for chunk in range(4):
        d_load(0, chunk).start()
    fc1_copy.start()
    loads(0)[0].start()
    loads(0)[2].start()
    proj_copy.start()
    qkv_copy(0, 0).start()
    qkv_copy(0, 1).start()
    qkv_copy(1, 0).start()
    gctx[...] = jnp.zeros_like(gctx)
    sums_out, totals = sums_out[:8], (sum1g, sum1b, sum2g, sum2b, sumproj, sumfc2, sumqkv, sumfc1)
    for total in totals:
        total[...] = jnp.zeros_like(total)
    g1[...] = low1[...].astype(F32)
    g2[...] = low2[...].astype(F32)
    everyone(stage, stages)

    def one_image(image, carry):
        slot = lax.rem(image, 2)
        more = image + 1 < images
        save_gy, save_mid, save_qkv = saves(image, slot)
        load_h, load_x, load_qkv = loads(image)

        @pl.when(is_last)
        def _():
            top_copy(image, slot).wait()

        @pl.when(jnp.logical_not(is_last))
        def _():
            next_copy(slot).wait_recv()

        save_gy.start()

        @pl.when(image == 0)
        def _():
            fc2_copy.wait()
            fc1_copy.wait()

        @pl.when(image > 0)
        def _():
            for chunk in range(2):
                g_save(image, chunk).wait()

        acc[...] = jnp.zeros_like(acc)

        def fc2(chunk):
            lines = pl.ds(pl.multiple_of(chunk * CHUNK, CHUNK), CHUNK)
            abuf[lax.rem(chunk, 2)] = dot(gin[slot], vfc2[lines, :], 1, 1).astype(BF16)

        def gelu(chunk):
            columns = pl.ds(pl.multiple_of(chunk * CHUNK, CHUNK), CHUNK)
            slot2 = lax.rem(chunk, 2)
            slot4 = lax.rem(chunk, 4)
            pre = abuf[slot2].astype(F32) * jnp.concatenate([shared[slot4 * 2], shared[slot4 * 2 + 1]], axis=1)
            sumfc1[:, columns] += fold(pre)
            low = pre.astype(BF16)
            gbuf[slot2] = low
            return low

        def fc1(chunk, low):
            columns = pl.ds(pl.multiple_of(chunk * CHUNK, CHUNK), CHUNK)
            acc[...] += dot(low, vfc1[:, columns], 1, 1)

        fc2(0)

        def mlp_step(chunk, carry):
            d_load(image, chunk - 1).wait()

            @pl.when(chunk >= 3)
            def _():
                g_save(image, chunk - 1).wait()

            @pl.when(chunk >= 2)
            def _():
                g_save(image, chunk - 2).start()

                @pl.when(chunk + 2 < chunks)
                def _():
                    d_load(image, chunk + 2).start()

            low = gelu(chunk - 1)
            fc2(chunk)
            fc1(chunk - 1, low)
            return carry

        lax.fori_loop(1, chunks, mlp_step, 0)
        d_load(image, chunks - 1).wait()
        g_save(image, chunks - 1).wait()
        g_save(image, chunks - 2).start()
        fc1(chunks - 1, gelu(chunks - 1))
        g_save(image, chunks - 1).start()

        for group in range(2):
            p_load(image, group).start()
        load_h.wait()

        @pl.when(image > 0)
        def _():
            save_mid.wait()
            save_qkv.wait()

        def back2(lines):
            grad = acc[lines, :].astype(BF16).astype(F32)
            grad_in, by_unit = norm_backward(grad, hid[lines, :], g2[...])
            sum2g[...] += fold(by_unit)
            sum2b[...] += fold(grad)
            top = gin[slot, lines, :].astype(F32)
            sumfc2[...] += fold(top)
            low = (top + grad_in).astype(BF16)
            gmid[lines, :] = low
            sumproj[...] += fold(low.astype(F32))

        by_rows(rows, back2)
        save_mid.start()
        load_x.start()
        save_gy.wait()

        @pl.when(jnp.logical_and(is_last, image + 2 < images))
        def _():
            top_copy(image + 2, slot).start()

        @pl.when(jnp.logical_and(stage < stages - 1, image + 2 < images))
        def _():
            pl.semaphore_signal(free_sem, inc=1, device_id={"pp": lax.rem(stage + 1, stages)}, device_id_type=MESH)

        @pl.when(image == 0)
        def _():
            proj_copy.wait()

        low = dot(gmid[...], vproj[...], 1, 1).astype(BF16)
        for number in range(heads):
            gctx[:, number * LANES:number * LANES + head] = low[:, number * head:(number + 1) * head]
        load_qkv.wait()
        def lanes_of(number):
            return slice(number * LANES, (number + 1) * LANES)

        def grad_probs_of(number):
            return dot(qkv[:, lanes_of(2 * heads + number)], gctx[:, lanes_of(number)], 1, 1)

        def attend(number, grad_probs):
            group, inner = number // GROUP, number % GROUP
            if inner == 0:
                p_load(image, group).wait()
            probs = shared[group % 2 * GROUP + inner, :, :rows]
            at = number * head
            mean = jnp.sum(grad_probs * probs, axis=0, keepdims=True)
            low = (probs * (grad_probs - mean) * scale).astype(BF16)
            value = dot(probs.astype(BF16), gctx[:, lanes_of(number)]).astype(BF16)
            gqkv[:, 2 * width + at:2 * width + at + head] = value[:, :head]
            key = dot(low, qkv[:, lanes_of(number)]).astype(BF16)
            gqkv[:, width + at:width + at + head] = key[:, :head]
            query = dot(low, qkv[:, lanes_of(heads + number)], 0, 0).astype(BF16)
            gqkv[:, at:at + head] = query[:, :head]

        def refill(group):
            if group + 2 < groups:
                p_load(image, group + 2).start()
            else:
                @pl.when(more)
                def _():
                    for chunk in range((group + 2 - groups) * 2, (group + 2 - groups) * 2 + 2):
                        d_load(image + 1, chunk).start()

        grad_probs = grad_probs_of(0)
        for number in range(heads):
            later = grad_probs_of(number + 1) if number + 1 < heads else None
            attend(number, grad_probs)
            grad_probs = later
            if number % GROUP == GROUP - 1:
                refill(number // GROUP)
        save_qkv.start()

        @pl.when(more)
        def _():
            loads(image + 1)[2].start()

        def qkv_part(part, carry):
            for side in range(2):
                at, size = pieces[side]
                index = image * 3 + part
                qkv_copy(index, side).wait()
                columns = pl.ds(pl.multiple_of(part * width + at, 128), size)
                piece = gqkv[:, columns]
                sumqkv[:, columns] += fold(piece.astype(F32))
                acc[...] += dot(piece, vqkv[lax.rem(index * 2 + side, 3), :size])

                @pl.when(index + 1 + side < images * 3)
                def _():
                    qkv_copy(index + 1 + side, 1 - side).start()

            return carry

        acc[...] = jnp.zeros_like(acc)
        lax.fori_loop(0, 3, qkv_part, 0)
        load_x.wait()

        @pl.when(image > 0)
        def _():
            wait_sent(image)

        def back1(lines):
            grad = acc[lines, :].astype(BF16).astype(F32)
            grad_in, by_unit = norm_backward(grad, hid[lines, :], g1[...])
            sum1g[...] += fold(by_unit)
            sum1b[...] += fold(grad)
            gout[lines, :] = (gmid[lines, :].astype(F32) + grad_in).astype(BF16)

        by_rows(rows, back1)

        @pl.when(more)
        def _():
            loads(image + 1)[0].start()

        @pl.when(jnp.logical_and(jnp.logical_not(is_first), image >= 2))
        def _():
            pl.semaphore_wait(free_sem, 1)

        @pl.when(jnp.logical_not(is_first))
        def _():
            next_copy(slot).start()

        @pl.when(is_first)
        def _():
            for other in range(1, stages):
                emb_send(image, other).start()
            emb_local(image).start()

        return carry

    lax.fori_loop(0, images, one_image, 0)
    wait_sent(images - 1)
    _, save_mid, save_qkv = saves(images - 1, 0)
    save_mid.wait()
    save_qkv.wait()
    for chunk in range(2):
        g_save(images - 1, chunk).wait()

    for out, total in zip(sums_out, totals):
        out[...] = jnp.sum(total[...], axis=0, keepdims=True)

    @pl.when(jnp.logical_not(is_first))
    def _():
        pltpu.make_async_copy(gemb, gemb, emb_sem).wait()


ANY = pl.BlockSpec(memory_space=pl.ANY)
VMEM = pl.BlockSpec(memory_space=pltpu.VMEM)
LIMIT = 67_043_328
DMA = pltpu.SemaphoreType.DMA


def run_forward(dims, emb, wqkv, wproj, wfc1, wfc2, vectors):
    stages, images, tokens, heads, head = dims
    rows, width = emb.shape[1:]
    hidden = wfc1.shape[1]
    hbm = lambda *shape, dtype=BF16: jax.ShapeDtypeStruct((images, rows) + shape, dtype)
    return pl.pallas_call(
        functools.partial(forward_kernel, dims),
        out_shape=(
            hbm(width), hbm(width), hbm(3 * heads * LANES), hbm(width), hbm(width), hbm(width),
            jax.ShapeDtypeStruct((images, hidden // HALF, rows, HALF), F32), hbm(hidden),
            jax.ShapeDtypeStruct((images, heads, rows, HALF), F32), jax.ShapeDtypeStruct((images, width), BF16)),
        in_specs=[ANY] * 5 + [VMEM] * 8,
        out_specs=(ANY,) * 9 + (VMEM,),
        scratch_shapes=[
            pltpu.VMEM((2, width, width), BF16), pltpu.VMEM(wproj.shape, BF16), pltpu.VMEM(wfc1.shape, BF16), pltpu.VMEM(wfc2.shape, BF16),
            pltpu.VMEM((2, rows, width), BF16), pltpu.VMEM((rows, width), BF16), pltpu.VMEM((rows, 3 * heads * LANES), BF16),
            pltpu.VMEM((rows, width), BF16), pltpu.VMEM((rows, width), F32),
            pltpu.VMEM((3, rows, CHUNK), F32), pltpu.VMEM((2, rows, CHUNK), BF16), pltpu.VMEM((2, GROUP, rows, HALF), F32),
            pltpu.VMEM((images, 16, width), BF16),
            *(pltpu.VMEM(vector.shape, F32) for vector in vectors),
            DMA((3,)), DMA((2,)), DMA((2,)), DMA((stages,)), DMA(()), DMA((6,)), DMA((3, 2)), DMA((2,)), DMA((2,)),
            pltpu.SemaphoreType.REGULAR],
        compiler_params=pltpu.CompilerParams(collective_id=0, has_side_effects=True, vmem_limit_bytes=LIMIT),
        name="forward",
    )(emb, wqkv, wproj, wfc1, wfc2, *vectors)


def run_backward(dims, gtop, wqkv, wproj, wfc1, wfc2, g1, g2, x_s, qkv_s, h_s, d_s, p_s):
    stages, images, tokens, heads, head = dims
    rows, width = x_s.shape[1:]
    hidden = wfc1.shape[1]
    hbm = lambda *shape: jax.ShapeDtypeStruct((images, rows) + shape, BF16)
    sizes = (width,) * 6 + (3 * width, hidden)
    return pl.pallas_call(
        functools.partial(backward_kernel, dims),
        out_shape=(hbm(width), hbm(hidden), hbm(width), hbm(3 * width), hbm(width)) + tuple(jax.ShapeDtypeStruct((1, size), F32) for size in sizes),
        in_specs=[ANY] * 5 + [VMEM] * 2 + [ANY] * 5,
        out_specs=(ANY,) * 5 + (VMEM,) * 8,
        scratch_shapes=[
            pltpu.VMEM((3, -(-width // 256) * LANES, width), BF16), pltpu.VMEM(wproj.shape, BF16), pltpu.VMEM(wfc1.shape, BF16), pltpu.VMEM(wfc2.shape, BF16),
            pltpu.VMEM((2, rows, width), BF16), pltpu.VMEM((rows, width), F32), pltpu.VMEM((2 * GROUP, rows, HALF), F32),
            pltpu.VMEM((2, rows, CHUNK), BF16), pltpu.VMEM((2, rows, CHUNK), BF16),
            pltpu.VMEM((rows, width), BF16), pltpu.VMEM((rows, width), BF16), pltpu.VMEM((rows, heads * LANES), BF16),
            pltpu.VMEM((rows, 3 * heads * LANES), BF16), pltpu.VMEM((rows, 3 * width), BF16),
            pltpu.VMEM((rows, width), BF16), pltpu.VMEM((1, width), F32), pltpu.VMEM((1, width), F32),
            *(pltpu.VMEM((8, size), F32) for size in sizes),
            DMA((3,)), DMA((3,)), DMA((2,)), DMA((2,)), DMA((stages,)), DMA(()), DMA((4,)), DMA((3,)), DMA((4,)), DMA((2,)), DMA((2,)),
            pltpu.SemaphoreType.REGULAR],
        compiler_params=pltpu.CompilerParams(collective_id=1, has_side_effects=True, vmem_limit_bytes=LIMIT),
        name="backward",
    )(gtop, wqkv, wproj, wfc1, wfc2, g1, g2, x_s, qkv_s, h_s, d_s, p_s)


def head_kernel(inv_count, tops, labels, gain, bias, w_head, b_head, loss, gtop, g_gain, g_bias, g_w_head, g_b_head):
    images, width = tops.shape
    wide_gain = gain[...].astype(F32)
    pooled = layer_norm(tops[...], wide_gain, bias[...].astype(F32))
    logits = dot(pooled, w_head[...], 1, 1) + b_head[...].astype(F32)
    shifted = logits - jnp.max(logits, axis=-1, keepdims=True)
    log_probs = shifted - jnp.log(jnp.sum(jnp.exp(shifted), axis=-1, keepdims=True))
    classes = logits.shape[-1]
    line = lax.broadcasted_iota(jnp.int32, (images, 1), 0)
    label = jnp.zeros((images, 1), jnp.int32)
    for image in range(images):
        label = jnp.where(line == image, labels[image // labels.shape[1], image % labels.shape[1]], label)
    chosen = (lax.broadcasted_iota(jnp.int32, logits.shape, 1) == label).astype(F32)
    target = (1.0 - SMOOTH) * chosen + SMOOTH / classes
    parts = jnp.sum(target * log_probs, axis=-1, keepdims=True)
    loss[...] = -jnp.sum(parts, axis=0, keepdims=True) * inv_count
    grad_logits = (jnp.exp(log_probs) - target) * inv_count
    low = grad_logits.astype(BF16)
    g_w_head[...] = dot(low, pooled, 0, 0)
    g_b_head[...] = jnp.sum(grad_logits, axis=0, keepdims=True)
    grad = dot(low, w_head[...]).astype(BF16).astype(F32)
    grad_in, by_unit = norm_backward(grad, tops[...], wide_gain)
    g_gain[...] = jnp.sum(by_unit, axis=0, keepdims=True)
    g_bias[...] = jnp.sum(grad, axis=0, keepdims=True)
    gtop[...] = jnp.zeros_like(gtop)
    for image in range(images):
        gtop[image, 0:1, :] = grad_in[image:image + 1].astype(BF16)


def run_head(inv_count, tops, labels, gain, bias, w_head, b_head):
    images, width = tops.shape
    classes = w_head.shape[0]
    shape = lambda *dims, dtype=F32: jax.ShapeDtypeStruct(dims, dtype)
    return pl.pallas_call(
        functools.partial(head_kernel, inv_count),
        out_shape=(shape(1, 1), shape(images, 16, width, dtype=BF16), shape(1, width), shape(1, width), shape(classes, width), shape(1, classes)),
        in_specs=[VMEM, pl.BlockSpec(memory_space=pltpu.SMEM)] + [VMEM] * 4,
        out_specs=(VMEM,) * 6,
        compiler_params=pltpu.CompilerParams(vmem_limit_bytes=LIMIT),
        name="head",
    )(tops, labels, gain, bias, w_head, b_head)


def outer_kernel(left, right, out):
    out[...] = dot(left[...], right[...], 0, 0)


def outer_by_left(left, right, block):
    rows, size = left.shape
    width = right.shape[1]
    return pl.pallas_call(
        outer_kernel,
        out_shape=jax.ShapeDtypeStruct((size, width), F32),
        grid=(size // block,),
        in_specs=[pl.BlockSpec((rows, block), lambda at: (0, at)), pl.BlockSpec((rows, width), lambda at: (0, 0))],
        out_specs=pl.BlockSpec((block, width), lambda at: (at, 0)),
        compiler_params=pltpu.CompilerParams(vmem_limit_bytes=LIMIT),
        cost_estimate=pl.CostEstimate(flops=2 * rows * size * width, bytes_accessed=2 * rows * (size + width) + 4 * size * width, transcendentals=0),
        name="outer_left",
    )(left, right)


def outer_right_kernel(left, right, *refs):
    count = len(refs) // 2 - 1
    sums, out, sums_out, turned = refs[:count], refs[count], refs[count + 1:-1], refs[-1]

    @pl.when(pl.program_id(0) == 0)
    def _():
        turned[...] = left[...].T
        for given, passed in zip(sums, sums_out):
            passed[...] = given[...]

    out[...] = dot(turned[...], right[...])


def outer_by_right(left, right, block, sums):
    rows, size = left.shape
    width = right.shape[1]
    return pl.pallas_call(
        outer_right_kernel,
        out_shape=(jax.ShapeDtypeStruct((size, width), F32),) + tuple(jax.ShapeDtypeStruct(total.shape, F32) for total in sums),
        grid=(width // block,),
        in_specs=[pl.BlockSpec((rows, size), lambda at: (0, 0)), pl.BlockSpec((rows, block), lambda at: (0, at))] + [VMEM] * len(sums),
        out_specs=(pl.BlockSpec((size, block), lambda at: (0, at)),) + (VMEM,) * len(sums),
        scratch_shapes=[pltpu.VMEM((size, rows), BF16)],
        compiler_params=pltpu.CompilerParams(vmem_limit_bytes=LIMIT),
        cost_estimate=pl.CostEstimate(flops=2 * rows * size * width, bytes_accessed=2 * rows * (size + width) + 4 * size * width, transcendentals=0),
        name="outer_right",
    )(left, right, *sums)


def matmul_rows(spec, left, right):
    return jnp.einsum(spec, left, right, preferred_element_type=F32)


def solution(mesh):
    stages = mesh.shape["pp"]
    in_specs = (P("dp"), P("dp"), P(), P(), P(), P()) + (P("pp"),) * 12 + (P(),) * 4
    out_specs = (P("dp"),) * 5 + (P(("dp", "pp")),) * 12 + (P("dp"),) * 4

    def body(patches, labels, w_patch, b_patch, cls_token, pos_embed, *rest):
        ln1_gain, ln1_bias, w_qkv, b_qkv, w_proj, b_proj, ln2_gain, ln2_bias, w_fc1, b_fc1, w_fc2, b_fc2 = (tensor[0] for tensor in rest[:12])
        lnf_gain, lnf_bias, w_head, b_head = rest[12:]
        tokens, width = pos_embed.shape
        heads, head = w_qkv.shape[2:]
        images = labels.size
        inv_count = 1.0 / images
        rows = -(-tokens // 16) * 16
        dims = (stages, images, tokens, heads, head)

        patch_rows = jnp.pad(patches.reshape((images,) + patches.shape[2:]), ((0, 0), (1, rows - tokens), (0, 0)))
        is_patch = lax.broadcasted_iota(jnp.int32, (rows, 1), 0) > 0
        base = jnp.pad(pos_embed, ((0, rows - tokens), (0, 0))).astype(F32) + jnp.where(is_patch, b_patch.astype(F32), cls_token.astype(F32))
        embedded = (matmul_rows("inp,pd->ind", patch_rows, w_patch) + base).astype(BF16)

        line = lambda tensor: tensor.reshape(1, -1)
        wqkv_t = jnp.transpose(w_qkv, (1, 2, 3, 0)).reshape(3 * width, width)
        big = (wqkv_t, w_proj.reshape(width, width), w_fc1, w_fc2)
        vectors = tuple(map(line, (ln1_gain, ln1_bias, b_qkv, b_proj, ln2_gain, ln2_bias, b_fc1, b_fc2)))
        vectors = vectors[:2] + (vectors[2].reshape(3, 1, width),) + vectors[3:]
        x_s, a_s, qkv_s, c_s, h_s, n_s, d_s, g_s, p_s, tops = run_forward(dims, embedded, *big, vectors)

        row = lambda tensor: tensor.reshape(1, -1)
        loss, gtop, g_lnf_gain, g_lnf_bias, g_w_head, g_b_head = run_head(
            inv_count, tops, labels, row(lnf_gain), row(lnf_bias), jnp.transpose(w_head), row(b_head))

        gy_s, gpre_s, gmid_s, gqkv_s, gemb, *sums = run_backward(dims, gtop, *big, vectors[0], vectors[4], x_s, qkv_s, h_s, d_s, p_s)
        flat = lambda array: array.reshape(images * rows, -1)
        g_w_fc1, *sums = outer_by_right(flat(n_s), flat(gpre_s), 4 * LANES, sums)
        g_ln1_gain, g_ln1_bias, g_ln2_gain, g_ln2_bias, g_b_proj, g_b_fc2, g_b_qkv, g_b_fc1 = sums
        g_w_qkv = outer_by_left(flat(gqkv_s), flat(a_s), 3 * LANES).reshape(3, heads, head, width)
        layer_grads = (
            g_ln1_gain, g_ln1_bias, jnp.transpose(g_w_qkv, (3, 0, 1, 2))[None], g_b_qkv.reshape(1, 3, heads, head),
            outer_by_left(flat(c_s), flat(gmid_s), LANES).reshape(1, heads, head, width), g_b_proj,
            g_ln2_gain, g_ln2_bias,
            g_w_fc1[None], g_b_fc1,
            outer_by_left(flat(g_s), flat(gy_s), 4 * LANES)[None], g_b_fc2,
        )
        g_pos_embed = jnp.sum(gemb[:, :tokens].astype(F32), axis=0)
        embed_grads = (
            matmul_rows("tp,td->pd", flat(patch_rows), flat(gemb)),
            jnp.sum(g_pos_embed[1:], axis=0), g_pos_embed[0], g_pos_embed,
        )
        return (loss.reshape(1),) + embed_grads + layer_grads + (g_lnf_gain[0], g_lnf_bias[0], jnp.transpose(g_w_head), g_b_head[0])

    return jax.shard_map(body, mesh=mesh, in_specs=in_specs, out_specs=out_specs, check_vma=False)
```

time: 1080 us -> 940 us (0.87)
  matrix products: 182 us -> 18.8 us
  Pallas kernels: 811 us -> 892 us
  local copies, waits for them, and re-layouts: 51.7 us -> 15 us
  other arithmetic: 22 us -> 8.81 us
    pallas_call x0 -> x5, Pallas kernels: none -> 162 us  [the longest x3 105 us: outer_by_left(): pl.pallas_call(outer_kernel, out_shape=jax.ShapeDtypeStruct((size, width)...]
    dot_general x8 -> x2, matrix products: 180 us -> 18.8 us  [matmul_rows(): return jnp.einsum(spec, left, right, preferred_element_type=F32)]
    pallas_call x1, Pallas kernels: 375 us -> 324 us  [run_forward(): pl.pallas_call(functools.partial(forward_kernel, dims), out_shape=(hbm(wi...]
    dot_general x2 -> x0, local copies, waits for them, and re-layouts: 33.9 us -> none  [matmul_rows(): return jnp.einsum(spec, left, right, preferred_element_type=F32)]
    pallas_call x1, Pallas kernels: 437 us -> 406 us  [run_backward(): pl.pallas_call(functools.partial(backward_kernel, dims), out_shape=(hbm(w...]
    convert_element_type x13 -> x1, other arithmetic: 16.3 us -> 0.69 us  [body(): cls_token.astype(F32)]
where the time goes in v3:
time: 940 us; the launch traced here: 936 us
  Pallas kernels  892 us (95%)
  matrix products  18.8 us (2%)
  local copies, waits for them, and re-layouts  15 us (2%)
    pallas_call x1, Pallas kernels, run_backward(): pl.pallas_call(functools.partial(backward_kernel, dims), out_shape=(hbm(w...  406 us
    pallas_call x1, Pallas kernels, run_forward(): pl.pallas_call(functools.partial(forward_kernel, dims), out_shape=(hbm(wi...  324 us
    pallas_call x3, Pallas kernels, outer_by_left(): pl.pallas_call(outer_kernel, out_shape=jax.ShapeDtypeStruct((size, width)...  105 us
    pallas_call x1, Pallas kernels, outer_by_right(): pl.pallas_call(outer_right_kernel, out_shape=(jax.ShapeDtypeStruct((size,...  49.5 us
    dot_general x2, matrix products, matmul_rows(): return jnp.einsum(spec, left, right, preferred_element_type=F32)  18.8 us

profile of v3, /device:TPU:7, one launch (start us, length us, event | category | flops | bytes accessed | tf_op | source)
XLA Modules:
  0.0 935.6 jit_solution(15141639293416535532)
XLA Ops:
  0.7 1.3 copy.47.labels
  2.0 1.3 reshape.105.b_head
  3.3 1.3 reshape.103.gain
  4.6 1.3 reshape.104.bias
  5.9 0.7 convert_element_type.20
  6.5 0.7 convert_element_type.21
  7.2 1.4 reshape_reshape_squeeze.4.refs_7_
  8.6 2.5 select_add_fusion
  11.1 5.1 copy.45
  16.2 0.0 copy-start.2
  16.2 1.5 copy-done.2
  17.7 9.0 add_convert_fusion.refs_0_
  26.7 324.3 %forward.1 = (bf16[8,272,1408]{2,1,0:T(8,128)(2,1)}, bf16[8,272,1408]{2,1,0:T(8,128)(2,1)}, bf16[8,272,6144]{2,1,0:T(8,128)(2,1)}, bf16[8,272,1408]{2,1,0:T(8,12...) custom-call(bf16[8,272,1408]{2,1,0:T(8,128)(2,1)} %add_convert_fusio, ...), custom_call_target="tpu_custom_call" | custom-call | tf_op jit(solution)/shard_map/forward/pallas_call | solution.py:682
  351.0 7.0 head.1
  358.0 405.9 %backward.1 = (bf16[8,272,1408]{2,1,0:T(8,128)(2,1)}, bf16[8,272,6144]{2,1,0:T(8,128)(2,1)}, bf16[8,272,1408]{2,1,0:T(8,128)(2,1)}, bf16[8,272,4224]{2,1,0:T(8,1...) custom-call(bf16[8,16,1408]{2,1,0:T(8,128)(2,1)} %get-tuple-element., ...), custom_call_target="tpu_custom_call" | custom-call | tf_op jit(solution)/shard_map/backward/pallas_call | solution.py:710
  763.9 1.3 reduce.2
  765.2 1.3 reduce.3
  766.5 0.0 copy-start.1
  766.5 9.9 %convolution_bitcast_fusion = f32[588,1408]{1,0:T(8,128)} fusion(bf16[8,272,1408]{2,1,0:T(8,128)(2,1)} %get-tuple-element.67, bf16[8,256,588]{2,1,0:T(8,128)(2,1)} %bitcast.47), kind=kOutput, calls=%fused_computation.2 | convolution fusion | flops 3603038208 | bytes 11847680 | tf_op jit(solution)/shard_map/tp,td->pd/dot_general | solution.py:822
  776.4 0.0 copy-done.1
  776.4 0.8 convert_reduce_fusion
  777.2 0.0 copy-start
  777.2 0.7 slice_reduce_fusion.1
  777.9 0.4 copy-done
  778.3 0.8 slice_reduce_fusion
  779.1 49.5 %outer_right.1 = (f32[1408,6144]{1,0:T(8,128)}, f32[1,1408]{1,0:T(1,128)}, f32[1,1408]{1,0:T(1,128)}, f32[1,1408]{1,0:T(1,128)}, f32[1,1408]{1,0:T(1,128)}, /*in...) custom-call(bf16[2176,1408]{1,0:T(8,128)(2,1)} %bitcast.53, ...), custom_call_target="tpu_custom_call" | custom-call | flops 37648072704 | bytes 67469312 | tf_op jit(solution)/shard_map/outer_right/pallas_call | solution.py:808
  828.6 0.8 reduce.1
  829.4 0.7 reshape.112
  830.1 17.2 %outer_left.4 = f32[1408,1408]{1,0:T(8,128)} custom-call(bf16[2176,1408]{1,0:T(8,128)(2,1)} %bitcast.52, bf16[2176,1408]{1,0:T(8,128)(2,1)} %bitcast.55), custom_call_target="tpu_custom_call" | custom-call | flops 8627683328 | bytes 20185088 | tf_op jit(solution)/shard_map/outer_left/pallas_call | solution.py:780
  847.3 51.3 %outer_left.5 = f32[6144,1408]{1,0:T(8,128)} custom-call(bf16[2176,6144]{1,0:T(8,128)(2,1)} %bitcast.48, bf16[2176,1408]{1,0:T(8,128)(2,1)} %bitcast.54), custom_call_target="tpu_custom_call" | custom-call | flops 37648072704 | bytes 67469312 | tf_op jit(solution)/shard_map/outer_left/pallas_call | solution.py:780
  898.6 36.8 %outer_left.3 = f32[4224,1408]{1,0:T(8,128)} custom-call(bf16[2176,4224]{1,0:T(8,128)(2,1)} %bitcast.50, bf16[2176,1408]{1,0:T(8,128)(2,1)} %bitcast.51), custom_call_target="tpu_custom_call" | custom-call | flops 25883049984 | bytes 48300032 | tf_op jit(solution)/shard_map/outer_left/pallas_call | solution.py:780
  (1 shorter events, 0.0 us)
Async XLA Ops:
  16.2 1.5 copy-start.2
  766.5 9.9 %copy-start.1 = (bf16[8,272,1408]{2,1,0:T(8,128)(2,1)S(1)}, bf16[8,272,1408]{2,1,0:T(8,128)(2,1)}, u32[]{:S(2)}) copy-start(bf16[8,272,1408]{2,1,0:T(8,128)(2,1)} %get-tuple-element.67) | copy-start | bytes 18382852
  777.2 1.1 copy-start

commit v4 on v3

--- a/solution.py
+++ b/solution.py
@@ -75,20 +75,20 @@
     def emb_copy(image, slot):
         return pltpu.make_async_copy(emb.at[image], xin.at[slot], recv_sem.at[slot])
 
-    qkv_copy(0).start()
-
     @pl.when(is_first)
     def _():
         emb_copy(0, 0).start()
+
+    qkv_copy(0).start()
+
+    @pl.when(is_first)
+    def _():
         emb_copy(1, 1).start()
 
     qkv_copy(1).start()
     proj_copy = pltpu.make_async_copy(wproj, vproj, wsem.at[0])
     fc1_copy = pltpu.make_async_copy(wfc1, vfc1, wsem.at[1])
     fc2_copy = pltpu.make_async_copy(wfc2, vfc2, wsem.at[2])
-    proj_copy.start()
-    fc1_copy.start()
-    fc2_copy.start()
     qkv[...] = jnp.zeros_like(qkv)
     for low, wide in zip(given, (g1, b1, bqkv, bproj, g2, b2, bfc1, bfc2)):
         wide[...] = low[...].astype(F32)
@@ -166,9 +166,15 @@
                 lane = part * (heads * LANES) + at * LANES
                 qkv[:, pl.ds(pl.multiple_of(lane, LANES), head)] = low[:, at * head:(at + 1) * head]
 
-            @pl.when(index + 2 < images * 3)
+            @pl.when(part == 0)
             def _():
                 qkv_copy(index + 2).start()
+
+            @pl.when(index == 0)
+            def _():
+                proj_copy.start()
+                fc1_copy.start()
+                fc2_copy.start()
 
             return carry
 
@@ -210,6 +216,11 @@
             scores = later
         save_c.start()
 
+        @pl.when(image + 1 < images)
+        def _():
+            qkv_copy(image * 3 + 3).start()
+            qkv_copy(image * 3 + 4).start()
+
         @pl.when(image == 0)
         def _():
             proj_copy.wait()
@@ -419,15 +430,21 @@
         top_copy(0, 0).start()
         top_copy(1, 1).start()
 
-    fc2_copy = pltpu.make_async_copy(wfc2, vfc2, wsem.at[2])
-    fc1_copy = pltpu.make_async_copy(wfc1, vfc1, wsem.at[1])
-    proj_copy = pltpu.make_async_copy(wproj, vproj, wsem.at[0])
-    fc2_copy.start()
-    for chunk in range(4):
-        d_load(0, chunk).start()
-    fc1_copy.start()
+    def fc2_copy(chunk):
+        lines = pl.ds(pl.multiple_of(chunk * CHUNK, CHUNK), CHUNK)
+        return pltpu.make_async_copy(wfc2.at[lines], vfc2.at[lines], wsem.at[2, chunk])
+
+    def fc1_copy(chunk):
+        columns = pl.ds(pl.multiple_of(chunk * CHUNK, CHUNK), CHUNK)
+        return pltpu.make_async_copy(wfc1.at[:, columns], vfc1.at[:, columns], wsem.at[1, chunk])
+
+    proj_copy = pltpu.make_async_copy(wproj, vproj, wsem.at[0, 0])
+    for chunk in range(chunks):
+        fc2_copy(chunk).start()
+        if chunk < 4:
+            d_load(0, chunk).start()
+        fc1_copy(chunk).start()
     loads(0)[0].start()
-    loads(0)[2].start()
     proj_copy.start()
     qkv_copy(0, 0).start()
     qkv_copy(0, 1).start()
@@ -456,10 +473,11 @@
 
         save_gy.start()
 
+        load_qkv.start()
+
         @pl.when(image == 0)
         def _():
-            fc2_copy.wait()
-            fc1_copy.wait()
+            fc2_copy(0).wait()
 
         @pl.when(image > 0)
         def _():
@@ -491,6 +509,11 @@
         def mlp_step(chunk, carry):
             d_load(image, chunk - 1).wait()
 
+            @pl.when(image == 0)
+            def _():
+                fc2_copy(chunk).wait()
+                fc1_copy(chunk - 1).wait()
+
             @pl.when(chunk >= 3)
             def _():
                 g_save(image, chunk - 1).wait()
@@ -510,6 +533,11 @@
 
         lax.fori_loop(1, chunks, mlp_step, 0)
         d_load(image, chunks - 1).wait()
+
+        @pl.when(image == 0)
+        def _():
+            fc1_copy(chunks - 1).wait()
+
         g_save(image, chunks - 1).wait()
         g_save(image, chunks - 2).start()
         fc1(chunks - 1, gelu(chunks - 1))
@@ -577,27 +605,14 @@
             query = dot(low, qkv[:, lanes_of(heads + number)], 0, 0).astype(BF16)
             gqkv[:, at:at + head] = query[:, :head]
 
-        def refill(group):
-            if group + 2 < groups:
-                p_load(image, group + 2).start()
-            else:
-                @pl.when(more)
-                def _():
-                    for chunk in range((group + 2 - groups) * 2, (group + 2 - groups) * 2 + 2):
-                        d_load(image + 1, chunk).start()
-
         grad_probs = grad_probs_of(0)
         for number in range(heads):
             later = grad_probs_of(number + 1) if number + 1 < heads else None
             attend(number, grad_probs)
             grad_probs = later
-            if number % GROUP == GROUP - 1:
-                refill(number // GROUP)
+            if number % GROUP == GROUP - 1 and number // GROUP + 2 < groups:
+                p_load(image, number // GROUP + 2).start()
         save_qkv.start()
-
-        @pl.when(more)
-        def _():
-            loads(image + 1)[2].start()
 
         def qkv_part(part, carry):
             for side in range(2):
@@ -617,6 +632,12 @@
 
         acc[...] = jnp.zeros_like(acc)
         lax.fori_loop(0, 3, qkv_part, 0)
+
+        @pl.when(more)
+        def _():
+            for chunk in range(4):
+                d_load(image + 1, chunk).start()
+
         load_x.wait()
 
         @pl.when(image > 0)
@@ -720,7 +741,7 @@
             pltpu.VMEM((rows, 3 * heads * LANES), BF16), pltpu.VMEM((rows, 3 * width), BF16),
             pltpu.VMEM((rows, width), BF16), pltpu.VMEM((1, width), F32), pltpu.VMEM((1, width), F32),
             *(pltpu.VMEM((8, size), F32) for size in sizes),
-            DMA((3,)), DMA((3,)), DMA((2,)), DMA((2,)), DMA((stages,)), DMA(()), DMA((4,)), DMA((3,)), DMA((4,)), DMA((2,)), DMA((2,)),
+            DMA((3, hidden // CHUNK)), DMA((3,)), DMA((2,)), DMA((2,)), DMA((stages,)), DMA(()), DMA((4,)), DMA((3,)), DMA((4,)), DMA((2,)), DMA((2,)),
             pltpu.SemaphoreType.REGULAR],
         compiler_params=pltpu.CompilerParams(collective_id=1, has_side_effects=True, vmem_limit_bytes=LIMIT),
         name="backward",
@@ -729,16 +750,17 @@
 
 def head_kernel(inv_count, tops, labels, gain, bias, w_head, b_head, loss, gtop, g_gain, g_bias, g_w_head, g_b_head):
     images, width = tops.shape
-    wide_gain = gain[...].astype(F32)
-    pooled = layer_norm(tops[...], wide_gain, bias[...].astype(F32))
-    logits = dot(pooled, w_head[...], 1, 1) + b_head[...].astype(F32)
+    line = lambda ref: ref[...].reshape(1, -1).astype(F32)
+    wide_gain = line(gain)
+    pooled = layer_norm(tops[...], wide_gain, line(bias))
+    logits = dot(pooled, w_head[...], 1, 1) + line(b_head)
     shifted = logits - jnp.max(logits, axis=-1, keepdims=True)
     log_probs = shifted - jnp.log(jnp.sum(jnp.exp(shifted), axis=-1, keepdims=True))
     classes = logits.shape[-1]
-    line = lax.broadcasted_iota(jnp.int32, (images, 1), 0)
+    number = lax.broadcasted_iota(jnp.int32, (images, 1), 0)
     label = jnp.zeros((images, 1), jnp.int32)
     for image in range(images):
-        label = jnp.where(line == image, labels[image // labels.shape[1], image % labels.shape[1]], label)
+        label = jnp.where(number == image, labels[image % labels.shape[0], image // labels.shape[0]], label)
     chosen = (lax.broadcasted_iota(jnp.int32, logits.shape, 1) == label).astype(F32)
     target = (1.0 - SMOOTH) * chosen + SMOOTH / classes
     parts = jnp.sum(target * log_probs, axis=-1, keepdims=True)
@@ -746,11 +768,11 @@
     grad_logits = (jnp.exp(log_probs) - target) * inv_count
     low = grad_logits.astype(BF16)
     g_w_head[...] = dot(low, pooled, 0, 0)
-    g_b_head[...] = jnp.sum(grad_logits, axis=0, keepdims=True)
+    g_b_head[...] = jnp.sum(grad_logits, axis=0)
     grad = dot(low, w_head[...]).astype(BF16).astype(F32)
     grad_in, by_unit = norm_backward(grad, tops[...], wide_gain)
-    g_gain[...] = jnp.sum(by_unit, axis=0, keepdims=True)
-    g_bias[...] = jnp.sum(grad, axis=0, keepdims=True)
+    g_gain[...] = jnp.sum(by_unit, axis=0)
+    g_bias[...] = jnp.sum(grad, axis=0)
     gtop[...] = jnp.zeros_like(gtop)
     for image in range(images):
         gtop[image, 0:1, :] = grad_in[image:image + 1].astype(BF16)
@@ -762,7 +784,7 @@
     shape = lambda *dims, dtype=F32: jax.ShapeDtypeStruct(dims, dtype)
     return pl.pallas_call(
         functools.partial(head_kernel, inv_count),
-        out_shape=(shape(1, 1), shape(images, 16, width, dtype=BF16), shape(1, width), shape(1, width), shape(classes, width), shape(1, classes)),
+        out_shape=(shape(1, 1), shape(images, 16, width, dtype=BF16), shape(width), shape(width), shape(classes, width), shape(classes)),
         in_specs=[VMEM, pl.BlockSpec(memory_space=pltpu.SMEM)] + [VMEM] * 4,
         out_specs=(VMEM,) * 6,
         compiler_params=pltpu.CompilerParams(vmem_limit_bytes=LIMIT),
@@ -770,52 +792,166 @@
     )(tops, labels, gain, bias, w_head, b_head)
 
 
-def outer_kernel(left, right, out):
-    out[...] = dot(left[...], right[...], 0, 0)
-
-
-def outer_by_left(left, right, block):
-    rows, size = left.shape
-    width = right.shape[1]
+def weight_kernel(*refs):
+    count = (len(refs) - 15 - 11) // 2
+    fc2_l, qkv_l, proj_l, patch_l, fc2_r, qkv_r, proj_r, patch_r, fc1_l, fc1_r = refs[:10]
+    sums = refs[10:10 + count]
+    fc2_o, qkv_o, proj_o, patch_o, fc1_o = refs[10 + count:15 + count]
+    sums_out = refs[15 + count:15 + 2 * count]
+    lhs, rhs, out, turned, block, wide, lsem, rsem, osem, bsem, wsem = refs[15 + 2 * count:]
+    width = rhs.shape[2]
+    size, wide_size = lhs.shape[2], block.shape[2]
+    tail = width % size
+    patches = patch_l.shape[1] // size + 1
+    ends = [fc2_l.shape[1] // size]
+    ends.append(ends[0] + qkv_l.shape[1] // size)
+    ends.append(ends[1] + width // size + 1)
+    ends.append(ends[2] + patches)
+    starts = [0] + ends[:3]
+    steps = ends[3]
+    wide_steps = fc1_r.shape[1] // wide_size
+
+    def lines(at, unit):
+        return pl.ds(pl.multiple_of(at * unit, LANES), unit)
+
+    def left_copy(step, act):
+        slot = lax.rem(step, 2)
+        for product, source in enumerate((fc2_l, qkv_l, proj_l, patch_l)):
+            full = source.shape[1] // size
+            first = starts[product]
+
+            @pl.when(jnp.logical_and(step >= first, step < first + full))
+            def _():
+                act(pltpu.make_async_copy(source.at[:, lines(step - first, size)], lhs.at[slot], lsem.at[slot]))
+
+            if source.shape[1] % size:
+                @pl.when(step == first + full)
+                def _():
+                    act(pltpu.make_async_copy(source.at[:, pl.ds(full * size, tail)], lhs.at[slot, :, pl.ds(0, tail)], lsem.at[slot]))
+
+    def out_copy(step, act):
+        slot = lax.rem(step, 2)
+        for product, target in enumerate((fc2_o, qkv_o, proj_o)):
+            full = target.shape[0] // size
+            first = starts[product]
+
+            @pl.when(jnp.logical_and(step >= first, step < first + full))
+            def _():
+                act(pltpu.make_async_copy(out.at[slot], target.at[lines(step - first, size)], osem.at[slot]))
+
+            if target.shape[0] % size:
+                @pl.when(step == first + full)
+                def _():
+                    act(pltpu.make_async_copy(out.at[slot, pl.ds(0, tail)], target.at[pl.ds(full * size, tail)], osem.at[slot]))
+
+    def right_copy(product):
+        source = (fc2_r, qkv_r, proj_r, patch_r, fc1_l)[product]
+        return pltpu.make_async_copy(source, rhs.at[product % 2], rsem.at[product % 2])
+
+    def block_copy(step):
+        slot = lax.rem(step, 2)
+        return pltpu.make_async_copy(fc1_r.at[:, lines(step, wide_size)], block.at[slot], bsem.at[slot])
+
+    def wide_copy(step):
+        slot = lax.rem(step, 2)
+        return pltpu.make_async_copy(wide.at[slot], fc1_o.at[:, lines(step, wide_size)], wsem.at[slot])
+
+    start = lambda copy: copy.start()
+    wait = lambda copy: copy.wait()
+    left_copy(0, start)
+    right_copy(0).start()
+    right_copy(1).start()
+    for given, passed in zip(sums, sums_out):
+        passed[...] = given[...]
+
+    def one_step(step, carry):
+        slot = lax.rem(step, 2)
+
+        @pl.when(step >= 1)
+        def _():
+            out_copy(step - 1, start)
+
+        @pl.when(step >= 2)
+        def _():
+            out_copy(step - 2, wait)
+
+        @pl.when(step + 1 < steps)
+        def _():
+            left_copy(step + 1, start)
+
+        for product, first in enumerate(starts):
+            @pl.when(step == first)
+            def _(product=product):
+                right_copy(product).wait()
+                if product >= 1:
+                    right_copy(product + 1).start()
+
+        @pl.when(step == steps - 1)
+        def _():
+            block_copy(0).start()
+
+        left_copy(step, wait)
+        which = lax.rem(sum((step >= end).astype(jnp.int32) for end in ends[:3]), 2)
+        out[slot] = dot(lhs[slot], rhs[which], 0, 0)
+        for at in range(patches):
+            count = min(size, patch_o.shape[0] - at * size)
+
+            @pl.when(step == starts[3] + at)
+            def _():
+                patch_o[at * size:at * size + count, :] = out[slot, :count, :]
+
+        return carry
+
+    lax.fori_loop(0, steps, one_step, 0)
+    right_copy(4).wait()
+    turned[...] = rhs[0].T
+
+    def wide_step(step, carry):
+        slot = lax.rem(step, 2)
+
+        @pl.when(step >= 1)
+        def _():
+            wide_copy(step - 1).start()
+
+        @pl.when(step >= 2)
+        def _():
+            wide_copy(step - 2).wait()
+
+        @pl.when(step + 1 < wide_steps)
+        def _():
+            block_copy(step + 1).start()
+
+        block_copy(step).wait()
+        wide[slot] = dot(turned[...], block[slot])
+        return carry
+
+    lax.fori_loop(0, wide_steps, wide_step, 0)
+    wide_copy(wide_steps - 1).start()
+    wide_copy(wide_steps - 2).wait()
+    wide_copy(wide_steps - 1).wait()
+
+
+def run_weights(lefts, rights, patch_size, sums):
+    fc2_l, qkv_l, proj_l, patch_l, fc1_l = lefts
+    fc2_r, qkv_r, proj_r, patch_r, fc1_r = rights
+    rows, width = fc2_r.shape
+    size, wide_size = 3 * LANES, 4 * LANES
+    shapes = [(left.shape[1], right.shape[1]) for left, right in zip(lefts, rights)]
+    shapes[3] = (patch_size, width)
+    flops = sum(2 * rows * a * b for a, b in shapes)
     return pl.pallas_call(
-        outer_kernel,
-        out_shape=jax.ShapeDtypeStruct((size, width), F32),
-        grid=(size // block,),
-        in_specs=[pl.BlockSpec((rows, block), lambda at: (0, at)), pl.BlockSpec((rows, width), lambda at: (0, 0))],
-        out_specs=pl.BlockSpec((block, width), lambda at: (at, 0)),
+        weight_kernel,
+        out_shape=tuple(jax.ShapeDtypeStruct(shape, F32) for shape in shapes) + tuple(jax.ShapeDtypeStruct(total.shape, F32) for total in sums),
+        in_specs=[ANY] * 10 + [VMEM] * len(sums),
+        out_specs=(ANY,) * 3 + (VMEM, ANY) + (VMEM,) * len(sums),
+        scratch_shapes=[
+            pltpu.VMEM((2, rows, size), BF16), pltpu.VMEM((2, rows, width), BF16), pltpu.VMEM((2, size, width), F32),
+            pltpu.VMEM((width, rows), BF16), pltpu.VMEM((2, rows, wide_size), BF16), pltpu.VMEM((2, width, wide_size), F32),
+            DMA((2,)), DMA((2,)), DMA((2,)), DMA((2,)), DMA((2,))],
         compiler_params=pltpu.CompilerParams(vmem_limit_bytes=LIMIT),
-        cost_estimate=pl.CostEstimate(flops=2 * rows * size * width, bytes_accessed=2 * rows * (size + width) + 4 * size * width, transcendentals=0),
-        name="outer_left",
-    )(left, right)
-
-
-def outer_right_kernel(left, right, *refs):
-    count = len(refs) // 2 - 1
-    sums, out, sums_out, turned = refs[:count], refs[count], refs[count + 1:-1], refs[-1]
-
-    @pl.when(pl.program_id(0) == 0)
-    def _():
-        turned[...] = left[...].T
-        for given, passed in zip(sums, sums_out):
-            passed[...] = given[...]
-
-    out[...] = dot(turned[...], right[...])
-
-
-def outer_by_right(left, right, block, sums):
-    rows, size = left.shape
-    width = right.shape[1]
-    return pl.pallas_call(
-        outer_right_kernel,
-        out_shape=(jax.ShapeDtypeStruct((size, width), F32),) + tuple(jax.ShapeDtypeStruct(total.shape, F32) for total in sums),
-        grid=(width // block,),
-        in_specs=[pl.BlockSpec((rows, size), lambda at: (0, 0)), pl.BlockSpec((rows, block), lambda at: (0, at))] + [VMEM] * len(sums),
-        out_specs=(pl.BlockSpec((size, block), lambda at: (0, at)),) + (VMEM,) * len(sums),
-        scratch_shapes=[pltpu.VMEM((size, rows), BF16)],
-        compiler_params=pltpu.CompilerParams(vmem_limit_bytes=LIMIT),
-        cost_estimate=pl.CostEstimate(flops=2 * rows * size * width, bytes_accessed=2 * rows * (size + width) + 4 * size * width, transcendentals=0),
-        name="outer_right",
-    )(left, right, *sums)
+        cost_estimate=pl.CostEstimate(flops=flops, bytes_accessed=4 * sum(a * b for a, b in shapes), transcendentals=0),
+        name="weights",
+    )(fc2_l, qkv_l, proj_l, patch_l, fc2_r, qkv_r, proj_r, patch_r, fc1_l, fc1_r, *sums)
 
 
 def matmul_rows(spec, left, right):
@@ -837,10 +973,13 @@
         rows = -(-tokens // 16) * 16
         dims = (stages, images, tokens, heads, head)
 
-        patch_rows = jnp.pad(patches.reshape((images,) + patches.shape[2:]), ((0, 0), (1, rows - tokens), (0, 0)))
+        patch_size = patches.shape[-1]
+        spare = -patch_size % LANES
+        patch_rows = jnp.pad(patches.reshape((images,) + patches.shape[2:]), ((0, 0), (1, rows - tokens), (0, spare)))
+        w_embed = jnp.pad(w_patch, ((0, spare), (0, 0)))
         is_patch = lax.broadcasted_iota(jnp.int32, (rows, 1), 0) > 0
         base = jnp.pad(pos_embed, ((0, rows - tokens), (0, 0))).astype(F32) + jnp.where(is_patch, b_patch.astype(F32), cls_token.astype(F32))
-        embedded = (matmul_rows("inp,pd->ind", patch_rows, w_patch) + base).astype(BF16)
+        embedded = (matmul_rows("inp,pd->ind", patch_rows, w_embed) + base).astype(BF16)
 
         line = lambda tensor: tensor.reshape(1, -1)
         wqkv_t = jnp.transpose(w_qkv, (1, 2, 3, 0)).reshape(3 * width, width)
@@ -849,27 +988,23 @@
         vectors = vectors[:2] + (vectors[2].reshape(3, 1, width),) + vectors[3:]
         x_s, a_s, qkv_s, c_s, h_s, n_s, d_s, g_s, p_s, tops = run_forward(dims, embedded, *big, vectors)
 
-        row = lambda tensor: tensor.reshape(1, -1)
         loss, gtop, g_lnf_gain, g_lnf_bias, g_w_head, g_b_head = run_head(
-            inv_count, tops, labels, row(lnf_gain), row(lnf_bias), jnp.transpose(w_head), row(b_head))
+            inv_count, tops, jnp.transpose(labels), lnf_gain, lnf_bias, jnp.transpose(w_head), b_head)
 
         gy_s, gpre_s, gmid_s, gqkv_s, gemb, *sums = run_backward(dims, gtop, *big, vectors[0], vectors[4], x_s, qkv_s, h_s, d_s, p_s)
         flat = lambda array: array.reshape(images * rows, -1)
-        g_w_fc1, *sums = outer_by_right(flat(n_s), flat(gpre_s), 4 * LANES, sums)
+        g_w_fc2, g_w_qkv, g_w_proj, g_w_patch, g_w_fc1, *sums = run_weights(
+            tuple(map(flat, (g_s, gqkv_s, c_s, patch_rows, n_s))), tuple(map(flat, (gy_s, a_s, gmid_s, gemb, gpre_s))), patch_size, sums)
         g_ln1_gain, g_ln1_bias, g_ln2_gain, g_ln2_bias, g_b_proj, g_b_fc2, g_b_qkv, g_b_fc1 = sums
-        g_w_qkv = outer_by_left(flat(gqkv_s), flat(a_s), 3 * LANES).reshape(3, heads, head, width)
+        g_w_qkv = jnp.transpose(g_w_qkv.reshape(3, heads, head, width), (3, 0, 1, 2))[None]
         layer_grads = (
-            g_ln1_gain, g_ln1_bias, jnp.transpose(g_w_qkv, (3, 0, 1, 2))[None], g_b_qkv.reshape(1, 3, heads, head),
-            outer_by_left(flat(c_s), flat(gmid_s), LANES).reshape(1, heads, head, width), g_b_proj,
-            g_ln2_gain, g_ln2_bias,
-            g_w_fc1[None], g_b_fc1,
-            outer_by_left(flat(g_s), flat(gy_s), 4 * LANES)[None], g_b_fc2,
+            g_ln1_gain, g_ln1_bias, g_w_qkv, g_b_qkv.reshape(1, 3, heads, head), g_w_proj.reshape(1, heads, head, width), g_b_proj,
+            g_ln2_gain, g_ln2_bias, g_w_fc1[None], g_b_fc1, g_w_fc2[None], g_b_fc2,
         )
         g_pos_embed = jnp.sum(gemb[:, :tokens].astype(F32), axis=0)
         embed_grads = (
-            matmul_rows("tp,td->pd", flat(patch_rows), flat(gemb)),
-            jnp.sum(g_pos_embed[1:], axis=0), g_pos_embed[0], g_pos_embed,
+            g_w_patch, jnp.sum(g_pos_embed[1:], axis=0), g_pos_embed[0], g_pos_embed,
         )
-        return (loss.reshape(1),) + embed_grads + layer_grads + (g_lnf_gain[0], g_lnf_bias[0], jnp.transpose(g_w_head), g_b_head[0])
+        return (loss.reshape(1),) + embed_grads + layer_grads + (g_lnf_gain, g_lnf_bias, jnp.transpose(g_w_head), g_b_head)
 
     return jax.shard_map(body, mesh=mesh, in_specs=in_specs, out_specs=out_specs, check_vma=False)

time: 940 us -> 932 us (level)
  matrix products: 18.8 us -> 8.61 us
    pallas_call x1, Pallas kernels: 324 us -> 356 us  [run_forward(): pl.pallas_call(functools.partial(forward_kernel, dims), out_shape=(hbm(wi...]
    pallas_call x1, Pallas kernels: 406 us -> 388 us  [run_backward(): pl.pallas_call(functools.partial(backward_kernel, dims), out_shape=(hbm(w...]
    dot_general x2 -> x1, matrix products: 18.8 us -> 8.61 us  [matmul_rows(): return jnp.einsum(spec, left, right, preferred_element_type=F32)]
    pallas_call x4 -> x1, Pallas kernels: 155 us -> 150 us  [run_weights(): pl.pallas_call(weight_kernel, out_shape=tuple((jax.ShapeDtypeStruct(shape...]
where the time goes in v4:
time: 932 us; the launch traced here: 930 us
  Pallas kernels  901 us (97%)
  local copies, waits for them, and re-layouts  11.2 us (1%)
    pallas_call x1, Pallas kernels, run_backward(): pl.pallas_call(functools.partial(backward_kernel, dims), out_shape=(hbm(w...  388 us
    pallas_call x1, Pallas kernels, run_forward(): pl.pallas_call(functools.partial(forward_kernel, dims), out_shape=(hbm(wi...  356 us
    pallas_call x1, Pallas kernels, run_weights(): pl.pallas_call(weight_kernel, out_shape=tuple((jax.ShapeDtypeStruct(shape...  150 us

profile of v4, /device:TPU:7, one launch (start us, length us, event | category | flops | bytes accessed | tf_op | source)
XLA Modules:
  0.0 930.2 jit_solution(2261835583980385750)
XLA Ops:
  0.7 5.1 copy.44
  5.8 0.0 copy-start
  5.8 0.7 convert_element_type.22
  6.5 0.7 convert_element_type.23
  7.2 1.3 select_add_fusion
  8.6 0.0 copy-start.2
  8.6 8.6 add_convert_fusion.refs_0_
  17.2 0.0 copy-done
  17.2 0.0 copy-done.2
  17.2 0.7 reshape_reshape_squeeze.4.refs_7_
  17.9 356.1 %forward.1 = (bf16[8,272,1408]{2,1,0:T(8,128)(2,1)}, bf16[8,272,1408]{2,1,0:T(8,128)(2,1)}, bf16[8,272,6144]{2,1,0:T(8,128)(2,1)}, bf16[8,272,1408]{2,1,0:T(8,12...) custom-call(bf16[8,272,1408]{2,1,0:T(8,128)(2,1)} %add_convert_fusio, ...), custom_call_target="tpu_custom_call" | custom-call | tf_op jit(solution)/shard_map/forward/pallas_call | solution.py:703
  374.1 7.0 head.1
  381.0 388.3 %backward.1 = (bf16[8,272,1408]{2,1,0:T(8,128)(2,1)}, bf16[8,272,6144]{2,1,0:T(8,128)(2,1)}, bf16[8,272,1408]{2,1,0:T(8,128)(2,1)}, bf16[8,272,4224]{2,1,0:T(8,1...) custom-call(bf16[8,16,1408]{2,1,0:T(8,128)(2,1)} %get-tuple-element., ...), custom_call_target="tpu_custom_call" | custom-call | tf_op jit(solution)/shard_map/backward/pallas_call | solution.py:731
  769.3 4.1 pad.12
  773.4 150.0 %weights.1 = (f32[6144,1408]{1,0:T(8,128)}, f32[4224,1408]{1,0:T(8,128)}, f32[1408,1408]{1,0:T(8,128)}, f32[588,1408]{1,0:T(8,128)}, f32[1408,6144]{1,0:T(8,128)...) custom-call(bf16[2176,6144]{1,0:T(8,128)(2,1)} %bitcast.50, ...), custom_call_target="tpu_custom_call" | custom-call | flops 113409916928 | bytes 104237056 | tf_op jit(solution)/shard_map/weights/pallas_call | solution.py:942
  923.4 0.8 reduce.1
  924.2 0.7 reshape.110
  924.9 3.7 convert_reduce_fusion
  928.6 0.0 copy-start.1
  928.6 0.9 slice_reduce_fusion
  929.5 0.6 slice_reduce_fusion.1
  930.2 0.0 copy-done.1
  (1 shorter events, 0.0 us)
Async XLA Ops:
  5.8 11.4 %copy-start = (bf16[4,2,256,588]{3,2,1,0:T(8,128)(2,1)}, bf16[4,2,256,588]{3,2,1,0:T(8,128)(2,1)S(1)}, u32[]{:S(2)}) copy-start(bf16[4,2,256,588]{3,2,1,0:T(8,128)(2,1)S(1)} %copy.44) | copy-start | bytes 7225348
  8.6 8.6 copy-start.2
  928.6 1.6 copy-start.1

commit v5 on v4

--- a/solution.py
+++ b/solution.py
@@ -17,12 +17,22 @@
 CHUNK = 2 * HALF
 GROUP = 4
 BLOCK = 136
+DOWN = {"axis": 0, "keepdims": True}
+ACROSS = {"axis": -1, "keepdims": True}
+
+
+def flip(index):
+    return lax.rem(index, 2)
+
+
+def third(index):
+    return lax.rem(index, 3)
 
 
 def layer_norm(hidden, gain, bias):
     values = hidden.astype(F32)
-    centered = values - jnp.mean(values, axis=-1, keepdims=True)
-    variance = jnp.mean(jnp.square(centered), axis=-1, keepdims=True)
+    centered = values - jnp.mean(values, **ACROSS)
+    variance = jnp.mean(jnp.square(centered), **ACROSS)
     return (centered * lax.rsqrt(variance + EPS) * gain + bias).astype(BF16)
 
 
@@ -48,8 +58,20 @@
 def everyone(stage, stages):
     barrier = pltpu.get_barrier_semaphore()
     for hop in range(1, stages):
-        pl.semaphore_signal(barrier, inc=1, device_id={"pp": lax.rem(stage + hop, stages)}, device_id_type=MESH)
+        pl.semaphore_signal(barrier, device_id={"pp": lax.rem(stage + hop, stages)}, device_id_type=MESH)
     pl.semaphore_wait(barrier, stages - 1)
+
+
+def weight_copies(wproj, wfc1, wfc2, vproj, vfc1, vfc2, sems, turned):
+    def of_chunk(source, target, which, by_lines):
+        def copy(chunk):
+            span = pl.ds(pl.multiple_of(chunk * CHUNK, CHUNK), CHUNK)
+            part = span if by_lines else (slice(None), span)
+            return pltpu.make_async_copy(source.at[part], target.at[part], sems.at[which, chunk])
+        return copy
+
+    proj = pltpu.make_async_copy(wproj, vproj, sems.at[0, 0])
+    return proj, of_chunk(wfc1, vfc1, 1, turned), of_chunk(wfc2, vfc2, 2, not turned)
 
 
 def forward_kernel(dims, *refs):
@@ -68,8 +90,8 @@
 
 
     def qkv_copy(index):
-        slot = lax.rem(index, 2)
-        lines = pl.ds(pl.multiple_of(lax.rem(index, 3) * width, 128), width)
+        slot = flip(index)
+        lines = pl.ds(pl.multiple_of(third(index) * width, 128), width)
         return pltpu.make_async_copy(wqkv.at[lines], vqkv.at[slot], qsem.at[slot])
 
     def emb_copy(image, slot):
@@ -86,12 +108,21 @@
         emb_copy(1, 1).start()
 
     qkv_copy(1).start()
-    proj_copy = pltpu.make_async_copy(wproj, vproj, wsem.at[0])
-    fc1_copy = pltpu.make_async_copy(wfc1, vfc1, wsem.at[1])
-    fc2_copy = pltpu.make_async_copy(wfc2, vfc2, wsem.at[2])
-    qkv[...] = jnp.zeros_like(qkv)
+    proj_copy, fc1_copy, fc2_copy = weight_copies(wproj, wfc1, wfc2, vproj, vfc1, vfc2, wsem, False)
+
+    def load_rest():
+        proj_copy.start()
+        for chunk in range(chunks):
+            fc1_copy(chunk).start()
+            fc2_copy(chunk).start()
+
+    @pl.when(jnp.logical_not(is_first))
+    def _():
+        load_rest()
+
+    qkv[:] = jnp.zeros_like(qkv)
     for low, wide in zip(given, (g1, b1, bqkv, bproj, g2, b2, bfc1, bfc2)):
-        wide[...] = low[...].astype(F32)
+        wide[:] = low[:].astype(F32)
     everyone(stage, stages)
 
     def saves(image, slot):
@@ -100,7 +131,7 @@
 
     class u_save:
         def __init__(self, image, chunk):
-            slot = lax.rem(chunk, 3)
+            slot = third(chunk)
             self.copies = [
                 pltpu.make_async_copy(ubuf.at[slot, :, pl.ds(side * HALF, HALF)], d_s.at[image, chunk * 2 + side], usem.at[slot, side])
                 for side in range(2)]
@@ -114,7 +145,7 @@
                 copy.wait()
 
     def g_save(image, chunk):
-        slot = lax.rem(chunk, 2)
+        slot = flip(chunk)
         return pltpu.make_async_copy(gbuf.at[slot], g_s.at[image, :, pl.ds(pl.multiple_of(chunk * CHUNK, CHUNK), CHUNK)], gsem.at[slot])
 
     def p_save(image, group):
@@ -142,7 +173,7 @@
                 top_copy(image, other).wait_send()
 
     def one_image(image, carry):
-        slot = lax.rem(image, 2)
+        slot = flip(image)
         save_x, save_a, save_qkv, save_c, save_h, save_n = saves(image, slot)
         emb_copy(image, slot).wait()
         save_x.start()
@@ -153,7 +184,7 @@
             save_qkv.wait()
 
         def norm1(lines):
-            act[lines, :] = layer_norm(xin[slot, lines, :], g1[...], b1[...])
+            act[lines, :] = layer_norm(xin[slot, lines, :], g1[:], b1[:])
 
         by_rows(rows, norm1)
         save_a.start()
@@ -161,7 +192,7 @@
         def qkv_part(part, carry):
             index = image * 3 + part
             qkv_copy(index).wait()
-            low = (dot(act[...], vqkv[lax.rem(index, 2)], 1, 1) + bqkv[part]).astype(BF16)
+            low = (dot(act[:], vqkv[flip(index)], 1, 1) + bqkv[part]).astype(BF16)
             for at in range(heads):
                 lane = part * (heads * LANES) + at * LANES
                 qkv[:, pl.ds(pl.multiple_of(lane, LANES), head)] = low[:, at * head:(at + 1) * head]
@@ -170,11 +201,9 @@
             def _():
                 qkv_copy(index + 2).start()
 
-            @pl.when(index == 0)
+            @pl.when(jnp.logical_and(is_first, index == 0))
             def _():
-                proj_copy.start()
-                fc1_copy.start()
-                fc2_copy.start()
+                load_rest()
 
             return carry
 
@@ -198,11 +227,11 @@
                 p_save(image, group).wait()
             v = qkv[:, (2 * heads + number) * LANES:(2 * heads + number + 1) * LANES]
             top, tail = scores[:tokens - 1], scores[tokens - 1:]
-            most = jnp.maximum(jnp.max(top, axis=0, keepdims=True), tail[:1])
+            most = jnp.maximum(jnp.max(top, **DOWN), tail[:1])
             top = jnp.exp2((top - most) * scale2)
             real = lax.broadcasted_iota(jnp.int32, tail.shape, 0) < 1
             tail = jnp.where(real, jnp.exp2(jnp.minimum(tail - most, 0.0) * scale2), 0.0)
-            inv = 1.0 / (jnp.sum(top, axis=0, keepdims=True) + jnp.sum(tail, axis=0, keepdims=True))
+            inv = 1.0 / (jnp.sum(top, **DOWN) + jnp.sum(tail, **DOWN))
             probs = jnp.concatenate([top, tail], axis=0) * inv
             pbuf[group % 2, inner, :, :rows] = probs
             act[:, number * head:(number + 1) * head] = dot(probs.astype(BF16), v, 0, 0).astype(BF16)[:, :head]
@@ -229,7 +258,7 @@
         def _():
             wait_sent(image)
 
-        mid[...] = (dot(act[...], vproj[...]) + bproj[...] + xin[slot].astype(F32)).astype(BF16)
+        mid[:] = (dot(act[:], vproj[:]) + bproj[:] + xin[slot].astype(F32)).astype(BF16)
         save_h.start()
         save_x.wait()
 
@@ -239,22 +268,21 @@
 
         @pl.when(jnp.logical_and(stage > 0, image + 2 < images))
         def _():
-            pl.semaphore_signal(free_sem, inc=1, device_id={"pp": lax.rem(stage + stages - 1, stages)}, device_id_type=MESH)
+            pl.semaphore_signal(free_sem, device_id={"pp": lax.rem(stage + stages - 1, stages)}, device_id_type=MESH)
 
         save_c.wait()
 
         def norm2(lines):
             hidden = mid[lines, :]
-            act[lines, :] = layer_norm(hidden, g2[...], b2[...])
-            yacc[lines, :] = hidden.astype(F32) + bfc2[...]
+            act[lines, :] = layer_norm(hidden, g2[:], b2[:])
+            yacc[lines, :] = hidden.astype(F32) + bfc2[:]
 
         by_rows(rows, norm2)
         save_n.start()
 
         @pl.when(image == 0)
         def _():
-            fc1_copy.wait()
-            fc2_copy.wait()
+            fc1_copy(0).wait()
 
         @pl.when(image > 0)
         def _():
@@ -265,10 +293,10 @@
 
         def fc1(chunk):
             columns = pl.ds(pl.multiple_of(chunk * CHUNK, CHUNK), CHUNK)
-            ubuf[lax.rem(chunk, 3)] = dot(act[...], vfc1[:, columns]) + bfc1[:, columns]
+            ubuf[third(chunk)] = dot(act[:], vfc1[:, columns]) + bfc1[:, columns]
 
         def gelu(chunk):
-            slot3, slot2 = lax.rem(chunk, 3), lax.rem(chunk, 2)
+            slot3, slot2 = third(chunk), flip(chunk)
             pre = ubuf[slot3]
             cdf = 0.5 + 0.5 * lax.erf(pre * (0.5 ** 0.5))
             pdf = jnp.exp2(pre * pre * (-0.5 / math.log(2.0))) * ((2.0 * math.pi) ** -0.5)
@@ -278,7 +306,7 @@
             return activ
 
         def fc2(chunk, activ):
-            yacc[...] += dot(activ, vfc2[pl.ds(pl.multiple_of(chunk * CHUNK, CHUNK), CHUNK), :])
+            yacc[:] += dot(activ, vfc2[pl.ds(pl.multiple_of(chunk * CHUNK, CHUNK), CHUNK), :])
 
         fc1(0)
 
@@ -288,6 +316,11 @@
                 u_save(image, chunk).wait()
                 g_save(image, chunk - 1).wait()
 
+            @pl.when(image == 0)
+            def _():
+                fc1_copy(chunk).wait()
+                fc2_copy(chunk - 1).wait()
+
             @pl.when(chunk >= 2)
             def _():
                 u_save(image, chunk - 2).start()
@@ -299,6 +332,11 @@
             return carry
 
         lax.fori_loop(1, chunks, mlp_step, 0)
+
+        @pl.when(image == 0)
+        def _():
+            fc2_copy(chunks - 1).wait()
+
         g_save(image, chunks - 1).wait()
         u_save(image, chunks - 2).start()
         g_save(image, chunks - 2).start()
@@ -307,7 +345,7 @@
         g_save(image, chunks - 1).start()
 
         save_h.wait()
-        mid[...] = yacc[...].astype(BF16)
+        mid[:] = yacc[:].astype(BF16)
 
         @pl.when(jnp.logical_and(jnp.logical_not(is_last), image >= 2))
         def _():
@@ -346,11 +384,11 @@
 
 def norm_backward(grad, hidden, gain):
     values = hidden.astype(F32)
-    centered = values - jnp.mean(values, axis=-1, keepdims=True)
-    inv = lax.rsqrt(jnp.mean(jnp.square(centered), axis=-1, keepdims=True) + EPS)
+    centered = values - jnp.mean(values, **ACROSS)
+    inv = lax.rsqrt(jnp.mean(jnp.square(centered), **ACROSS) + EPS)
     unit = centered * inv
     scaled = grad * gain
-    grad_in = inv * (scaled - jnp.mean(scaled, axis=-1, keepdims=True) - unit * jnp.mean(scaled * unit, axis=-1, keepdims=True))
+    grad_in = inv * (scaled - jnp.mean(scaled, **ACROSS) - unit * jnp.mean(scaled * unit, **ACROSS))
     return grad_in, grad * unit
 
 
@@ -362,7 +400,7 @@
      wsem, qsem, recv_sem, top_sem, send_sem, emb_sem, save_sem, load_sem, dsem, gsem, psem, free_sem) = refs
     stages, images, tokens, heads, head = dims
     rows, width = gmid.shape
-    chunks = vfc1.shape[1] // CHUNK
+    chunks = vfc2.shape[1] // CHUNK
     groups = heads // GROUP
     stage = lax.axis_index("pp")
     is_first = stage == 0
@@ -372,9 +410,9 @@
     pieces = ((0, vqkv.shape[1]), (vqkv.shape[1], width - vqkv.shape[1]))
 
     def qkv_copy(part, side):
-        slot = lax.rem(part * 2 + side, 3)
+        slot = third(part * 2 + side)
         at, size = pieces[side]
-        lines = pl.ds(pl.multiple_of(lax.rem(part, 3) * width + at, 128), size)
+        lines = pl.ds(pl.multiple_of(third(part) * width + at, 128), size)
         return pltpu.make_async_copy(wqkv.at[lines], vqkv.at[slot, pl.ds(0, size)], qsem.at[slot])
 
     def top_copy(image, slot):
@@ -385,7 +423,7 @@
         return pltpu.make_async_copy(d_s.at[image, pl.ds(chunk * 2, 2)], shared.at[pl.ds(slot * 2, 2)], dsem.at[slot])
 
     def g_save(image, chunk):
-        slot = lax.rem(chunk, 2)
+        slot = flip(chunk)
         return pltpu.make_async_copy(gbuf.at[slot], gpre_s.at[image, :, pl.ds(pl.multiple_of(chunk * CHUNK, CHUNK), CHUNK)], gsem.at[slot])
 
     def p_load(image, group):
@@ -426,19 +464,11 @@
 
     @pl.when(is_last)
     def _():
-        gin[...] = jnp.zeros_like(gin)
+        gin[:] = jnp.zeros_like(gin)
         top_copy(0, 0).start()
         top_copy(1, 1).start()
 
-    def fc2_copy(chunk):
-        lines = pl.ds(pl.multiple_of(chunk * CHUNK, CHUNK), CHUNK)
-        return pltpu.make_async_copy(wfc2.at[lines], vfc2.at[lines], wsem.at[2, chunk])
-
-    def fc1_copy(chunk):
-        columns = pl.ds(pl.multiple_of(chunk * CHUNK, CHUNK), CHUNK)
-        return pltpu.make_async_copy(wfc1.at[:, columns], vfc1.at[:, columns], wsem.at[1, chunk])
-
-    proj_copy = pltpu.make_async_copy(wproj, vproj, wsem.at[0, 0])
+    proj_copy, fc1_copy, fc2_copy = weight_copies(wproj, wfc1, wfc2, vproj, vfc1, vfc2, wsem, True)
     for chunk in range(chunks):
         fc2_copy(chunk).start()
         if chunk < 4:
@@ -449,16 +479,16 @@
     qkv_copy(0, 0).start()
     qkv_copy(0, 1).start()
     qkv_copy(1, 0).start()
-    gctx[...] = jnp.zeros_like(gctx)
+    gctx[:] = jnp.zeros_like(gctx)
     sums_out, totals = sums_out[:8], (sum1g, sum1b, sum2g, sum2b, sumproj, sumfc2, sumqkv, sumfc1)
     for total in totals:
-        total[...] = jnp.zeros_like(total)
-    g1[...] = low1[...].astype(F32)
-    g2[...] = low2[...].astype(F32)
+        total[:] = jnp.zeros_like(total)
+    g1[:] = low1[:].astype(F32)
+    g2[:] = low2[:].astype(F32)
     everyone(stage, stages)
 
     def one_image(image, carry):
-        slot = lax.rem(image, 2)
+        slot = flip(image)
         more = image + 1 < images
         save_gy, save_mid, save_qkv = saves(image, slot)
         load_h, load_x, load_qkv = loads(image)
@@ -484,15 +514,15 @@
             for chunk in range(2):
                 g_save(image, chunk).wait()
 
-        acc[...] = jnp.zeros_like(acc)
+        acc[:] = jnp.zeros_like(acc)
 
         def fc2(chunk):
-            lines = pl.ds(pl.multiple_of(chunk * CHUNK, CHUNK), CHUNK)
-            abuf[lax.rem(chunk, 2)] = dot(gin[slot], vfc2[lines, :], 1, 1).astype(BF16)
+            columns = pl.ds(pl.multiple_of(chunk * CHUNK, CHUNK), CHUNK)
+            abuf[flip(chunk)] = dot(gin[slot], vfc2[:, columns]).astype(BF16)
 
         def gelu(chunk):
             columns = pl.ds(pl.multiple_of(chunk * CHUNK, CHUNK), CHUNK)
-            slot2 = lax.rem(chunk, 2)
+            slot2 = flip(chunk)
             slot4 = lax.rem(chunk, 4)
             pre = abuf[slot2].astype(F32) * jnp.concatenate([shared[slot4 * 2], shared[slot4 * 2 + 1]], axis=1)
             sumfc1[:, columns] += fold(pre)
@@ -501,8 +531,8 @@
             return low
 
         def fc1(chunk, low):
-            columns = pl.ds(pl.multiple_of(chunk * CHUNK, CHUNK), CHUNK)
-            acc[...] += dot(low, vfc1[:, columns], 1, 1)
+            lines = pl.ds(pl.multiple_of(chunk * CHUNK, CHUNK), CHUNK)
+            acc[:] += dot(low, vfc1[lines, :])
 
         fc2(0)
 
@@ -554,14 +584,14 @@
 
         def back2(lines):
             grad = acc[lines, :].astype(BF16).astype(F32)
-            grad_in, by_unit = norm_backward(grad, hid[lines, :], g2[...])
-            sum2g[...] += fold(by_unit)
-            sum2b[...] += fold(grad)
+            grad_in, by_unit = norm_backward(grad, hid[lines, :], g2[:])
+            sum2g[:] += fold(by_unit)
+            sum2b[:] += fold(grad)
             top = gin[slot, lines, :].astype(F32)
-            sumfc2[...] += fold(top)
+            sumfc2[:] += fold(top)
             low = (top + grad_in).astype(BF16)
             gmid[lines, :] = low
-            sumproj[...] += fold(low.astype(F32))
+            sumproj[:] += fold(low.astype(F32))
 
         by_rows(rows, back2)
         save_mid.start()
@@ -574,13 +604,13 @@
 
         @pl.when(jnp.logical_and(stage < stages - 1, image + 2 < images))
         def _():
-            pl.semaphore_signal(free_sem, inc=1, device_id={"pp": lax.rem(stage + 1, stages)}, device_id_type=MESH)
+            pl.semaphore_signal(free_sem, device_id={"pp": lax.rem(stage + 1, stages)}, device_id_type=MESH)
 
         @pl.when(image == 0)
         def _():
             proj_copy.wait()
 
-        low = dot(gmid[...], vproj[...], 1, 1).astype(BF16)
+        low = dot(gmid[:], vproj[:]).astype(BF16)
         for number in range(heads):
             gctx[:, number * LANES:number * LANES + head] = low[:, number * head:(number + 1) * head]
         load_qkv.wait()
@@ -596,7 +626,7 @@
                 p_load(image, group).wait()
             probs = shared[group % 2 * GROUP + inner, :, :rows]
             at = number * head
-            mean = jnp.sum(grad_probs * probs, axis=0, keepdims=True)
+            mean = jnp.sum(grad_probs * probs, **DOWN)
             low = (probs * (grad_probs - mean) * scale).astype(BF16)
             value = dot(probs.astype(BF16), gctx[:, lanes_of(number)]).astype(BF16)
             gqkv[:, 2 * width + at:2 * width + at + head] = value[:, :head]
@@ -622,7 +652,7 @@
                 columns = pl.ds(pl.multiple_of(part * width + at, 128), size)
                 piece = gqkv[:, columns]
                 sumqkv[:, columns] += fold(piece.astype(F32))
-                acc[...] += dot(piece, vqkv[lax.rem(index * 2 + side, 3), :size])
+                acc[:] += dot(piece, vqkv[third(index * 2 + side), :size])
 
                 @pl.when(index + 1 + side < images * 3)
                 def _():
@@ -630,7 +660,7 @@
 
             return carry
 
-        acc[...] = jnp.zeros_like(acc)
+        acc[:] = jnp.zeros_like(acc)
         lax.fori_loop(0, 3, qkv_part, 0)
 
         @pl.when(more)
@@ -646,9 +676,9 @@
 
         def back1(lines):
             grad = acc[lines, :].astype(BF16).astype(F32)
-            grad_in, by_unit = norm_backward(grad, hid[lines, :], g1[...])
-            sum1g[...] += fold(by_unit)
-            sum1b[...] += fold(grad)
+            grad_in, by_unit = norm_backward(grad, hid[lines, :], g1[:])
+            sum1g[:] += fold(by_unit)
+            sum1b[:] += fold(grad)
             gout[lines, :] = (gmid[lines, :].astype(F32) + grad_in).astype(BF16)
 
         by_rows(rows, back1)
@@ -682,7 +712,7 @@
         g_save(images - 1, chunk).wait()
 
     for out, total in zip(sums_out, totals):
-        out[...] = jnp.sum(total[...], axis=0, keepdims=True)
+        out[:] = jnp.sum(total[:], **DOWN)
 
     @pl.when(jnp.logical_not(is_first))
     def _():
@@ -693,6 +723,8 @@
 VMEM = pl.BlockSpec(memory_space=pltpu.VMEM)
 LIMIT = 67_043_328
 DMA = pltpu.SemaphoreType.DMA
+PAIR = DMA((2,))
+TRIPLE = DMA((3,))
 
 
 def run_forward(dims, emb, wqkv, wproj, wfc1, wfc2, vectors):
@@ -715,7 +747,7 @@
             pltpu.VMEM((3, rows, CHUNK), F32), pltpu.VMEM((2, rows, CHUNK), BF16), pltpu.VMEM((2, GROUP, rows, HALF), F32),
             pltpu.VMEM((images, 16, width), BF16),
             *(pltpu.VMEM(vector.shape, F32) for vector in vectors),
-            DMA((3,)), DMA((2,)), DMA((2,)), DMA((stages,)), DMA(()), DMA((6,)), DMA((3, 2)), DMA((2,)), DMA((2,)),
+            DMA((3, hidden // CHUNK)), PAIR, PAIR, DMA((stages,)), DMA(()), DMA((6,)), DMA((3, 2)), PAIR, PAIR,
             pltpu.SemaphoreType.REGULAR],
         compiler_params=pltpu.CompilerParams(collective_id=0, has_side_effects=True, vmem_limit_bytes=LIMIT),
         name="forward",
@@ -725,7 +757,7 @@
 def run_backward(dims, gtop, wqkv, wproj, wfc1, wfc2, g1, g2, x_s, qkv_s, h_s, d_s, p_s):
     stages, images, tokens, heads, head = dims
     rows, width = x_s.shape[1:]
-    hidden = wfc1.shape[1]
+    hidden = wfc1.shape[0]
     hbm = lambda *shape: jax.ShapeDtypeStruct((images, rows) + shape, BF16)
     sizes = (width,) * 6 + (3 * width, hidden)
     return pl.pallas_call(
@@ -741,7 +773,7 @@
             pltpu.VMEM((rows, 3 * heads * LANES), BF16), pltpu.VMEM((rows, 3 * width), BF16),
             pltpu.VMEM((rows, width), BF16), pltpu.VMEM((1, width), F32), pltpu.VMEM((1, width), F32),
             *(pltpu.VMEM((8, size), F32) for size in sizes),
-            DMA((3, hidden // CHUNK)), DMA((3,)), DMA((2,)), DMA((2,)), DMA((stages,)), DMA(()), DMA((4,)), DMA((3,)), DMA((4,)), DMA((2,)), DMA((2,)),
+            DMA((3, hidden // CHUNK)), TRIPLE, PAIR, PAIR, DMA((stages,)), DMA(()), DMA((4,)), TRIPLE, DMA((4,)), PAIR, PAIR,
             pltpu.SemaphoreType.REGULAR],
         compiler_params=pltpu.CompilerParams(collective_id=1, has_side_effects=True, vmem_limit_bytes=LIMIT),
         name="backward",
@@ -750,12 +782,12 @@
 
 def head_kernel(inv_count, tops, labels, gain, bias, w_head, b_head, loss, gtop, g_gain, g_bias, g_w_head, g_b_head):
     images, width = tops.shape
-    line = lambda ref: ref[...].reshape(1, -1).astype(F32)
+    line = lambda ref: ref[:].reshape(1, -1).astype(F32)
     wide_gain = line(gain)
-    pooled = layer_norm(tops[...], wide_gain, line(bias))
-    logits = dot(pooled, w_head[...], 1, 1) + line(b_head)
-    shifted = logits - jnp.max(logits, axis=-1, keepdims=True)
-    log_probs = shifted - jnp.log(jnp.sum(jnp.exp(shifted), axis=-1, keepdims=True))
+    pooled = layer_norm(tops[:], wide_gain, line(bias))
+    logits = dot(pooled, w_head[:], 1, 1) + line(b_head)
+    shifted = logits - jnp.max(logits, **ACROSS)
+    log_probs = shifted - jnp.log(jnp.sum(jnp.exp(shifted), **ACROSS))
     classes = logits.shape[-1]
     number = lax.broadcasted_iota(jnp.int32, (images, 1), 0)
     label = jnp.zeros((images, 1), jnp.int32)
@@ -763,17 +795,17 @@
         label = jnp.where(number == image, labels[image % labels.shape[0], image // labels.shape[0]], label)
     chosen = (lax.broadcasted_iota(jnp.int32, logits.shape, 1) == label).astype(F32)
     target = (1.0 - SMOOTH) * chosen + SMOOTH / classes
-    parts = jnp.sum(target * log_probs, axis=-1, keepdims=True)
-    loss[...] = -jnp.sum(parts, axis=0, keepdims=True) * inv_count
+    parts = jnp.sum(target * log_probs, **ACROSS)
+    loss[:] = -jnp.sum(parts, **DOWN) * inv_count
     grad_logits = (jnp.exp(log_probs) - target) * inv_count
     low = grad_logits.astype(BF16)
-    g_w_head[...] = dot(low, pooled, 0, 0)
-    g_b_head[...] = jnp.sum(grad_logits, axis=0)
-    grad = dot(low, w_head[...]).astype(BF16).astype(F32)
-    grad_in, by_unit = norm_backward(grad, tops[...], wide_gain)
-    g_gain[...] = jnp.sum(by_unit, axis=0)
-    g_bias[...] = jnp.sum(grad, axis=0)
-    gtop[...] = jnp.zeros_like(gtop)
+    g_w_head[:] = dot(low, pooled, 0, 0)
+    g_b_head[:] = jnp.sum(grad_logits, axis=0)
+    grad = dot(low, w_head[:]).astype(BF16).astype(F32)
+    grad_in, by_unit = norm_backward(grad, tops[:], wide_gain)
+    g_gain[:] = jnp.sum(by_unit, axis=0)
+    g_bias[:] = jnp.sum(grad, axis=0)
+    gtop[:] = jnp.zeros_like(gtop)
     for image in range(images):
         gtop[image, 0:1, :] = grad_in[image:image + 1].astype(BF16)
 
@@ -815,7 +847,7 @@
         return pl.ds(pl.multiple_of(at * unit, LANES), unit)
 
     def left_copy(step, act):
-        slot = lax.rem(step, 2)
+        slot = flip(step)
         for product, source in enumerate((fc2_l, qkv_l, proj_l, patch_l)):
             full = source.shape[1] // size
             first = starts[product]
@@ -830,7 +862,7 @@
                     act(pltpu.make_async_copy(source.at[:, pl.ds(full * size, tail)], lhs.at[slot, :, pl.ds(0, tail)], lsem.at[slot]))
 
     def out_copy(step, act):
-        slot = lax.rem(step, 2)
+        slot = flip(step)
         for product, target in enumerate((fc2_o, qkv_o, proj_o)):
             full = target.shape[0] // size
             first = starts[product]
@@ -849,11 +881,11 @@
         return pltpu.make_async_copy(source, rhs.at[product % 2], rsem.at[product % 2])
 
     def block_copy(step):
-        slot = lax.rem(step, 2)
+        slot = flip(step)
         return pltpu.make_async_copy(fc1_r.at[:, lines(step, wide_size)], block.at[slot], bsem.at[slot])
 
     def wide_copy(step):
-        slot = lax.rem(step, 2)
+        slot = flip(step)
         return pltpu.make_async_copy(wide.at[slot], fc1_o.at[:, lines(step, wide_size)], wsem.at[slot])
 
     start = lambda copy: copy.start()
@@ -862,10 +894,10 @@
     right_copy(0).start()
     right_copy(1).start()
     for given, passed in zip(sums, sums_out):
-        passed[...] = given[...]
+        passed[:] = given[:]
 
     def one_step(step, carry):
-        slot = lax.rem(step, 2)
+        slot = flip(step)
 
         @pl.when(step >= 1)
         def _():
@@ -904,10 +936,10 @@
 
     lax.fori_loop(0, steps, one_step, 0)
     right_copy(4).wait()
-    turned[...] = rhs[0].T
+    turned[:] = rhs[0].T
 
     def wide_step(step, carry):
-        slot = lax.rem(step, 2)
+        slot = flip(step)
 
         @pl.when(step >= 1)
         def _():
@@ -922,7 +954,7 @@
             block_copy(step + 1).start()
 
         block_copy(step).wait()
-        wide[slot] = dot(turned[...], block[slot])
+        wide[slot] = dot(turned[:], block[slot])
         return carry
 
     lax.fori_loop(0, wide_steps, wide_step, 0)
@@ -947,7 +979,7 @@
         scratch_shapes=[
             pltpu.VMEM((2, rows, size), BF16), pltpu.VMEM((2, rows, width), BF16), pltpu.VMEM((2, size, width), F32),
             pltpu.VMEM((width, rows), BF16), pltpu.VMEM((2, rows, wide_size), BF16), pltpu.VMEM((2, width, wide_size), F32),
-            DMA((2,)), DMA((2,)), DMA((2,)), DMA((2,)), DMA((2,))],
+            PAIR, PAIR, PAIR, PAIR, PAIR],
         compiler_params=pltpu.CompilerParams(vmem_limit_bytes=LIMIT),
         cost_estimate=pl.CostEstimate(flops=flops, bytes_accessed=4 * sum(a * b for a, b in shapes), transcendentals=0),
         name="weights",
@@ -991,7 +1023,7 @@
         loss, gtop, g_lnf_gain, g_lnf_bias, g_w_head, g_b_head = run_head(
             inv_count, tops, jnp.transpose(labels), lnf_gain, lnf_bias, jnp.transpose(w_head), b_head)
 
-        gy_s, gpre_s, gmid_s, gqkv_s, gemb, *sums = run_backward(dims, gtop, *big, vectors[0], vectors[4], x_s, qkv_s, h_s, d_s, p_s)
+        gy_s, gpre_s, gmid_s, gqkv_s, gemb, *sums = run_backward(dims, gtop, big[0], *map(jnp.transpose, big[1:]), vectors[0], vectors[4], x_s, qkv_s, h_s, d_s, p_s)
         flat = lambda array: array.reshape(images * rows, -1)
         g_w_fc2, g_w_qkv, g_w_proj, g_w_patch, g_w_fc1, *sums = run_weights(
             tuple(map(flat, (g_s, gqkv_s, c_s, patch_rows, n_s))), tuple(map(flat, (gy_s, a_s, gmid_s, gemb, gpre_s))), patch_size, sums)

time: 932 us -> 952 us (1.021)
  local copies, waits for them, and re-layouts: 11.2 us -> 62.6 us
  Pallas kernels: 901 us -> 865 us
    unnamed x7 -> x9, local copies, waits for them, and re-layouts: 5.14 us -> 50.3 us
    pallas_call x1, Pallas kernels: 356 us -> 323 us  [run_forward(): pl.pallas_call(functools.partial(forward_kernel, dims), out_shape=(hbm(wi...]
where the time goes in v5:
time: 952 us; the launch traced here: 946 us
  Pallas kernels  865 us (91%)
  local copies, waits for them, and re-layouts  62.6 us (7%)
    pallas_call x1, Pallas kernels, run_backward(): pl.pallas_call(functools.partial(backward_kernel, dims), out_shape=(hbm(w...  385 us
    pallas_call x1, Pallas kernels, run_forward(): pl.pallas_call(functools.partial(forward_kernel, dims), out_shape=(hbm(wi...  323 us
    pallas_call x1, Pallas kernels, run_weights(): pl.pallas_call(weight_kernel, out_shape=tuple((jax.ShapeDtypeStruct(shape...  150 us
    unnamed x9, local copies, waits for them, and re-layouts  50.3 us

profile of v5, /device:TPU:7, one launch (start us, length us, event | category | flops | bytes accessed | tf_op | source)
XLA Modules:
  0.0 945.8 jit_solution(2831848356020807372)
XLA Ops:
  0.7 5.1 copy.50
  5.8 0.0 copy-start
  5.8 0.7 convert_element_type.22
  6.5 0.7 convert_element_type.23
  7.2 1.3 select_add_fusion
  8.6 0.0 copy-start.2
  8.6 8.6 add_convert_fusion.refs_0_
  17.2 0.0 copy-done
  17.2 0.0 copy-done.2
  17.2 0.7 reshape_reshape_squeeze.4.refs_7_
  17.9 323.2 %forward.1 = (bf16[8,272,1408]{2,1,0:T(8,128)(2,1)}, bf16[8,272,1408]{2,1,0:T(8,128)(2,1)}, bf16[8,272,6144]{2,1,0:T(8,128)(2,1)}, bf16[8,272,1408]{2,1,0:T(8,12...) custom-call(bf16[8,272,1408]{2,1,0:T(8,128)(2,1)} %add_convert_fusio, ...), custom_call_target="tpu_custom_call" | custom-call | tf_op jit(solution)/shard_map/forward/pallas_call | solution.py:735
  341.1 7.0 head.1
  348.1 6.3 copy.56
  354.3 22.6 %copy.51 = bf16[1,1408,6144]{1,2,0:T(8,128)(2,1)} copy(bf16[1,1408,6144]{2,1,0:T(8,128)(2,1)} %param.36) | data formatting | bytes 34603008 | tf_op args[14]
  376.9 22.6 %copy.52 = bf16[1,6144,1408]{1,2,0:T(8,128)(2,1)} copy(bf16[1,6144,1408]{2,1,0:T(8,128)(2,1)} %param.38) | data formatting | bytes 34603008 | tf_op args[16]
  399.5 385.0 %backward.1 = (bf16[8,272,1408]{2,1,0:T(8,128)(2,1)}, bf16[8,272,6144]{2,1,0:T(8,128)(2,1)}, bf16[8,272,1408]{2,1,0:T(8,128)(2,1)}, bf16[8,272,4224]{2,1,0:T(8,1...) custom-call(bf16[8,16,1408]{2,1,0:T(8,128)(2,1)} %get-tuple-element., ...), custom_call_target="tpu_custom_call" | custom-call | tf_op jit(solution)/shard_map/backward/pallas_call | solution.py:763
  784.5 4.1 pad.12
  788.6 150.0 %weights.1 = (f32[6144,1408]{1,0:T(8,128)}, f32[4224,1408]{1,0:T(8,128)}, f32[1408,1408]{1,0:T(8,128)}, f32[588,1408]{1,0:T(8,128)}, f32[1408,6144]{1,0:T(8,128)...) custom-call(bf16[2176,6144]{1,0:T(8,128)(2,1)} %bitcast.58, ...), custom_call_target="tpu_custom_call" | custom-call | flops 113409916928 | bytes 104237056 | tf_op jit(solution)/shard_map/weights/pallas_call | solution.py:974
  938.6 0.8 reduce.1
  939.4 0.7 reshape.110
  940.1 3.7 convert_reduce_fusion
  943.8 0.0 copy-start.1
  943.8 0.9 slice_reduce_fusion
  944.7 0.6 slice_reduce_fusion.1
  945.3 0.0 copy-done.1
  (1 shorter events, 0.0 us)
Async XLA Ops:
  5.8 11.4 %copy-start = (bf16[4,2,256,588]{3,2,1,0:T(8,128)(2,1)}, bf16[4,2,256,588]{3,2,1,0:T(8,128)(2,1)S(1)}, u32[]{:S(2)}) copy-start(bf16[4,2,256,588]{3,2,1,0:T(8,128)(2,1)S(1)} %copy.50) | copy-start | bytes 7225348
  8.6 8.6 copy-start.2
  943.8 1.6 copy-start.1

commit v6 on v5

--- a/solution.py
+++ b/solution.py
@@ -62,7 +62,7 @@
     pl.semaphore_wait(barrier, stages - 1)
 
 
-def weight_copies(wproj, wfc1, wfc2, vproj, vfc1, vfc2, sems, turned):
+def weight_copies(wproj, wfc1, wfc2, vproj, vfc1, vfc2, sems):
     def of_chunk(source, target, which, by_lines):
         def copy(chunk):
             span = pl.ds(pl.multiple_of(chunk * CHUNK, CHUNK), CHUNK)
@@ -71,14 +71,14 @@
         return copy
 
     proj = pltpu.make_async_copy(wproj, vproj, sems.at[0, 0])
-    return proj, of_chunk(wfc1, vfc1, 1, turned), of_chunk(wfc2, vfc2, 2, not turned)
+    return proj, of_chunk(wfc1, vfc1, 1, False), of_chunk(wfc2, vfc2, 2, True)
 
 
 def forward_kernel(dims, *refs):
     (emb, wqkv, wproj, wfc1, wfc2, *given,
      x_s, a_s, qkv_s, c_s, h_s, n_s, d_s, g_s, p_s, tops_out,
-     vqkv, vproj, vfc1, vfc2, xin, act, qkv, mid, yacc, ubuf, gbuf, pbuf, tops,
-     g1, b1, bqkv, bproj, g2, b2, bfc1, bfc2,
+     vqkv, vproj, vfc1, vfc2, xin, act, qkv, mid, yacc, ubuf, gbuf, tops,
+     g1, b1, bqkv, bproj, g2, b2, bfc2,
      wsem, qsem, recv_sem, send_sem, top_sem, save_sem, usem, gsem, psem, free_sem) = refs
     stages, images, tokens, heads, head = dims
     rows, width = mid.shape
@@ -89,10 +89,9 @@
     scale2 = head ** -0.5 / math.log(2.0)
 
 
-    def qkv_copy(index):
-        slot = flip(index)
-        lines = pl.ds(pl.multiple_of(third(index) * width, 128), width)
-        return pltpu.make_async_copy(wqkv.at[lines], vqkv.at[slot], qsem.at[slot])
+    def qkv_copy(part):
+        lines = pl.ds(pl.multiple_of(part * width, LANES), width)
+        return pltpu.make_async_copy(wqkv.at[lines], vqkv.at[lines], qsem.at[part])
 
     def emb_copy(image, slot):
         return pltpu.make_async_copy(emb.at[image], xin.at[slot], recv_sem.at[slot])
@@ -100,28 +99,18 @@
     @pl.when(is_first)
     def _():
         emb_copy(0, 0).start()
-
-    qkv_copy(0).start()
-
-    @pl.when(is_first)
-    def _():
         emb_copy(1, 1).start()
 
-    qkv_copy(1).start()
-    proj_copy, fc1_copy, fc2_copy = weight_copies(wproj, wfc1, wfc2, vproj, vfc1, vfc2, wsem, False)
-
-    def load_rest():
-        proj_copy.start()
-        for chunk in range(chunks):
-            fc1_copy(chunk).start()
-            fc2_copy(chunk).start()
-
-    @pl.when(jnp.logical_not(is_first))
-    def _():
-        load_rest()
-
+    proj_copy, fc1_copy, fc2_copy = weight_copies(wproj, wfc1, wfc2, vproj, vfc1, vfc2, wsem)
+    for part in range(3):
+        qkv_copy(part).start()
+    proj_copy.start()
+    for chunk in range(chunks):
+        fc1_copy(chunk).start()
+        fc2_copy(chunk).start()
     qkv[:] = jnp.zeros_like(qkv)
-    for low, wide in zip(given, (g1, b1, bqkv, bproj, g2, b2, bfc1, bfc2)):
+    *lows, bfc1, low = given
+    for low, wide in zip((*lows, low), (g1, b1, bqkv, bproj, g2, b2, bfc2)):
         wide[:] = low[:].astype(F32)
     everyone(stage, stages)
 
@@ -148,13 +137,18 @@
         slot = flip(chunk)
         return pltpu.make_async_copy(gbuf.at[slot], g_s.at[image, :, pl.ds(pl.multiple_of(chunk * CHUNK, CHUNK), CHUNK)], gsem.at[slot])
 
-    def p_save(image, group):
-        slot = group % 2
-        return pltpu.make_async_copy(pbuf.at[slot], p_s.at[image, pl.ds(group * GROUP, GROUP)], psem.at[slot])
+    def p_slot(number):
+        slot = number % 9
+        if slot < 6:
+            return ubuf.at[slot // 2, :, pl.ds(slot % 2 * HALF, HALF)]
+        return yacc.at[:, pl.ds((slot - 6) * HALF, HALF)]
+
+    def p_save(image, number):
+        return pltpu.make_async_copy(p_slot(number), p_s.at[image, number], psem.at[number % 9])
 
     def top_copy(image, other):
         return pltpu.make_async_remote_copy(
-            src_ref=mid.at[pl.ds(0, 16)], dst_ref=tops.at[image], send_sem=send_sem.at[1 + other], recv_sem=top_sem,
+            src_ref=mid.at[pl.ds(0, 8)], dst_ref=tops.at[image], send_sem=send_sem.at[1 + other], recv_sem=top_sem,
             device_id={"pp": other}, device_id_type=MESH)
 
     def next_copy(image, slot):
@@ -190,21 +184,15 @@
         save_a.start()
 
         def qkv_part(part, carry):
-            index = image * 3 + part
-            qkv_copy(index).wait()
-            low = (dot(act[:], vqkv[flip(index)], 1, 1) + bqkv[part]).astype(BF16)
+            @pl.when(image == 0)
+            def _():
+                qkv_copy(part).wait()
+
+            lines = pl.ds(pl.multiple_of(part * width, LANES), width)
+            low = (dot(act[:], vqkv[lines, :], 1, 1) + bqkv[part]).astype(BF16)
             for at in range(heads):
                 lane = part * (heads * LANES) + at * LANES
                 qkv[:, pl.ds(pl.multiple_of(lane, LANES), head)] = low[:, at * head:(at + 1) * head]
-
-            @pl.when(part == 0)
-            def _():
-                qkv_copy(index + 2).start()
-
-            @pl.when(jnp.logical_and(is_first, index == 0))
-            def _():
-                load_rest()
-
             return carry
 
         lax.fori_loop(0, 3, qkv_part, 0)
@@ -214,17 +202,19 @@
 
         @pl.when(image > 0)
         def _():
-            p_save(image, 0).wait()
-            p_save(image, 1).wait()
+            for chunk in range(3):
+                u_save(image, chunk).wait()
 
         def scores_of(number):
             q, k = (qkv[:, lane:lane + LANES] for lane in (number * LANES, (heads + number) * LANES))
             return dot(k, q, 1, 1)
 
         def attend(number, scores):
-            group, inner = number // GROUP, number % GROUP
-            if group >= 2 and inner == 0:
-                p_save(image, group).wait()
+            if number == 9:
+                for slot in range(6):
+                    p_save(image, slot).wait()
+            if number > 14:
+                p_save(image, number - 9).wait()
             v = qkv[:, (2 * heads + number) * LANES:(2 * heads + number + 1) * LANES]
             top, tail = scores[:tokens - 1], scores[tokens - 1:]
             most = jnp.maximum(jnp.max(top, **DOWN), tail[:1])
@@ -233,10 +223,9 @@
             tail = jnp.where(real, jnp.exp2(jnp.minimum(tail - most, 0.0) * scale2), 0.0)
             inv = 1.0 / (jnp.sum(top, **DOWN) + jnp.sum(tail, **DOWN))
             probs = jnp.concatenate([top, tail], axis=0) * inv
-            pbuf[group % 2, inner, :, :rows] = probs
+            p_slot(number)[:, :rows] = probs
             act[:, number * head:(number + 1) * head] = dot(probs.astype(BF16), v, 0, 0).astype(BF16)[:, :head]
-            if inner == GROUP - 1:
-                p_save(image, group).start()
+            p_save(image, number).start()
 
         scores = scores_of(0)
         for number in range(heads):
@@ -245,11 +234,6 @@
             scores = later
         save_c.start()
 
-        @pl.when(image + 1 < images)
-        def _():
-            qkv_copy(image * 3 + 3).start()
-            qkv_copy(image * 3 + 4).start()
-
         @pl.when(image == 0)
         def _():
             proj_copy.wait()
@@ -271,6 +255,8 @@
             pl.semaphore_signal(free_sem, device_id={"pp": lax.rem(stage + stages - 1, stages)}, device_id_type=MESH)
 
         save_c.wait()
+        for number in (7, 8, 15):
+            p_save(image, number).wait()
 
         def norm2(lines):
             hidden = mid[lines, :]
@@ -284,16 +270,17 @@
         def _():
             fc1_copy(0).wait()
 
+        for number in range(9, 15):
+            p_save(image, number).wait()
+
         @pl.when(image > 0)
         def _():
-            for chunk in range(3):
-                u_save(image, chunk).wait()
             for chunk in range(2):
                 g_save(image, chunk).wait()
 
         def fc1(chunk):
             columns = pl.ds(pl.multiple_of(chunk * CHUNK, CHUNK), CHUNK)
-            ubuf[third(chunk)] = dot(act[:], vfc1[:, columns]) + bfc1[:, columns]
+            ubuf[third(chunk)] = dot(act[:], vfc1[:, columns]) + bfc1[:, columns].astype(F32)
 
         def gelu(chunk):
             slot3, slot2 = third(chunk), flip(chunk)
@@ -359,7 +346,7 @@
         def _():
             for other in range(stages - 1):
                 top_copy(image, other).start()
-            tops[image] = mid[pl.ds(0, 16), :]
+            tops[image] = mid[pl.ds(0, 8), :]
 
         return carry
 
@@ -372,7 +359,6 @@
         u_save(images - 1, chunk).wait()
     for chunk in range(2):
         g_save(images - 1, chunk).wait()
-        p_save(images - 1, chunk).wait()
 
     @pl.when(jnp.logical_not(is_last))
     def _():
@@ -397,10 +383,10 @@
      gy_s, gpre_s, gmid_s, gqkv_s, gemb, *sums_out,
      vqkv, vproj, vfc1, vfc2, gin, acc, shared, abuf, gbuf, hid, gmid, gctx, qkv, gqkv, gout, g1, g2,
      sum1g, sum1b, sum2g, sum2b, sumproj, sumfc2, sumqkv, sumfc1,
-     wsem, qsem, recv_sem, top_sem, send_sem, emb_sem, save_sem, load_sem, dsem, gsem, psem, free_sem) = refs
+     wsem, qsem, recv_sem, top_sem, send_sem, emb_sem, relay_sem, save_sem, load_sem, dsem, gsem, psem, free_sem) = refs
     stages, images, tokens, heads, head = dims
     rows, width = gmid.shape
-    chunks = vfc2.shape[1] // CHUNK
+    chunks = vfc1.shape[1] // CHUNK
     groups = heads // GROUP
     stage = lax.axis_index("pp")
     is_first = stage == 0
@@ -445,8 +431,13 @@
 
     def emb_send(image, other):
         return pltpu.make_async_remote_copy(
-            src_ref=gout, dst_ref=gemb.at[image], send_sem=send_sem.at[other], recv_sem=emb_sem,
+            src_ref=gout, dst_ref=gemb.at[image], send_sem=send_sem.at[other], recv_sem=emb_sem.at[image],
             device_id={"pp": other}, device_id_type=MESH)
+
+    def emb_relay(image):
+        return pltpu.make_async_remote_copy(
+            src_ref=gemb.at[image], dst_ref=gemb.at[image], send_sem=relay_sem.at[image], recv_sem=emb_sem.at[image],
+            device_id={"pp": stages - 1}, device_id_type=MESH)
 
     def emb_local(image):
         return pltpu.make_async_copy(gout, gemb.at[image], save_sem.at[3])
@@ -458,7 +449,7 @@
 
         @pl.when(is_first)
         def _():
-            for other in range(1, stages):
+            for other in range(1, stages - 1):
                 emb_send(image, other).wait_send()
             emb_local(image).wait()
 
@@ -468,7 +459,7 @@
         top_copy(0, 0).start()
         top_copy(1, 1).start()
 
-    proj_copy, fc1_copy, fc2_copy = weight_copies(wproj, wfc1, wfc2, vproj, vfc1, vfc2, wsem, True)
+    proj_copy, fc1_copy, fc2_copy = weight_copies(wproj, wfc1, wfc2, vproj, vfc1, vfc2, wsem)
     for chunk in range(chunks):
         fc2_copy(chunk).start()
         if chunk < 4:
@@ -476,9 +467,8 @@
         fc1_copy(chunk).start()
     loads(0)[0].start()
     proj_copy.start()
-    qkv_copy(0, 0).start()
-    qkv_copy(0, 1).start()
-    qkv_copy(1, 0).start()
+    for part, side in ((0, 0), (0, 1), (1, 0)):
+        qkv_copy(part, side).start()
     gctx[:] = jnp.zeros_like(gctx)
     sums_out, totals = sums_out[:8], (sum1g, sum1b, sum2g, sum2b, sumproj, sumfc2, sumqkv, sumfc1)
     for total in totals:
@@ -517,8 +507,8 @@
         acc[:] = jnp.zeros_like(acc)
 
         def fc2(chunk):
-            columns = pl.ds(pl.multiple_of(chunk * CHUNK, CHUNK), CHUNK)
-            abuf[flip(chunk)] = dot(gin[slot], vfc2[:, columns]).astype(BF16)
+            lines = pl.ds(pl.multiple_of(chunk * CHUNK, CHUNK), CHUNK)
+            abuf[flip(chunk)] = dot(gin[slot], vfc2[lines, :], 1, 1).astype(BF16)
 
         def gelu(chunk):
             columns = pl.ds(pl.multiple_of(chunk * CHUNK, CHUNK), CHUNK)
@@ -531,8 +521,8 @@
             return low
 
         def fc1(chunk, low):
-            lines = pl.ds(pl.multiple_of(chunk * CHUNK, CHUNK), CHUNK)
-            acc[:] += dot(low, vfc1[lines, :])
+            columns = pl.ds(pl.multiple_of(chunk * CHUNK, CHUNK), CHUNK)
+            acc[:] += dot(low, vfc1[:, columns], 1, 1)
 
         fc2(0)
 
@@ -610,7 +600,7 @@
         def _():
             proj_copy.wait()
 
-        low = dot(gmid[:], vproj[:]).astype(BF16)
+        low = dot(gmid[:], vproj[:], 1, 1).astype(BF16)
         for number in range(heads):
             gctx[:, number * LANES:number * LANES + head] = low[:, number * head:(number + 1) * head]
         load_qkv.wait()
@@ -697,7 +687,7 @@
 
         @pl.when(is_first)
         def _():
-            for other in range(1, stages):
+            for other in range(1, stages - 1):
                 emb_send(image, other).start()
             emb_local(image).start()
 
@@ -716,7 +706,17 @@
 
     @pl.when(jnp.logical_not(is_first))
     def _():
-        pltpu.make_async_copy(gemb, gemb, emb_sem).wait()
+        for image in range(images):
+            emb_relay(image).wait_recv()
+
+            @pl.when(stage == stages - 2)
+            def _():
+                emb_relay(image).start()
+
+    @pl.when(stage == stages - 2)
+    def _():
+        for image in range(images):
+            emb_relay(image).wait_send()
 
 
 ANY = pl.BlockSpec(memory_space=pl.ANY)
@@ -741,13 +741,13 @@
         in_specs=[ANY] * 5 + [VMEM] * 8,
         out_specs=(ANY,) * 9 + (VMEM,),
         scratch_shapes=[
-            pltpu.VMEM((2, width, width), BF16), pltpu.VMEM(wproj.shape, BF16), pltpu.VMEM(wfc1.shape, BF16), pltpu.VMEM(wfc2.shape, BF16),
+            pltpu.VMEM(wqkv.shape, BF16), pltpu.VMEM(wproj.shape, BF16), pltpu.VMEM(wfc1.shape, BF16), pltpu.VMEM(wfc2.shape, BF16),
             pltpu.VMEM((2, rows, width), BF16), pltpu.VMEM((rows, width), BF16), pltpu.VMEM((rows, 3 * heads * LANES), BF16),
             pltpu.VMEM((rows, width), BF16), pltpu.VMEM((rows, width), F32),
-            pltpu.VMEM((3, rows, CHUNK), F32), pltpu.VMEM((2, rows, CHUNK), BF16), pltpu.VMEM((2, GROUP, rows, HALF), F32),
-            pltpu.VMEM((images, 16, width), BF16),
-            *(pltpu.VMEM(vector.shape, F32) for vector in vectors),
-            DMA((3, hidden // CHUNK)), PAIR, PAIR, DMA((stages,)), DMA(()), DMA((6,)), DMA((3, 2)), PAIR, PAIR,
+            pltpu.VMEM((3, rows, CHUNK), F32), pltpu.VMEM((2, rows, CHUNK), BF16),
+            pltpu.VMEM((images, 8, width), BF16),
+            *(pltpu.VMEM(vector.shape, F32) for vector in vectors[:6]), pltpu.VMEM(vectors[7].shape, F32),
+            DMA((3, hidden // CHUNK)), TRIPLE, PAIR, DMA((stages,)), DMA(()), DMA((6,)), DMA((3, 2)), PAIR, DMA((9,)),
             pltpu.SemaphoreType.REGULAR],
         compiler_params=pltpu.CompilerParams(collective_id=0, has_side_effects=True, vmem_limit_bytes=LIMIT),
         name="forward",
@@ -757,7 +757,7 @@
 def run_backward(dims, gtop, wqkv, wproj, wfc1, wfc2, g1, g2, x_s, qkv_s, h_s, d_s, p_s):
     stages, images, tokens, heads, head = dims
     rows, width = x_s.shape[1:]
-    hidden = wfc1.shape[0]
+    hidden = wfc1.shape[1]
     hbm = lambda *shape: jax.ShapeDtypeStruct((images, rows) + shape, BF16)
     sizes = (width,) * 6 + (3 * width, hidden)
     return pl.pallas_call(
@@ -773,7 +773,7 @@
             pltpu.VMEM((rows, 3 * heads * LANES), BF16), pltpu.VMEM((rows, 3 * width), BF16),
             pltpu.VMEM((rows, width), BF16), pltpu.VMEM((1, width), F32), pltpu.VMEM((1, width), F32),
             *(pltpu.VMEM((8, size), F32) for size in sizes),
-            DMA((3, hidden // CHUNK)), TRIPLE, PAIR, PAIR, DMA((stages,)), DMA(()), DMA((4,)), TRIPLE, DMA((4,)), PAIR, PAIR,
+            DMA((3, hidden // CHUNK)), TRIPLE, PAIR, PAIR, DMA((stages,)), DMA((images,)), DMA((images,)), DMA((4,)), TRIPLE, DMA((4,)), PAIR, PAIR,
             pltpu.SemaphoreType.REGULAR],
         compiler_params=pltpu.CompilerParams(collective_id=1, has_side_effects=True, vmem_limit_bytes=LIMIT),
         name="backward",
@@ -1023,7 +1023,7 @@
         loss, gtop, g_lnf_gain, g_lnf_bias, g_w_head, g_b_head = run_head(
             inv_count, tops, jnp.transpose(labels), lnf_gain, lnf_bias, jnp.transpose(w_head), b_head)
 
-        gy_s, gpre_s, gmid_s, gqkv_s, gemb, *sums = run_backward(dims, gtop, big[0], *map(jnp.transpose, big[1:]), vectors[0], vectors[4], x_s, qkv_s, h_s, d_s, p_s)
+        gy_s, gpre_s, gmid_s, gqkv_s, gemb, *sums = run_backward(dims, gtop, *big, vectors[0], vectors[4], x_s, qkv_s, h_s, d_s, p_s)
         flat = lambda array: array.reshape(images * rows, -1)
         g_w_fc2, g_w_qkv, g_w_proj, g_w_patch, g_w_fc1, *sums = run_weights(
             tuple(map(flat, (g_s, gqkv_s, c_s, patch_rows, n_s))), tuple(map(flat, (gy_s, a_s, gmid_s, gemb, gpre_s))), patch_size, sums)

time: 952 us -> 890 us (0.935)
  local copies, waits for them, and re-layouts: 62.6 us -> 11.2 us
    unnamed x9 -> x7, local copies, waits for them, and re-layouts: 50.3 us -> 5.14 us
where the time goes in v6:
time: 890 us; the launch traced here: 889 us
  Pallas kernels  861 us (97%)
  local copies, waits for them, and re-layouts  11.2 us (1%)
    pallas_call x1, Pallas kernels, run_backward(): pl.pallas_call(functools.partial(backward_kernel, dims), out_shape=(hbm(w...  383 us
    pallas_call x1, Pallas kernels, run_forward(): pl.pallas_call(functools.partial(forward_kernel, dims), out_shape=(hbm(wi...  321 us
    pallas_call x1, Pallas kernels, run_weights(): pl.pallas_call(weight_kernel, out_shape=tuple((jax.ShapeDtypeStruct(shape...  150 us

profile of v6, /device:TPU:7, one launch (start us, length us, event | category | flops | bytes accessed | tf_op | source)
XLA Modules:
  0.0 889.3 jit_solution(4210609518877711262)
XLA Ops:
  0.7 5.1 copy.44
  5.8 0.0 copy-start
  5.8 0.7 convert_element_type.22
  6.5 0.7 convert_element_type.23
  7.2 1.3 select_add_fusion
  8.6 0.0 copy-start.2
  8.6 8.6 add_convert_fusion.refs_0_
  17.2 0.0 copy-done
  17.2 0.0 copy-done.2
  17.2 0.7 reshape_reshape_squeeze.4.refs_7_
  17.9 321.0 %forward.1 = (bf16[8,272,1408]{2,1,0:T(8,128)(2,1)}, bf16[8,272,1408]{2,1,0:T(8,128)(2,1)}, bf16[8,272,6144]{2,1,0:T(8,128)(2,1)}, bf16[8,272,1408]{2,1,0:T(8,12...) custom-call(bf16[8,272,1408]{2,1,0:T(8,128)(2,1)} %add_convert_fusio, ...), custom_call_target="tpu_custom_call" | custom-call | tf_op jit(solution)/shard_map/forward/pallas_call | solution.py:735
  338.9 7.0 head.1
  345.9 382.6 %backward.1 = (bf16[8,272,1408]{2,1,0:T(8,128)(2,1)}, bf16[8,272,6144]{2,1,0:T(8,128)(2,1)}, bf16[8,272,1408]{2,1,0:T(8,128)(2,1)}, bf16[8,272,4224]{2,1,0:T(8,1...) custom-call(bf16[8,16,1408]{2,1,0:T(8,128)(2,1)} %get-tuple-element., ...), custom_call_target="tpu_custom_call" | custom-call | tf_op jit(solution)/shard_map/backward/pallas_call | solution.py:763
  728.4 4.1 pad.12
  732.5 150.0 %weights.1 = (f32[6144,1408]{1,0:T(8,128)}, f32[4224,1408]{1,0:T(8,128)}, f32[1408,1408]{1,0:T(8,128)}, f32[588,1408]{1,0:T(8,128)}, f32[1408,6144]{1,0:T(8,128)...) custom-call(bf16[2176,6144]{1,0:T(8,128)(2,1)} %bitcast.50, ...), custom_call_target="tpu_custom_call" | custom-call | flops 113409916928 | bytes 104237056 | tf_op jit(solution)/shard_map/weights/pallas_call | solution.py:974
  882.5 0.8 reduce.1
  883.3 0.7 reshape.110
  884.0 3.7 convert_reduce_fusion
  887.7 0.0 copy-start.1
  887.7 0.9 slice_reduce_fusion
  888.6 0.6 slice_reduce_fusion.1
  889.3 0.0 copy-done.1
  (1 shorter events, 0.0 us)
Async XLA Ops:
  5.8 11.4 %copy-start = (bf16[4,2,256,588]{3,2,1,0:T(8,128)(2,1)}, bf16[4,2,256,588]{3,2,1,0:T(8,128)(2,1)S(1)}, u32[]{:S(2)}) copy-start(bf16[4,2,256,588]{3,2,1,0:T(8,128)(2,1)S(1)} %copy.44) | copy-start | bytes 7225348
  8.6 8.6 copy-start.2
  887.7 1.6 copy-start.1

commit v7 on v6

--- a/solution.py
+++ b/solution.py
@@ -183,19 +183,14 @@
         by_rows(rows, norm1)
         save_a.start()
 
-        def qkv_part(part, carry):
-            @pl.when(image == 0)
-            def _():
+        @pl.when(image == 0)
+        def _():
+            for part in range(3):
                 qkv_copy(part).wait()
 
-            lines = pl.ds(pl.multiple_of(part * width, LANES), width)
-            low = (dot(act[:], vqkv[lines, :], 1, 1) + bqkv[part]).astype(BF16)
-            for at in range(heads):
-                lane = part * (heads * LANES) + at * LANES
-                qkv[:, pl.ds(pl.multiple_of(lane, LANES), head)] = low[:, at * head:(at + 1) * head]
-            return carry
-
-        lax.fori_loop(0, 3, qkv_part, 0)
+        low = (dot(act[:], vqkv[:], 1, 1) + bqkv[:]).astype(BF16)
+        for at in range(3 * heads):
+            qkv[:, at * LANES:at * LANES + head] = low[:, at * head:(at + 1) * head]
         save_qkv.start()
 
         save_a.wait()
@@ -387,7 +382,6 @@
     stages, images, tokens, heads, head = dims
     rows, width = gmid.shape
     chunks = vfc1.shape[1] // CHUNK
-    groups = heads // GROUP
     stage = lax.axis_index("pp")
     is_first = stage == 0
     is_last = stage == stages - 1
@@ -412,9 +406,16 @@
         slot = flip(chunk)
         return pltpu.make_async_copy(gbuf.at[slot], gpre_s.at[image, :, pl.ds(pl.multiple_of(chunk * CHUNK, CHUNK), CHUNK)], gsem.at[slot])
 
-    def p_load(image, group):
-        slot = group % 2
-        return pltpu.make_async_copy(p_s.at[image, pl.ds(group * GROUP, GROUP)], shared.at[pl.ds(slot * GROUP, GROUP)], psem.at[slot])
+    held = shared.shape[0] + 3
+
+    def p_slot(number):
+        slot = number % held
+        if slot < shared.shape[0]:
+            return shared.at[slot]
+        return acc.at[:, pl.ds((slot - shared.shape[0]) * HALF, HALF)]
+
+    def p_load(image, number):
+        return pltpu.make_async_copy(p_s.at[image, number], p_slot(number), psem.at[number % held])
 
     def saves(image, slot):
         pairs = ((gin.at[slot], gy_s), (gmid, gmid_s), (gqkv, gqkv_s))
@@ -563,8 +564,8 @@
         fc1(chunks - 1, gelu(chunks - 1))
         g_save(image, chunks - 1).start()
 
-        for group in range(2):
-            p_load(image, group).start()
+        for number in range(shared.shape[0]):
+            p_load(image, number).start()
         load_h.wait()
 
         @pl.when(image > 0)
@@ -584,6 +585,8 @@
             sumproj[:] += fold(low.astype(F32))
 
         by_rows(rows, back2)
+        for number in range(shared.shape[0], held):
+            p_load(image, number).start()
         save_mid.start()
         load_x.start()
         save_gy.wait()
@@ -604,6 +607,8 @@
         for number in range(heads):
             gctx[:, number * LANES:number * LANES + head] = low[:, number * head:(number + 1) * head]
         load_qkv.wait()
+        for number in range(held):
+            p_load(image, number).wait()
         def lanes_of(number):
             return slice(number * LANES, (number + 1) * LANES)
 
@@ -611,10 +616,10 @@
             return dot(qkv[:, lanes_of(2 * heads + number)], gctx[:, lanes_of(number)], 1, 1)
 
         def attend(number, grad_probs):
-            group, inner = number // GROUP, number % GROUP
-            if inner == 0:
-                p_load(image, group).wait()
-            probs = shared[group % 2 * GROUP + inner, :, :rows]
+            if number == held:
+                for later in range(held, heads):
+                    p_load(image, later).wait()
+            probs = p_slot(number)[:, :rows]
             at = number * head
             mean = jnp.sum(grad_probs * probs, **DOWN)
             low = (probs * (grad_probs - mean) * scale).astype(BF16)
@@ -630,8 +635,8 @@
             later = grad_probs_of(number + 1) if number + 1 < heads else None
             attend(number, grad_probs)
             grad_probs = later
-            if number % GROUP == GROUP - 1 and number // GROUP + 2 < groups:
-                p_load(image, number // GROUP + 2).start()
+            if number + held < heads:
+                p_load(image, number + held).start()
         save_qkv.start()
 
         def qkv_part(part, carry):
@@ -773,14 +778,14 @@
             pltpu.VMEM((rows, 3 * heads * LANES), BF16), pltpu.VMEM((rows, 3 * width), BF16),
             pltpu.VMEM((rows, width), BF16), pltpu.VMEM((1, width), F32), pltpu.VMEM((1, width), F32),
             *(pltpu.VMEM((8, size), F32) for size in sizes),
-            DMA((3, hidden // CHUNK)), TRIPLE, PAIR, PAIR, DMA((stages,)), DMA((images,)), DMA((images,)), DMA((4,)), TRIPLE, DMA((4,)), PAIR, PAIR,
+            DMA((3, hidden // CHUNK)), TRIPLE, PAIR, PAIR, DMA((stages,)), DMA((images,)), DMA((images,)), DMA((4,)), TRIPLE, DMA((4,)), PAIR, DMA((2 * GROUP + 3,)),
             pltpu.SemaphoreType.REGULAR],
         compiler_params=pltpu.CompilerParams(collective_id=1, has_side_effects=True, vmem_limit_bytes=LIMIT),
         name="backward",
     )(gtop, wqkv, wproj, wfc1, wfc2, g1, g2, x_s, qkv_s, h_s, d_s, p_s)
 
 
-def head_kernel(inv_count, tops, labels, gain, bias, w_head, b_head, loss, gtop, g_gain, g_bias, g_w_head, g_b_head):
+def head_kernel(inv_count, tops, labels, gain, bias, w_head, b_head, loss, gtop, g_gain, g_bias, low_out, pooled_out, g_b_head):
     images, width = tops.shape
     line = lambda ref: ref[:].reshape(1, -1).astype(F32)
     wide_gain = line(gain)
@@ -799,7 +804,8 @@
     loss[:] = -jnp.sum(parts, **DOWN) * inv_count
     grad_logits = (jnp.exp(log_probs) - target) * inv_count
     low = grad_logits.astype(BF16)
-    g_w_head[:] = dot(low, pooled, 0, 0)
+    low_out[:] = low
+    pooled_out[:] = pooled
     g_b_head[:] = jnp.sum(grad_logits, axis=0)
     grad = dot(low, w_head[:]).astype(BF16).astype(F32)
     grad_in, by_unit = norm_backward(grad, tops[:], wide_gain)
@@ -816,21 +822,19 @@
     shape = lambda *dims, dtype=F32: jax.ShapeDtypeStruct(dims, dtype)
     return pl.pallas_call(
         functools.partial(head_kernel, inv_count),
-        out_shape=(shape(1, 1), shape(images, 16, width, dtype=BF16), shape(width), shape(width), shape(classes, width), shape(classes)),
+        out_shape=(shape(1, 1), shape(images, 16, width, dtype=BF16), shape(width), shape(width),
+            shape(images, classes, dtype=BF16), shape(images, width, dtype=BF16), shape(classes)),
         in_specs=[VMEM, pl.BlockSpec(memory_space=pltpu.SMEM)] + [VMEM] * 4,
-        out_specs=(VMEM,) * 6,
+        out_specs=(VMEM,) * 7,
         compiler_params=pltpu.CompilerParams(vmem_limit_bytes=LIMIT),
         name="head",
     )(tops, labels, gain, bias, w_head, b_head)
 
 
-def weight_kernel(*refs):
-    count = (len(refs) - 15 - 11) // 2
-    fc2_l, qkv_l, proj_l, patch_l, fc2_r, qkv_r, proj_r, patch_r, fc1_l, fc1_r = refs[:10]
-    sums = refs[10:10 + count]
-    fc2_o, qkv_o, proj_o, patch_o, fc1_o = refs[10 + count:15 + count]
-    sums_out = refs[15 + count:15 + 2 * count]
-    lhs, rhs, out, turned, block, wide, lsem, rsem, osem, bsem, wsem = refs[15 + 2 * count:]
+def weight_kernel(rows, given, made, *refs):
+    fc2_l, qkv_l, proj_l, patch_l, fc2_r, qkv_r, proj_r, patch_r, fc1_l, fc1_r, logit_l, logit_r, *sums = refs[:given]
+    fc2_o, qkv_o, proj_o, fc1_o, head_o, patch_o, pos_o, bias_o, first_o, *sums_out = refs[given:given + made]
+    lhs, rhs, out, turned, block, wide, logit, lsem, rsem, osem, bsem, wsem, hsem = refs[given + made:]
     width = rhs.shape[2]
     size, wide_size = lhs.shape[2], block.shape[2]
     tail = width % size
@@ -893,8 +897,23 @@
     left_copy(0, start)
     right_copy(0).start()
     right_copy(1).start()
-    for given, passed in zip(sums, sums_out):
-        passed[:] = given[:]
+    for total, passed in zip(sums, sums_out):
+        passed[:] = total[:]
+    logit[:] = dot(logit_l[:], logit_r[:], 0, 0)
+    head_copy = pltpu.make_async_copy(logit, head_o, hsem)
+    head_copy.start()
+
+    def embedding_sums(source):
+        bias = jnp.zeros_like(bias_o)
+        for at in range(0, rows, BLOCK):
+            total = sum(source[image + at:image + at + BLOCK, :].astype(F32) for image in range(0, source.shape[0], rows))
+            count = min(BLOCK, pos_o.shape[0] - at)
+            pos_o[at:at + count, :] = total[:count]
+            is_first = lax.broadcasted_iota(jnp.int32, total.shape, 0) + at < 1
+            bias = bias + jnp.sum(jnp.where(is_first, 0.0, total), axis=0)
+            if at == 0:
+                first_o[:] = jnp.sum(jnp.where(is_first, total, 0.0), axis=0)
+        bias_o[:] = bias
 
     def one_step(step, carry):
         slot = flip(step)
@@ -917,6 +936,8 @@
                 right_copy(product).wait()
                 if product >= 1:
                     right_copy(product + 1).start()
+                if product == 3:
+                    embedding_sums(rhs.at[1])
 
         @pl.when(step == steps - 1)
         def _():
@@ -961,29 +982,34 @@
     wide_copy(wide_steps - 1).start()
     wide_copy(wide_steps - 2).wait()
     wide_copy(wide_steps - 1).wait()
-
-
-def run_weights(lefts, rights, patch_size, sums):
+    head_copy.wait()
+
+
+def run_weights(lefts, rights, logit_parts, patch_size, tokens, images, sums):
     fc2_l, qkv_l, proj_l, patch_l, fc1_l = lefts
     fc2_r, qkv_r, proj_r, patch_r, fc1_r = rights
     rows, width = fc2_r.shape
     size, wide_size = 3 * LANES, 4 * LANES
-    shapes = [(left.shape[1], right.shape[1]) for left, right in zip(lefts, rights)]
-    shapes[3] = (patch_size, width)
-    flops = sum(2 * rows * a * b for a, b in shapes)
+    classes = logit_parts[0].shape[1]
+    outs = [(left.shape[1], right.shape[1]) for left, right in zip(lefts, rights)]
+    outs = outs[:3] + outs[4:]
+    flops = sum(2 * rows * a * b for a, b in outs)
+    stored = sum(4 * a * b for a, b in outs)
+    outs += [(classes, width), (patch_size, width), (tokens, width), (width,), (width,)] + [total.shape for total in sums]
+    inputs = (fc2_l, qkv_l, proj_l, patch_l, fc2_r, qkv_r, proj_r, patch_r, fc1_l, fc1_r, *logit_parts, *sums)
     return pl.pallas_call(
-        weight_kernel,
-        out_shape=tuple(jax.ShapeDtypeStruct(shape, F32) for shape in shapes) + tuple(jax.ShapeDtypeStruct(total.shape, F32) for total in sums),
-        in_specs=[ANY] * 10 + [VMEM] * len(sums),
-        out_specs=(ANY,) * 3 + (VMEM, ANY) + (VMEM,) * len(sums),
+        functools.partial(weight_kernel, rows // images, len(inputs), len(outs)),
+        out_shape=tuple(jax.ShapeDtypeStruct(shape, F32) for shape in outs),
+        in_specs=[ANY] * 10 + [VMEM] * (2 + len(sums)),
+        out_specs=(ANY,) * 5 + (VMEM,) * (len(outs) - 5),
         scratch_shapes=[
             pltpu.VMEM((2, rows, size), BF16), pltpu.VMEM((2, rows, width), BF16), pltpu.VMEM((2, size, width), F32),
             pltpu.VMEM((width, rows), BF16), pltpu.VMEM((2, rows, wide_size), BF16), pltpu.VMEM((2, width, wide_size), F32),
-            PAIR, PAIR, PAIR, PAIR, PAIR],
+            pltpu.VMEM((classes, width), F32), PAIR, PAIR, PAIR, PAIR, PAIR, DMA(())],
         compiler_params=pltpu.CompilerParams(vmem_limit_bytes=LIMIT),
-        cost_estimate=pl.CostEstimate(flops=flops, bytes_accessed=4 * sum(a * b for a, b in shapes), transcendentals=0),
+        cost_estimate=pl.CostEstimate(flops=flops, bytes_accessed=stored, transcendentals=0),
         name="weights",
-    )(fc2_l, qkv_l, proj_l, patch_l, fc2_r, qkv_r, proj_r, patch_r, fc1_l, fc1_r, *sums)
+    )(*inputs)
 
 
 def matmul_rows(spec, left, right):
@@ -1017,26 +1043,23 @@
         wqkv_t = jnp.transpose(w_qkv, (1, 2, 3, 0)).reshape(3 * width, width)
         big = (wqkv_t, w_proj.reshape(width, width), w_fc1, w_fc2)
         vectors = tuple(map(line, (ln1_gain, ln1_bias, b_qkv, b_proj, ln2_gain, ln2_bias, b_fc1, b_fc2)))
-        vectors = vectors[:2] + (vectors[2].reshape(3, 1, width),) + vectors[3:]
         x_s, a_s, qkv_s, c_s, h_s, n_s, d_s, g_s, p_s, tops = run_forward(dims, embedded, *big, vectors)
 
-        loss, gtop, g_lnf_gain, g_lnf_bias, g_w_head, g_b_head = run_head(
+        loss, gtop, g_lnf_gain, g_lnf_bias, *logit_parts, g_b_head = run_head(
             inv_count, tops, jnp.transpose(labels), lnf_gain, lnf_bias, jnp.transpose(w_head), b_head)
 
         gy_s, gpre_s, gmid_s, gqkv_s, gemb, *sums = run_backward(dims, gtop, *big, vectors[0], vectors[4], x_s, qkv_s, h_s, d_s, p_s)
         flat = lambda array: array.reshape(images * rows, -1)
-        g_w_fc2, g_w_qkv, g_w_proj, g_w_patch, g_w_fc1, *sums = run_weights(
-            tuple(map(flat, (g_s, gqkv_s, c_s, patch_rows, n_s))), tuple(map(flat, (gy_s, a_s, gmid_s, gemb, gpre_s))), patch_size, sums)
+        g_w_fc2, g_w_qkv, g_w_proj, g_w_fc1, g_w_head, g_w_patch, g_pos_embed, g_b_patch, g_cls_token, *sums = run_weights(
+            tuple(map(flat, (g_s, gqkv_s, c_s, patch_rows, n_s))), tuple(map(flat, (gy_s, a_s, gmid_s, gemb, gpre_s))),
+            logit_parts, patch_size, tokens, images, sums)
         g_ln1_gain, g_ln1_bias, g_ln2_gain, g_ln2_bias, g_b_proj, g_b_fc2, g_b_qkv, g_b_fc1 = sums
         g_w_qkv = jnp.transpose(g_w_qkv.reshape(3, heads, head, width), (3, 0, 1, 2))[None]
         layer_grads = (
             g_ln1_gain, g_ln1_bias, g_w_qkv, g_b_qkv.reshape(1, 3, heads, head), g_w_proj.reshape(1, heads, head, width), g_b_proj,
             g_ln2_gain, g_ln2_bias, g_w_fc1[None], g_b_fc1, g_w_fc2[None], g_b_fc2,
         )
-        g_pos_embed = jnp.sum(gemb[:, :tokens].astype(F32), axis=0)
-        embed_grads = (
-            g_w_patch, jnp.sum(g_pos_embed[1:], axis=0), g_pos_embed[0], g_pos_embed,
-        )
+        embed_grads = (g_w_patch, g_b_patch, g_cls_token, g_pos_embed)
         return (loss.reshape(1),) + embed_grads + layer_grads + (g_lnf_gain, g_lnf_bias, jnp.transpose(g_w_head), g_b_head)
 
     return jax.shard_map(body, mesh=mesh, in_specs=in_specs, out_specs=out_specs, check_vma=False)

time: 890 us -> 868 us (0.975)
  Pallas kernels: 861 us -> 840 us
    pallas_call x1, Pallas kernels: 321 us -> 306 us  [run_forward(): pl.pallas_call(functools.partial(forward_kernel, dims), out_shape=(hbm(wi...]
where the time goes in v7:
time: 868 us; the launch traced here: 864 us
  Pallas kernels  840 us (97%)
  local copies, waits for them, and re-layouts  10.5 us (1%)
    pallas_call x1, Pallas kernels, run_backward(): pl.pallas_call(functools.partial(backward_kernel, dims), out_shape=(hbm(w...  376 us
    pallas_call x1, Pallas kernels, run_forward(): pl.pallas_call(functools.partial(forward_kernel, dims), out_shape=(hbm(wi...  306 us
    pallas_call x1, Pallas kernels, run_weights(): pl.pallas_call(functools.partial(weight_kernel, rows // images, len(input...  153 us

profile of v7, /device:TPU:7, one launch (start us, length us, event | category | flops | bytes accessed | tf_op | source)
XLA Modules:
  0.0 864.1 jit_solution(11628429644228084911)
XLA Ops:
  0.7 5.1 copy.43
  5.8 0.0 copy-start
  5.8 0.7 convert_element_type.19
  6.5 0.7 convert_element_type.20
  7.2 1.3 select_add_fusion
  8.6 0.0 copy-start.1
  8.6 8.6 add_convert_fusion.refs_0_
  17.2 0.0 copy-done
  17.2 0.0 copy-done.1
  17.2 0.7 reshape_squeeze.7.refs_7_
  17.9 306.0 %forward.1 = (bf16[8,272,1408]{2,1,0:T(8,128)(2,1)}, bf16[8,272,1408]{2,1,0:T(8,128)(2,1)}, bf16[8,272,6144]{2,1,0:T(8,128)(2,1)}, bf16[8,272,1408]{2,1,0:T(8,12...) custom-call(bf16[8,272,1408]{2,1,0:T(8,128)(2,1)} %add_convert_fusio, ...), custom_call_target="tpu_custom_call" | custom-call | tf_op jit(solution)/shard_map/forward/pallas_call | solution.py:740
  323.9 4.3 head.1
  328.2 376.5 %backward.1 = (bf16[8,272,1408]{2,1,0:T(8,128)(2,1)}, bf16[8,272,6144]{2,1,0:T(8,128)(2,1)}, bf16[8,272,1408]{2,1,0:T(8,128)(2,1)}, bf16[8,272,4224]{2,1,0:T(8,1...) custom-call(bf16[8,16,1408]{2,1,0:T(8,128)(2,1)} %get-tuple-element., ...), custom_call_target="tpu_custom_call" | custom-call | tf_op jit(solution)/shard_map/backward/pallas_call | solution.py:768
  704.7 3.9 pad.12
  708.7 153.5 %weights.1 = (f32[6144,1408]{1,0:T(8,128)}, f32[4224,1408]{1,0:T(8,128)}, f32[1408,1408]{1,0:T(8,128)}, f32[1408,6144]{1,0:T(8,128)}, f32[1000,1408]{1,0:T(8,128...) custom-call(bf16[2176,6144]{1,0:T(8,128)(2,1)} %bitcast.49, ...), custom_call_target="tpu_custom_call" | custom-call | flops 109806878720 | bytes 100925440 | tf_op jit(solution)/shard_map/weights/pallas_call | solution.py:1000
  862.2 0.8 reduce
  862.9 0.7 reshape.110
  (1 shorter events, 0.0 us)
Async XLA Ops:
  5.8 11.4 %copy-start = (bf16[4,2,256,588]{3,2,1,0:T(8,128)(2,1)}, bf16[4,2,256,588]{3,2,1,0:T(8,128)(2,1)S(1)}, u32[]{:S(2)}) copy-start(bf16[4,2,256,588]{3,2,1,0:T(8,128)(2,1)S(1)} %copy.43) | copy-start | bytes 7225348
  8.6 8.6 copy-start.1

commit v8 on v7

--- a/solution.py
+++ b/solution.py
@@ -376,11 +376,16 @@
 def backward_kernel(dims, *refs):
     (gtop, wqkv, wproj, wfc1, wfc2, low1, low2, x_s, qkv_s, h_s, d_s, p_s,
      gy_s, gpre_s, gmid_s, gqkv_s, gemb, *sums_out,
-     vqkv, vproj, vfc1, vfc2, gin, acc, shared, abuf, gbuf, hid, gmid, gctx, qkv, gqkv, gout, g1, g2,
+     vqkv, vproj, vfc1, vfc2, gin, acc, shared, gbuf, gmid, gctx, qkv, gqkv, g1, g2,
      sum1g, sum1b, sum2g, sum2b, sumproj, sumfc2, sumqkv, sumfc1,
      wsem, qsem, recv_sem, top_sem, send_sem, emb_sem, relay_sem, save_sem, load_sem, dsem, gsem, psem, free_sem) = refs
     stages, images, tokens, heads, head = dims
     rows, width = gmid.shape
+    hid, old, gout = gqkv.at[:, :width], qkv.at[:, :width], gctx.at[:, :width]
+
+    def abuf(chunk):
+        return gqkv.at[:, pl.ds(pl.multiple_of(width + flip(chunk) * CHUNK, LANES), CHUNK)]
+
     chunks = vfc1.shape[1] // CHUNK
     stage = lax.axis_index("pp")
     is_first = stage == 0
@@ -390,7 +395,7 @@
     pieces = ((0, vqkv.shape[1]), (vqkv.shape[1], width - vqkv.shape[1]))
 
     def qkv_copy(part, side):
-        slot = third(part * 2 + side)
+        slot = flip(part) * 2 + side
         at, size = pieces[side]
         lines = pl.ds(pl.multiple_of(third(part) * width + at, 128), size)
         return pltpu.make_async_copy(wqkv.at[lines], vqkv.at[slot, pl.ds(0, size)], qsem.at[slot])
@@ -422,7 +427,7 @@
         return [pltpu.make_async_copy(src, dst.at[image], save_sem.at[at]) for at, (src, dst) in enumerate(pairs)]
 
     def loads(image):
-        pairs = ((h_s, hid), (x_s, hid), (qkv_s, qkv))
+        pairs = ((h_s, hid), (x_s, old), (qkv_s, qkv))
         return [pltpu.make_async_copy(src.at[image], dst, load_sem.at[at]) for at, (src, dst) in enumerate(pairs)]
 
     def next_copy(slot):
@@ -466,10 +471,10 @@
         if chunk < 4:
             d_load(0, chunk).start()
         fc1_copy(chunk).start()
-    loads(0)[0].start()
     proj_copy.start()
-    for part, side in ((0, 0), (0, 1), (1, 0)):
-        qkv_copy(part, side).start()
+    for part in range(2):
+        for side in range(2):
+            qkv_copy(part, side).start()
     gctx[:] = jnp.zeros_like(gctx)
     sums_out, totals = sums_out[:8], (sum1g, sum1b, sum2g, sum2b, sumproj, sumfc2, sumqkv, sumfc1)
     for total in totals:
@@ -496,6 +501,12 @@
 
         load_qkv.start()
 
+        @pl.when(image > 0)
+        def _():
+            save_qkv.wait()
+
+        load_h.start()
+
         @pl.when(image == 0)
         def _():
             fc2_copy(0).wait()
@@ -509,13 +520,13 @@
 
         def fc2(chunk):
             lines = pl.ds(pl.multiple_of(chunk * CHUNK, CHUNK), CHUNK)
-            abuf[flip(chunk)] = dot(gin[slot], vfc2[lines, :], 1, 1).astype(BF16)
+            abuf(chunk)[:] = dot(gin[slot], vfc2[lines, :], 1, 1).astype(BF16)
 
         def gelu(chunk):
             columns = pl.ds(pl.multiple_of(chunk * CHUNK, CHUNK), CHUNK)
             slot2 = flip(chunk)
             slot4 = lax.rem(chunk, 4)
-            pre = abuf[slot2].astype(F32) * jnp.concatenate([shared[slot4 * 2], shared[slot4 * 2 + 1]], axis=1)
+            pre = abuf(chunk)[:].astype(F32) * jnp.concatenate([shared[slot4 * 2], shared[slot4 * 2 + 1]], axis=1)
             sumfc1[:, columns] += fold(pre)
             low = pre.astype(BF16)
             gbuf[slot2] = low
@@ -571,7 +582,6 @@
         @pl.when(image > 0)
         def _():
             save_mid.wait()
-            save_qkv.wait()
 
         def back2(lines):
             grad = acc[lines, :].astype(BF16).astype(F32)
@@ -588,7 +598,6 @@
         for number in range(shared.shape[0], held):
             p_load(image, number).start()
         save_mid.start()
-        load_x.start()
         save_gy.wait()
 
         @pl.when(jnp.logical_and(is_last, image + 2 < images))
@@ -602,6 +611,11 @@
         @pl.when(image == 0)
         def _():
             proj_copy.wait()
+
+
+        @pl.when(image > 0)
+        def _():
+            wait_sent(image)
 
         low = dot(gmid[:], vproj[:], 1, 1).astype(BF16)
         for number in range(heads):
@@ -638,20 +652,23 @@
             if number + held < heads:
                 p_load(image, number + held).start()
         save_qkv.start()
+        load_x.start()
 
         def qkv_part(part, carry):
+            index = image * 3 + part
+            for side in range(2):
+                qkv_copy(index, side).wait()
             for side in range(2):
                 at, size = pieces[side]
-                index = image * 3 + part
-                qkv_copy(index, side).wait()
-                columns = pl.ds(pl.multiple_of(part * width + at, 128), size)
+                columns = pl.ds(pl.multiple_of(part * width + at, LANES), size)
                 piece = gqkv[:, columns]
                 sumqkv[:, columns] += fold(piece.astype(F32))
-                acc[:] += dot(piece, vqkv[third(index * 2 + side), :size])
-
-                @pl.when(index + 1 + side < images * 3)
-                def _():
-                    qkv_copy(index + 1 + side, 1 - side).start()
+                acc[:] += dot(piece, vqkv[flip(index) * 2 + side, :size])
+
+            @pl.when(index + 2 < images * 3)
+            def _():
+                for side in range(2):
+                    qkv_copy(index + 2, side).start()
 
             return carry
 
@@ -665,22 +682,14 @@
 
         load_x.wait()
 
-        @pl.when(image > 0)
-        def _():
-            wait_sent(image)
-
         def back1(lines):
             grad = acc[lines, :].astype(BF16).astype(F32)
-            grad_in, by_unit = norm_backward(grad, hid[lines, :], g1[:])
+            grad_in, by_unit = norm_backward(grad, old[lines, :], g1[:])
             sum1g[:] += fold(by_unit)
             sum1b[:] += fold(grad)
             gout[lines, :] = (gmid[lines, :].astype(F32) + grad_in).astype(BF16)
 
         by_rows(rows, back1)
-
-        @pl.when(more)
-        def _():
-            loads(image + 1)[0].start()
 
         @pl.when(jnp.logical_and(jnp.logical_not(is_first), image >= 2))
         def _():
@@ -771,14 +780,14 @@
         in_specs=[ANY] * 5 + [VMEM] * 2 + [ANY] * 5,
         out_specs=(ANY,) * 5 + (VMEM,) * 8,
         scratch_shapes=[
-            pltpu.VMEM((3, -(-width // 256) * LANES, width), BF16), pltpu.VMEM(wproj.shape, BF16), pltpu.VMEM(wfc1.shape, BF16), pltpu.VMEM(wfc2.shape, BF16),
+            pltpu.VMEM((4, -(-width // 256) * LANES, width), BF16), pltpu.VMEM(wproj.shape, BF16), pltpu.VMEM(wfc1.shape, BF16), pltpu.VMEM(wfc2.shape, BF16),
             pltpu.VMEM((2, rows, width), BF16), pltpu.VMEM((rows, width), F32), pltpu.VMEM((2 * GROUP, rows, HALF), F32),
-            pltpu.VMEM((2, rows, CHUNK), BF16), pltpu.VMEM((2, rows, CHUNK), BF16),
-            pltpu.VMEM((rows, width), BF16), pltpu.VMEM((rows, width), BF16), pltpu.VMEM((rows, heads * LANES), BF16),
+            pltpu.VMEM((2, rows, CHUNK), BF16),
+            pltpu.VMEM((rows, width), BF16), pltpu.VMEM((rows, heads * LANES), BF16),
             pltpu.VMEM((rows, 3 * heads * LANES), BF16), pltpu.VMEM((rows, 3 * width), BF16),
-            pltpu.VMEM((rows, width), BF16), pltpu.VMEM((1, width), F32), pltpu.VMEM((1, width), F32),
+            pltpu.VMEM((1, width), F32), pltpu.VMEM((1, width), F32),
             *(pltpu.VMEM((8, size), F32) for size in sizes),
-            DMA((3, hidden // CHUNK)), TRIPLE, PAIR, PAIR, DMA((stages,)), DMA((images,)), DMA((images,)), DMA((4,)), TRIPLE, DMA((4,)), PAIR, DMA((2 * GROUP + 3,)),
+            DMA((3, hidden // CHUNK)), DMA((4,)), PAIR, PAIR, DMA((stages,)), DMA((images,)), DMA((images,)), DMA((4,)), TRIPLE, DMA((4,)), PAIR, DMA((2 * GROUP + 3,)),
             pltpu.SemaphoreType.REGULAR],
         compiler_params=pltpu.CompilerParams(collective_id=1, has_side_effects=True, vmem_limit_bytes=LIMIT),
         name="backward",

time: 868 us -> 870 us (level)
  no operation moved by 1% of the time
where the time goes in v8:
time: 870 us; the launch traced here: 867 us
  Pallas kernels  843 us (97%)
  local copies, waits for them, and re-layouts  10.5 us (1%)
    pallas_call x1, Pallas kernels, run_backward(): pl.pallas_call(functools.partial(backward_kernel, dims), out_shape=(hbm(w...  379 us
    pallas_call x1, Pallas kernels, run_forward(): pl.pallas_call(functools.partial(forward_kernel, dims), out_shape=(hbm(wi...  306 us
    pallas_call x1, Pallas kernels, run_weights(): pl.pallas_call(functools.partial(weight_kernel, rows // images, len(input...  153 us

profile of v8, /device:TPU:7, one launch (start us, length us, event | category | flops | bytes accessed | tf_op | source)
XLA Modules:
  0.0 866.8 jit_solution(6578131147025849619)
XLA Ops:
  0.7 5.1 copy.43
  5.8 0.0 copy-start
  5.8 0.7 convert_element_type.19
  6.5 0.7 convert_element_type.20
  7.2 1.3 select_add_fusion
  8.6 0.0 copy-start.1
  8.6 8.6 add_convert_fusion.refs_0_
  17.2 0.0 copy-done
  17.2 0.0 copy-done.1
  17.2 0.7 reshape_squeeze.7.refs_7_
  17.9 306.0 %forward.1 = (bf16[8,272,1408]{2,1,0:T(8,128)(2,1)}, bf16[8,272,1408]{2,1,0:T(8,128)(2,1)}, bf16[8,272,6144]{2,1,0:T(8,128)(2,1)}, bf16[8,272,1408]{2,1,0:T(8,12...) custom-call(bf16[8,272,1408]{2,1,0:T(8,128)(2,1)} %add_convert_fusio, ...), custom_call_target="tpu_custom_call" | custom-call | tf_op jit(solution)/shard_map/forward/pallas_call | solution.py:749
  323.9 4.3 head.1
  328.2 379.2 %backward.1 = (bf16[8,272,1408]{2,1,0:T(8,128)(2,1)}, bf16[8,272,6144]{2,1,0:T(8,128)(2,1)}, bf16[8,272,1408]{2,1,0:T(8,128)(2,1)}, bf16[8,272,4224]{2,1,0:T(8,1...) custom-call(bf16[8,16,1408]{2,1,0:T(8,128)(2,1)} %get-tuple-element., ...), custom_call_target="tpu_custom_call" | custom-call | tf_op jit(solution)/shard_map/backward/pallas_call | solution.py:777
  707.5 3.9 pad.12
  711.4 153.5 %weights.1 = (f32[6144,1408]{1,0:T(8,128)}, f32[4224,1408]{1,0:T(8,128)}, f32[1408,1408]{1,0:T(8,128)}, f32[1408,6144]{1,0:T(8,128)}, f32[1000,1408]{1,0:T(8,128...) custom-call(bf16[2176,6144]{1,0:T(8,128)(2,1)} %bitcast.49, ...), custom_call_target="tpu_custom_call" | custom-call | flops 109806878720 | bytes 100925440 | tf_op jit(solution)/shard_map/weights/pallas_call | solution.py:1009
  864.9 0.8 reduce
  865.7 0.7 reshape.110
  (1 shorter events, 0.0 us)
Async XLA Ops:
  5.8 11.4 %copy-start = (bf16[4,2,256,588]{3,2,1,0:T(8,128)(2,1)}, bf16[4,2,256,588]{3,2,1,0:T(8,128)(2,1)S(1)}, u32[]{:S(2)}) copy-start(bf16[4,2,256,588]{3,2,1,0:T(8,128)(2,1)S(1)} %copy.43) | copy-start | bytes 7225348
  8.6 8.6 copy-start.1
